TPU v7x, 32 devices: a whole 2x2x4 slice. The times are simulated.
32 devices in a mesh: dp: 16 (over z, y, core), mp: 2 (over x).
Axes of the slice: x: 2, y: 2, z: 4, core: 2. Of those that a mesh axis runs over, the one named last changes fastest.
Arguments:
- layer_input: bfloat16 [24576, 768], P('dp'), may hold values from -6 to 6
- doc_lengths: int32 [48, 8], P('dp'), may hold values from 1 to 256, 512 in all within a row
- q_weight: bfloat16 [768, 768], P(None, 'mp'), may hold values from -0.3125 to 0.3125
- q_bias: bfloat16 [768], P('mp'), may hold values from -3 to 3
- k_weight: bfloat16 [768, 768], P(None, 'mp'), may hold values from -0.3125 to 0.3125
- v_weight: bfloat16 [768, 768], P(None, 'mp'), may hold values from -0.21875 to 0.21875
- v_bias: bfloat16 [768], P('mp'), may hold values from -3 to 3
- out_weight: bfloat16 [768, 768], P('mp'), may hold values from -1.75 to 1.75
- out_bias: bfloat16 [768], replicated, may hold values from -3 to 3
- attn_gain: bfloat16 [768], replicated, may hold values from 0.5 to 1.5
- attn_shift: bfloat16 [768], replicated, may hold values from -3 to 3
- up_weight: bfloat16 [768, 3072], P(None, 'mp'), may hold values from -0.21875 to 0.21875
- up_bias: bfloat16 [3072], P('mp'), may hold values from -3 to 3
- down_weight: bfloat16 [3072, 768], P('mp'), may hold values from -0.109375 to 0.109375
- down_bias: bfloat16 [768], replicated, may hold values from -3 to 3
- ffn_gain: bfloat16 [768], replicated, may hold values from 0.5 to 1.5
- ffn_shift: bfloat16 [768], replicated, may hold values from -3 to 3
- cotangent: bfloat16 [24576, 768], P('dp'), may hold values from -6 to 6
Outputs:
- layer_output: bfloat16 [24576, 768], P('dp')
- input_grad: bfloat16 [24576, 768], P('dp')
- q_weight_grad: float32 [768, 768], P('dp', 'mp')
- q_bias_grad: float32 [768], P('mp')
- k_weight_grad: float32 [768, 768], P('dp', 'mp')
- v_weight_grad: float32 [768, 768], P('dp', 'mp')
- v_bias_grad: float32 [768], P('mp')
- out_weight_grad: float32 [768, 768], P('mp', 'dp')
- out_bias_grad: float32 [768], replicated
- attn_gain_grad: float32 [768], replicated
- attn_shift_grad: float32 [768], replicated
- up_weight_grad: float32 [768, 3072], P('dp', 'mp')
- up_bias_grad: float32 [3072], P('mp')
- down_weight_grad: float32 [3072, 768], P('mp', 'dp')
- down_bias_grad: float32 [768], replicated
- ffn_gain_grad: float32 [768], replicated
- ffn_shift_grad: float32 [768], replicated
Inputs may be any that keep to these rules, and one draw needn't show every extreme that they name: Each row of doc_lengths sums to 512, and each row holds one document of exactly 256 tokens.
All inputs are finite; a program needn't handle non-finite values.
Results may differ from a plain program's by a relative error of at most 0.019.
Values may be sent and summed in bfloat16 or wider, within the bound.
A program may use at most 192 MiB of HBM per device.

v0:
```python
import jax
import jax.numpy as jnp
from jax import lax
from jax.sharding import PartitionSpec as P

HD = 64


EPS = 1e-12
GELU_C = 0.7978845608028654


def matmul(a, b):
    return jnp.dot(a, b, preferred_element_type=jnp.float32)


def inner_rows(a, b):
    return lax.dot_general(a, b, (((0,), (0,)), ((), ())), preferred_element_type=jnp.float32)


def outer_cols(a, b):
    return lax.dot_general(a, b, (((1,), (1,)), ((), ())), preferred_element_type=jnp.float32)


def lowered(v):
    return v.astype(jnp.bfloat16)


def layer_norm(v, gain, shift):
    mean = jnp.mean(v, -1, keepdims=True)
    centred = v - mean
    var = jnp.mean(centred * centred, -1, keepdims=True)
    return centred * lax.rsqrt(var + EPS) * gain + shift


def gelu_new(v):
    return 0.5 * v * (1.0 + jnp.tanh(GELU_C * (v + 0.044715 * v * v * v)))


def same_doc(lengths, length):
    ends = jnp.cumsum(lengths, axis=-1, dtype=jnp.int32)
    place = jnp.arange(length, dtype=jnp.int32)
    segment = jnp.sum(
        (place[None, :, None] >= ends[:, None, :]).astype(jnp.int32), -1, dtype=jnp.int32
    )
    return segment[:, :, None] == segment[:, None, :]


def masked_scores(query, key, mask):
    scores = jnp.einsum("rqhd,rkhd->rhqk", query, key, preferred_element_type=jnp.float32)
    return jnp.where(mask[:, None], scores, -1000000000.0)


def per_device(
    layer_input,
    doc_lengths,
    q_weight,
    q_bias,
    k_weight,
    v_weight,
    v_bias,
    out_weight,
    out_bias,
    attn_gain,
    attn_shift,
    up_weight,
    up_bias,
    down_weight,
    down_bias,
    ffn_gain,
    ffn_shift,
    cotangent,
):
    rows = doc_lengths.shape[0]
    tokens = layer_input.shape[0]
    length = tokens // rows
    heads = q_weight.shape[1] // HD
    mask = same_doc(doc_lengths, length)
    inputs = layer_input.astype(jnp.float32)
    query = lowered(0.125 * (matmul(layer_input, q_weight) + q_bias.astype(jnp.float32)))
    key = lowered(matmul(layer_input, k_weight))
    value = lowered(matmul(layer_input, v_weight) + v_bias.astype(jnp.float32))
    query = query.reshape(rows, length, heads, HD)
    key = key.reshape(rows, length, heads, HD)
    value = value.reshape(rows, length, heads, HD)
    scores = masked_scores(query, key, mask)
    top = jnp.max(scores, -1, keepdims=True)
    expo = jnp.exp(scores - top)
    total = jnp.sum(expo, -1, keepdims=True)
    probs = expo / total
    log_total = top + jnp.log(total)
    context = jnp.einsum(
        "rhqk,rkhd->rqhd", lowered(probs), value, preferred_element_type=jnp.float32
    )
    context = lowered(context.reshape(tokens, heads * HD))
    attn = lax.psum(matmul(context, out_weight).astype(jnp.bfloat16), "mp").astype(jnp.float32)
    resid1 = inputs + attn + out_bias.astype(jnp.float32)
    normed1, pull_first = jax.vjp(
        layer_norm, resid1, attn_gain.astype(jnp.float32), attn_shift.astype(jnp.float32)
    )
    normed_low = lowered(normed1)
    upper = matmul(normed_low, up_weight) + up_bias.astype(jnp.float32)
    activated, pull_gelu = jax.vjp(gelu_new, upper)
    act = lowered(activated)
    ffn = lax.psum(matmul(act, down_weight).astype(jnp.bfloat16), "mp").astype(jnp.float32)
    resid2 = normed1 + ffn + down_bias.astype(jnp.float32)
    result, pull_second = jax.vjp(
        layer_norm, resid2, ffn_gain.astype(jnp.float32), ffn_shift.astype(jnp.float32)
    )
    layer_output = lowered(result)
    d_resid2, ffn_gain_grad, ffn_shift_grad = pull_second(cotangent.astype(jnp.float32))
    down_bias_grad = jnp.sum(d_resid2, 0)
    d_ffn = lowered(d_resid2)
    down_weight_grad = inner_rows(act, d_ffn)
    d_act = outer_cols(d_ffn, down_weight)
    (d_upper,) = pull_gelu(d_act)
    up_bias_grad = jnp.sum(d_upper, 0)
    d_upper_low = lowered(d_upper)
    up_weight_grad = inner_rows(normed_low, d_upper_low)
    d_normed1 = d_resid2 + lax.psum(
        outer_cols(d_upper_low, up_weight).astype(jnp.bfloat16), "mp"
    ).astype(jnp.float32)
    d_resid1, attn_gain_grad, attn_shift_grad = pull_first(d_normed1)
    out_bias_grad = jnp.sum(d_resid1, 0)
    d_attn = lowered(d_resid1)
    out_weight_grad = inner_rows(context, d_attn)
    d_context = lowered(outer_cols(d_attn, out_weight)).reshape(rows, length, heads, HD)
    scores = masked_scores(query, key, mask)
    probs = jnp.exp(scores - log_total)
    d_probs = jnp.einsum("rqhd,rkhd->rhqk", d_context, value, preferred_element_type=jnp.float32)
    d_value = lowered(
        jnp.einsum("rhqk,rqhd->rkhd", lowered(probs), d_context, preferred_element_type=jnp.float32)
    )
    d_scores = lowered(probs * (d_probs - jnp.sum(probs * d_probs, -1, keepdims=True)))
    d_query = lowered(
        0.125 * jnp.einsum("rhqk,rkhd->rqhd", d_scores, key, preferred_element_type=jnp.float32)
    )
    d_key = lowered(
        jnp.einsum("rhqk,rqhd->rkhd", d_scores, query, preferred_element_type=jnp.float32)
    )
    d_query = d_query.reshape(tokens, heads * HD)
    d_key = d_key.reshape(tokens, heads * HD)
    d_value = d_value.reshape(tokens, heads * HD)
    q_weight_grad = inner_rows(layer_input, d_query)
    k_weight_grad = inner_rows(layer_input, d_key)
    v_weight_grad = inner_rows(layer_input, d_value)
    q_bias_grad = jnp.sum(d_query, 0, dtype=jnp.float32)
    v_bias_grad = jnp.sum(d_value, 0, dtype=jnp.float32)
    input_part = (
        outer_cols(d_query, q_weight) + outer_cols(d_key, k_weight) + outer_cols(d_value, v_weight)
    )
    input_grad = lowered(
        d_resid1 + lax.psum(input_part.astype(jnp.bfloat16), "mp").astype(jnp.float32)
    )
    (
        q_weight_grad,
        k_weight_grad,
        v_weight_grad,
        out_weight_grad,
        up_weight_grad,
        down_weight_grad,
    ) = (
        lax.psum_scatter(q_weight_grad, "dp", scatter_dimension=0, tiled=True),
        lax.psum_scatter(k_weight_grad, "dp", scatter_dimension=0, tiled=True),
        lax.psum_scatter(v_weight_grad, "dp", scatter_dimension=0, tiled=True),
        lax.psum_scatter(out_weight_grad, "dp", scatter_dimension=1, tiled=True),
        lax.psum_scatter(up_weight_grad, "dp", scatter_dimension=0, tiled=True),
        lax.psum_scatter(down_weight_grad, "dp", scatter_dimension=1, tiled=True),
    )
    (
        q_bias_grad,
        v_bias_grad,
        out_bias_grad,
        attn_gain_grad,
        attn_shift_grad,
        up_bias_grad,
        down_bias_grad,
        ffn_gain_grad,
        ffn_shift_grad,
    ) = lax.psum(
        (
            q_bias_grad,
            v_bias_grad,
            out_bias_grad,
            attn_gain_grad,
            attn_shift_grad,
            up_bias_grad,
            down_bias_grad,
            ffn_gain_grad,
            ffn_shift_grad,
        ),
        "dp",
    )
    return (
        layer_output,
        input_grad,
        q_weight_grad,
        q_bias_grad,
        k_weight_grad,
        v_weight_grad,
        v_bias_grad,
        out_weight_grad,
        out_bias_grad,
        attn_gain_grad,
        attn_shift_grad,
        up_weight_grad,
        up_bias_grad,
        down_weight_grad,
        down_bias_grad,
        ffn_gain_grad,
        ffn_shift_grad,
    )


def solution(mesh):
    in_specs = (
        P("dp", None),
        P("dp", None),
        P(None, "mp"),
        P("mp"),
        P(None, "mp"),
        P(None, "mp"),
        P("mp"),
        P("mp", None),
        P(),
        P(),
        P(),
        P(None, "mp"),
        P("mp"),
        P("mp", None),
        P(),
        P(),
        P(),
        P("dp", None),
    )
    out_specs = (
        P("dp", None),
        P("dp", None),
        P("dp", "mp"),
        P("mp"),
        P("dp", "mp"),
        P("dp", "mp"),
        P("mp"),
        P("mp", "dp"),
        P(),
        P(),
        P(),
        P("dp", "mp"),
        P("mp"),
        P("mp", "dp"),
        P(),
        P(),
        P(),
    )
    return jax.shard_map(
        per_device, mesh=mesh, in_specs=in_specs, out_specs=out_specs, check_vma=False
    )
```

profile of v0, /device:TPU:0, one launch (start us, length us, event | category | flops | bytes accessed | tf_op | source)
XLA Modules:
  0.0 908.0 jit_solution(11018000517071338901)
XLA Ops:
  9.6 4.2 fusion.21
  13.7 4.7 reshape.159
  18.4 4.4 copy.99
  22.8 4.2 convolution_convert_fusion.4
  27.0 4.7 reshape.160
  31.7 4.4 copy.100
  36.1 4.2 fusion.22
  40.3 4.7 reshape.158
  44.9 4.4 copy.101
  49.3 11.0 %select_reduce_fusion = (f32[3,6,512]{2,1,0:T(8,128)S(1)}, f32[3,6,512,512]{2,3,1,0:T(8,128)}) fusion(pred[3,512,512]{1,2,0:T(8,128)(4,1)S(1)} %broadcast_compare_fusion, bf16[3,512,6,64]{1,3,2,0:T(8,128)(2,1)} %copy.99, bf16[3,512,6,64]{1,3,2,0:T(8,128)(2,1)} %copy.100), kind=kOutput, calls=%fused_computation.6 | convolution fusion | flops 613407744 | bytes 22056960 | tf_op jit(solution)/shard_map/rqhd,rkhd->rhqk/dot_general | solution.py:50
  60.3 9.8 %fusion = f32[3,6,512]{2,1,0:T(8,128)S(1)} fusion(f32[3,6,512,512]{2,3,1,0:T(8,128)} %get-tuple-element.111, f32[3,6,512]{2,1,0:T(8,128)S(1)} %get-tuple-element.110, pred[3,512,512]{1,2,0:T(8,128)(4,1)S(1)} %broadcast_compare_fusion), kind=kLoop, calls=%fused_computation.5 | loop fusion | flops 14146560 | bytes 19734528 | tf_op jit(solution)/shard_map/reduce_sum | solution.py:89
  70.1 9.3 %fusion.30 = bf16[3,512,6,64]{1,3,2,0:T(8,128)(2,1)S(1)} fusion(bf16[3,512,6,64]{1,3,2,0:T(8,128)(2,1)} %copy.101, f32[3,6,512,512]{2,3,1,0:T(8,128)} %get-tuple-element.111, f32[3,6,512]{2,1,0:T(8,128)S(1)} %fusion, f32[3,6,512]{2,1,0:T(8,128)S(1)} %get-tuple-element.110, pred[3,512,512]{1,2,0:T(8,128)(4,1)S(1)} %broadcast_compare_fusion), kind=kOutput, calls=%fused_computation.71 | convolution fusion | flops 623443968 | bytes 22093824 | tf_op jit(solution)/shard_map/rhqk,rkhd->rqhd/dot_general | solution.py:92
  81.9 2.8 convolution_convert_fusion.2
  84.9 71.4 %all-reduce.6.cloned.1.call-done = bf16[1536,768]{1,0:T(8,128)(2,1)} async-done(((bf16[1536,768]{1,0:T(8,128)(2,1)}), bf16[1536,768]{1,0:T(8,128)(2,1)}) %all-reduce.6.cloned.1.call-update) | async-done | bytes 2359312 | tf_op jit(solution)/shard_map/psum | solution.py:96
  156.3 3.4 fusion.18
  161.4 4.6 convolution_add_fusion
  166.0 3.6 copy-done.47
  169.6 7.0 convolution_convert_fusion.1
  176.7 68.7 %all-reduce.8.cloned.1.call-done = bf16[1536,768]{1,0:T(8,128)(2,1)} async-done(((bf16[1536,768]{1,0:T(8,128)(2,1)}), bf16[1536,768]{1,0:T(8,128)(2,1)}) %all-reduce.8.cloned.1.call-update) | async-done | bytes 2359312 | tf_op jit(solution)/shard_map/psum | solution.py:105
  245.4 4.5 fusion.49
  251.6 2.8 fusion.16
  254.4 3.5 fusion.48
  257.9 12.8 %fusion.50 = (f32[1536]{0:T(1024)}, bf16[1536,1536]{1,0:T(8,128)(2,1)}) fusion(f32[1536,1536]{1,0:T(8,128)S(1)} %bitcast.88, bf16[1536,768]{1,0:T(8,128)(2,1)S(1)} %copy-done, f32[1536,768]{1,0:T(8,128)S(1)} %get-tuple-element.104, f32[1536]{0:T(1024)S(1)} %negate_multiply_fusion.1), kind=kOutput, calls=%fused_computation.99 | convolution fusion | flops 3685218816 | bytes 21245952 | tf_op jit(solution)/shard_map/dot_general | solution.py:22
  270.7 7.7 convolution_convert_fusion
  278.5 68.8 %all-reduce.10.cloned.1.call-done = bf16[1536,768]{1,0:T(8,128)(2,1)} async-done(((bf16[1536,768]{1,0:T(8,128)(2,1)}), bf16[1536,768]{1,0:T(8,128)(2,1)}) %all-reduce.10.cloned.1.call-update) | async-done | bytes 2359312 | tf_op jit(solution)/shard_map/psum | solution.py:120
  347.3 7.6 multiply_reduce_fusion.1
  354.9 4.8 fusion.47
  364.3 4.7 reshape.161
  369.0 4.4 copy.105
  373.4 11.8 %convert_reduce_fusion.1 = (f32[6,64]{1,0:T(8,128)}, bf16[3,512,6,64]{1,3,2,0:T(8,128)(2,1)S(1)}) fusion(bf16[3,512,6,64]{1,3,2,0:T(8,128)(2,1)} %copy.105, f32[3,6,512,512]{2,3,1,0:T(8,128)} %get-tuple-element.111, f32[3,6,512]{2,1,0:T(8,128)S(1)} %log_add_fusion, pred[3,512,512]{1,2,0:T(8,128)(4,1)S(1)} %broadcast_compare_fusion), kind=kOutput, calls=%fused_computation.61 | convolution fusion | flops 619904640 | bytes 22058496 | tf_op jit(solution)/shard_map/rhqk,rqhd->rkhd/dot_general | solution.py:132
  385.2 12.8 %multiply_reduce_fusion = (f32[3,6,512]{2,1,0:T(8,128)S(1)}, f32[3,6,512,512]{2,3,1,0:T(8,128)}) fusion(f32[3,6,512,512]{2,3,1,0:T(8,128)} %get-tuple-element.111, f32[3,6,512]{2,1,0:T(8,128)S(1)} %log_add_fusion, pred[3,512,512]{1,2,0:T(8,128)(4,1)S(1)} %broadcast_compare_fusion, bf16[3,512,6,64]{1,3,2,0:T(8,128)(2,1)S(1)} %copy-done.15, ...), kind=kOutput, calls=%fused_computation.1 | convolution fusion | flops 622844928 | bytes 40968192 | tf_op jit(solution)/shard_map/rqhd,rkhd->rhqk/dot_general | solution.py:130
  398.0 14.0 %multiply_convert_fusion = bf16[3,6,512,512]{2,3,1,0:T(8,128)(2,1)S(1)} fusion(f32[3,6,512,512]{2,3,1,0:T(8,128)} %get-tuple-element.113, f32[3,6,512,512]{2,3,1,0:T(8,128)} %get-tuple-element.111, f32[3,6,512]{2,1,0:T(8,128)S(1)} %get-tuple-element.112, f32[3,6,512]{2,1,0:T(8,128)S(1)} %log_add_fusion, pred[3,512,512]{1,2,0:T(8,128)(4,1)S(1)} %broadcast_compare_fusion), kind=kLoop, calls=%fused_computation | loop fusion | flops 23592960 | bytes 48046080 | tf_op jit(solution)/shard_map/convert_element_type | solution.py:26
  412.0 2.9 fusion.31
  424.4 2.9 add_convert_fusion.1
  427.6 5.4 fusion.41
  433.0 3.6 convolution_bitcast_fusion
  439.4 3.4 convolution_bitcast_fusion.1
  442.7 2.7 copy.125
  450.4 10.4 %fusion.40 = f32[1536,768]{0,1:T(8,128)} fusion(f32[1536,768]{1,0:T(8,128)} %copy-done.6, f32[1536]{0:T(1024)} %copy-done.22, f32[1536,1536]{1,0:T(8,128)} %copy-done.47), kind=kOutput, calls=%fused_computation.93 | convolution fusion | flops 3647471616 | bytes 18880512 | tf_op jit(solution)/shard_map/dot_general | solution.py:18
  461.4 9.6 %fusion.23 = f32[768,1536]{1,0:T(8,128)} fusion(bf16[1536,1536]{1,0:T(8,128)(2,1)} %get-tuple-element.119, f32[768]{0:T(1024)S(1)} %copy-done.26, f32[768]{0:T(1024)S(1)} %convert_element_type.151, f32[1536]{0:T(1024)S(1)} %copy-done.21, bf16[1536,768]{1,0:T(8,128)(2,1)} %all-reduce.6.cloned.1.call-done, bf16[1536,768]{1,0:T(8,128)(2,1)S(1)} %copy-done.3, ...), kind=kOutput, calls=%fused_computation.64 | convolution fusion | flops 3634495488 | bytes 14177280 | tf_op jit(solution)/shard_map/dot_general | solution.py:18
  471.9 24.3 %all-reduce.12.cloned.1.call-done = bf16[1536,768]{1,0:T(8,128)(2,1)} async-done(((bf16[1536,768]{1,0:T(8,128)(2,1)}), bf16[1536,768]{1,0:T(8,128)(2,1)}) %all-reduce.12.cloned.1.call-update) | async-done | bytes 2359312 | tf_op jit(solution)/shard_map/psum | solution.py:153
  496.2 5.3 add_reduce_fusion
  501.5 61.8 %all-reduce = (f32[384]{0:T(512)}, f32[384]{0:T(512)}, f32[768]{0:T(1024)}, f32[768]{0:T(1024)}, f32[768]{0:T(1024)}, /*index=5*/f32[1536]{0:T(1024)}, f32[768]{0:T(1024)}, f32[768]{0:T(1024)}, f32[768]{0:T(1024)}) all-reduce(f32[384]{0:T(512)S(1)} %reduce_sum.228, f32[384]{0:T(512)S(1)} %reduce_sum.230, ...), channel_id=1, replica_groups=mesh['dp'=16,'mp'=2] {'dp'}, use_global_device_ids=true, to_apply=%region_19.20 | all-reduce | flops 6912 | bytes 55296 | tf_op jit(solution)/shard_map/psum | solution.py:180
  563.3 56.4 %reduce-scatter.23.cloned.1.call-done = f32[48,384]{1,0:T(8,128)} async-done(((f32[768,384]{1,0:T(8,128)}), f32[48,384]{1,0:T(8,128)}) %reduce-scatter.23.cloned.1.call-update) | async-done | bytes 73744
  619.7 61.4 %reduce-scatter.21.cloned.1.call-done = f32[48,384]{1,0:T(8,128)} async-done(((f32[768,384]{1,0:T(8,128)}), f32[48,384]{1,0:T(8,128)}) %reduce-scatter.21.cloned.1.call-update) | async-done | bytes 73744
  681.1 61.4 %reduce-scatter.19.cloned.1.call-done = f32[48,384]{1,0:T(8,128)} async-done(((f32[768,384]{1,0:T(8,128)}), f32[48,384]{1,0:T(8,128)}) %reduce-scatter.19.cloned.1.call-update) | async-done | bytes 73744
  742.5 79.1 %reduce-scatter.17.cloned.1.call-done = f32[1536,48]{0,1:T(8,128)} async-done(((f32[1536,768]{0,1:T(8,128)}), f32[1536,48]{0,1:T(8,128)}) %reduce-scatter.17.cloned.1.call-update) | async-done | bytes 294928 | tf_op jit(solution)/shard_map/reduce_scatter | solution.py:168
  821.6 79.1 %reduce-scatter.15.cloned.1.call-done = f32[48,1536]{1,0:T(8,128)} async-done(((f32[768,1536]{1,0:T(8,128)}), f32[48,1536]{1,0:T(8,128)}) %reduce-scatter.15.cloned.1.call-update) | async-done | bytes 294928 | tf_op jit(solution)/shard_map/reduce_scatter | solution.py:167
  (163 shorter events, 31.8 us)
Async XLA Ops:
  7.2 162.4 %copy-start = (bf16[1536,768]{1,0:T(8,128)(2,1)S(1)}, bf16[1536,768]{1,0:T(8,128)(2,1)}, u32[]{:S(2)}) copy-start(bf16[1536,768]{1,0:T(8,128)(2,1)} %param.31) | copy-start | bytes 7077892
  7.2 149.1 %all-reduce.6.cloned.1.call-start = ((), (), s32[]{:S(2)}) async-start(), calls=%async_computation.6 | async-start | bytes 4718592 | tf_op jit(solution)/shard_map/psum | solution.py:96
  27.0 9.1 %copy-start.42 = (bf16[384]{0:T(512)(128)(2,1)S(1)}, bf16[384]{0:T(512)(128)(2,1)}, u32[]{:S(2)}) copy-start(bf16[384]{0:T(512)(128)(2,1)} %param.24) | copy-start | bytes 2308
  81.8 3.0 copy-start.37
  81.8 3.0 copy-start.38
  81.8 3.0 copy-start.34
  84.7 160.7 %all-reduce.8.cloned.1.call-start = ((), (), s32[]{:S(2)}) async-start(), calls=%async_computation.7 | async-start | bytes 4718592 | tf_op jit(solution)/shard_map/psum | solution.py:105
  84.8 160.6 %copy-start.25 = (f32[768]{0:T(1024)}, f32[768]{0:T(1024)S(1)}, u32[]{:S(2)}) copy-start(f32[768]{0:T(1024)S(1)} %convert_element_type.152) | copy-start | bytes 9220
  156.3 3.4 copy-start.2
  156.3 3.8 copy-start.4
  156.3 5.1 copy-start.43
  161.3 193.5 %copy-start.20 = (f32[1536]{0:T(1024)}, f32[1536]{0:T(1024)S(1)}, u32[]{:S(2)}) copy-start(f32[1536]{0:T(1024)S(1)} %fusion.36) | copy-start | bytes 18436
  165.9 3.6 copy-start.47
  169.6 7.1 copy-start.39
  169.6 7.1 copy-start.40
  169.6 7.1 copy-start.41
  176.6 170.7 %all-reduce.10.cloned.1.call-start = ((), (), s32[]{:S(2)}) async-start(), calls=%async_computation.8 | async-start | bytes 4718592 | tf_op jit(solution)/shard_map/psum | solution.py:120
  250.0 7.9 slice-start
  251.6 6.3 slice-start.1
  254.4 3.5 slice-start.2
  257.9 12.8 %copy-start.6 = (f32[1536,768]{1,0:T(8,128)}, f32[1536,768]{1,0:T(8,128)S(1)}, u32[]{:S(2)}) copy-start(f32[1536,768]{1,0:T(8,128)S(1)} %get-tuple-element.104) | copy-start | bytes 14155780
  257.9 97.0 %copy-start.22 = (f32[1536]{0:T(1024)}, f32[1536]{0:T(1024)S(1)}, u32[]{:S(2)}) copy-start(f32[1536]{0:T(1024)S(1)} %negate_multiply_fusion.1) | copy-start | bytes 18436
  257.9 12.8 %copy-start.44 = (bf16[768,1536]{1,0:T(8,128)(2,1)S(1)}, bf16[768,1536]{1,0:T(8,128)(2,1)}, u32[]{:S(2)}) copy-start(bf16[768,1536]{1,0:T(8,128)(2,1)} %param.29) | copy-start | bytes 7077892
  270.7 76.5 %copy-start.3 = (bf16[1536,768]{1,0:T(8,128)(2,1)S(1)}, bf16[1536,768]{1,0:T(8,128)(2,1)}, u32[]{:S(2)}) copy-start(bf16[1536,768]{1,0:T(8,128)(2,1)} %param.18) | copy-start | bytes 7077892
  278.4 217.7 %all-reduce.12.cloned.1.call-start = ((), (), s32[]{:S(2)}) async-start(), calls=%async_computation.9 | async-start | bytes 4718592 | tf_op jit(solution)/shard_map/psum | solution.py:153
  347.3 7.6 copy-start.5
  347.3 7.6 copy-start.10
  354.9 7.0 copy-start.46
  359.8 9.2 %copy-start.23 = (f32[1536]{0:T(1024)}, f32[1536]{0:T(1024)S(1)}, u32[]{:S(2)}) copy-start(f32[1536]{0:T(1024)S(1)} %negate_multiply_fusion) | copy-start | bytes 18436
  373.4 11.8 %copy-start.13 = (bf16[3,512,6,64]{1,3,2,0:T(8,128)(2,1)S(1)}, bf16[3,512,6,64]{1,3,2,0:T(8,128)(2,1)}, u32[]{:S(2)}) copy-start(bf16[3,512,6,64]{1,3,2,0:T(8,128)(2,1)} %copy.101) | copy-start | bytes 3538948
  373.4 11.8 %copy-start.15 = (bf16[3,512,6,64]{1,3,2,0:T(8,128)(2,1)S(1)}, bf16[3,512,6,64]{1,3,2,0:T(8,128)(2,1)}, u32[]{:S(2)}) copy-start(bf16[3,512,6,64]{1,3,2,0:T(8,128)(2,1)} %copy.105) | copy-start | bytes 3538948
  398.0 14.0 %copy-start.8 = (bf16[3,512,6,64]{1,3,2,0:T(8,128)(2,1)S(1)}, bf16[3,512,6,64]{1,3,2,0:T(8,128)(2,1)}, u32[]{:S(2)}) copy-start(bf16[3,512,6,64]{1,3,2,0:T(8,128)(2,1)} %copy.99) | copy-start | bytes 3538948
  412.0 3.0 copy-start.9
  418.7 5.7 copy-start.14
  427.3 135.9 %reduce-scatter.13.cloned.1.call-start = ((), (), s32[]{:S(2)}) async-start(), calls=%async_computation.10 | async-start | bytes 1253376 | tf_op jit(solution)/shard_map/reduce_scatter | solution.py:166
  433.0 186.7 %reduce-scatter.23.cloned.1.call-start = ((), (), s32[]{:S(2)}) async-start(), calls=%async_computation.15 | async-start | bytes 1253376
  439.3 241.7 %reduce-scatter.21.cloned.1.call-start = ((), (), s32[]{:S(2)}) async-start(), calls=%async_computation.14 | async-start | bytes 1253376
  445.5 297.0 %reduce-scatter.19.cloned.1.call-start = ((), (), s32[]{:S(2)}) async-start(), calls=%async_computation.13 | async-start | bytes 1253376
  450.3 371.3 %reduce-scatter.17.cloned.1.call-start = ((), (), s32[]{:S(2)}) async-start(), calls=%async_computation.12 | async-start | bytes 5013504 | tf_op jit(solution)/shard_map/reduce_scatter | solution.py:168
  460.8 440.0 %reduce-scatter.15.cloned.1.call-start = ((), (), s32[]{:S(2)}) async-start(), calls=%async_computation.11 | async-start | bytes 5013504 | tf_op jit(solution)/shard_map/reduce_scatter | solution.py:167
  471.0 25.1 %copy-start.24 = (f32[1536]{0:T(1024)S(1)}, f32[1536]{0:T(1024)}, u32[]{:S(2)}) copy-start(f32[1536]{0:T(1024)} %copy-done.23) | copy-start | bytes 18436
  471.8 429.0 %copy-start.1 = (bf16[1536,768]{1,0:T(8,128)(2,1)S(1)}, bf16[1536,768]{1,0:T(8,128)(2,1)}, u32[]{:S(2)}) copy-start(bf16[1536,768]{1,0:T(8,128)(2,1)} %param.31) | copy-start | bytes 7077892
  471.9 29.6 %copy-start.27 = (f32[768]{0:T(1024)S(1)}, f32[768]{0:T(1024)}, u32[]{:S(2)}) copy-start(f32[768]{0:T(1024)} %get-tuple-element.87) | copy-start | bytes 9220
  471.9 29.6 %copy-start.28 = (f32[768]{0:T(1024)S(1)}, f32[768]{0:T(1024)}, u32[]{:S(2)}) copy-start(f32[768]{0:T(1024)} %get-tuple-element.91) | copy-start | bytes 9220
  471.9 29.6 %copy-start.29 = (f32[768]{0:T(1024)S(1)}, f32[768]{0:T(1024)}, u32[]{:S(2)}) copy-start(f32[768]{0:T(1024)} %get-tuple-element.85) | copy-start | bytes 9220
  471.9 29.6 %copy-start.30 = (f32[768]{0:T(1024)S(1)}, f32[768]{0:T(1024)}, u32[]{:S(2)}) copy-start(f32[768]{0:T(1024)} %get-tuple-element.89) | copy-start | bytes 9220
  471.9 29.6 %copy-start.31 = (f32[768]{0:T(1024)S(1)}, f32[768]{0:T(1024)}, u32[]{:S(2)}) copy-start(f32[768]{0:T(1024)} %get-tuple-element.90) | copy-start | bytes 9220
  471.9 29.6 %copy-start.33 = (f32[1536]{0:T(1024)S(1)}, f32[1536]{0:T(1024)}, u32[]{:S(2)}) copy-start(f32[1536]{0:T(1024)} %get-tuple-element.118) | copy-start | bytes 18436
  (13 other events, 19.1 us)
Sparse Core Ops, SparseCore 0:
  84.8 71.3 all-reduce.5
  176.7 68.6 all-reduce.7
  278.6 68.6 all-reduce.9
  427.5 68.6 all-reduce.11
  500.2 58.2 reduce-scatter.12
  562.6 57.1 reduce-scatter.22
  623.9 57.1 reduce-scatter.20
  685.3 57.1 reduce-scatter.18
  746.9 74.6 reduce-scatter.16
  825.9 74.8 reduce-scatter.14
where the time goes:
time: 919 us; the launch traced here: 908 us
  waiting for transfers between devices  571 us (62%)
  matrix products  140 us (15%)
  blocking collectives  61.8 us (7%)
  other arithmetic  59.9 us (7%)
  local copies, waits for them, and re-layouts  59.3 us (6%)
  between operations  15.3 us (2%)
    unnamed x13, waiting for transfers between devices  179 us
    reduce_scatter x1, waiting for transfers between devices, per_device(): lax.psum_scatter(up_weight_grad, 'dp', scatter_dimension=0, tiled=True)  79.1 us
    reduce_scatter x1, waiting for transfers between devices, per_device(): lax.psum_scatter(down_weight_grad, 'dp', scatter_dimension=1, tiled=True)  79.1 us
    psum x1, waiting for transfers between devices, per_device(): lax.psum(matmul(context, out_weight).astype(jnp.bfloat16), 'mp')  71.4 us
    psum x1, waiting for transfers between devices, per_device(): lax.psum(outer_cols(d_upper_low, up_weight).astype(jnp.bfloat16), 'mp')  68.8 us
    psum x1, waiting for transfers between devices, per_device(): lax.psum(matmul(act, down_weight).astype(jnp.bfloat16), 'mp')  68.7 us
    psum x1, blocking collectives, per_device(): lax.psum((q_bias_grad, v_bias_grad, out_bias_grad, attn_gain_grad, attn_s...  61.8 us
    dot_general x6, matrix products, inner_rows(): lax.dot_general(a, b, (((0,), (0,)), ((), ())), preferred_element_type=jn...  34.3 us
  transfers between devices with their start and end apart: 10, of which 9 were waited for; matrix products, arithmetic and copies ran while one was open for 5% of the time, Pallas kernels for 0%

commit v1 on v0

v1 whole, which is shorter than its diff:
```python
import functools

import jax
import jax.numpy as jnp
from jax import lax
from jax.experimental import pallas as pl
from jax.experimental.pallas import tpu as pltpu
from jax.sharding import PartitionSpec as P

HD = 64
PAIR = 2 * HD
EPS = 1e-12
GELU_C = 0.7978845608028654
F32 = jnp.float32
BF16 = jnp.bfloat16
CHUNK = 512
VMEM_LIMIT = 60 * 1024 * 1024


def mm(a, b):
    return jnp.dot(a, b, preferred_element_type=F32)


def mm_t(a, b):
    return lax.dot_general(a, b, (((1,), (1,)), ((), ())), preferred_element_type=F32)


def t_mm(a, b):
    return lax.dot_general(a, b, (((0,), (0,)), ((), ())), preferred_element_type=F32)


def halves(v):
    lane = lax.broadcasted_iota(jnp.int32, v.shape, 1)
    zero = jnp.zeros_like(v)
    return jnp.where(lane < HD, v, zero), jnp.where(lane < HD, zero, v)


def attention_forward(
    x_ref, w_ref, b_ref, wo_ref, seg_c_ref, seg_r_ref, bo_ref, gain_ref, shift_ref,
    qkv_ref, p_ref, ctx_ref, xhat_ref, rstd_ref, low_ref,
):
    seqs, length = seg_c_ref.shape[0], seg_c_ref.shape[1]
    groups, width = wo_ref.shape[0], wo_ref.shape[1]
    pairs = width // PAIR

    @pl.loop(0, seqs)
    def _(s):
        rows = pl.ds(pl.multiple_of(s * length, length), length)
        x = x_ref[rows, :]
        mask = seg_c_ref[s] == seg_r_ref[s]
        attn = x.astype(F32) + bo_ref[...]
        for g in range(groups):
            y = mm(x, w_ref[g]) + b_ref[g]
            query = (0.125 * y[:, :width]).astype(BF16)
            key = y[:, width : 2 * width].astype(BF16)
            value = y[:, 2 * width :].astype(BF16)
            qkv_ref[g, rows, :width] = query
            qkv_ref[g, rows, width : 2 * width] = key
            qkv_ref[g, rows, 2 * width :] = value
            parts = []
            for p in range(pairs):
                at = slice(p * PAIR, (p + 1) * PAIR)
                k = key[:, at]
                both = None
                for h, (q, v) in enumerate(zip(halves(query[:, at]), halves(value[:, at]))):
                    scores = jnp.where(mask, mm_t(q, k), -1000000000.0)
                    expo = jnp.exp(scores - jnp.max(scores, -1, keepdims=True))
                    probs = (expo * (1.0 / jnp.sum(expo, -1, keepdims=True))).astype(BF16)
                    p_ref[s, (g * pairs + p) * 2 + h] = probs
                    part = mm(probs, v)
                    both = part if both is None else both + part
                parts.append(both.astype(BF16))
            ctx = jnp.concatenate(parts, 1)
            ctx_ref[g, rows, :] = ctx
            attn = attn + mm(ctx, wo_ref[g])
        mean = jnp.mean(attn, -1, keepdims=True)
        centred = attn - mean
        rstd = lax.rsqrt(jnp.mean(centred * centred, -1, keepdims=True) + EPS)
        xhat = centred * rstd
        xhat_ref[rows, :] = xhat
        rstd_ref[rows, :] = rstd
        low_ref[rows, :] = (xhat * gain_ref[...] + shift_ref[...]).astype(BF16)


def norm_backward(xhat, rstd, gain, grad):
    scaled = grad * gain
    return rstd * (
        scaled
        - jnp.mean(scaled, -1, keepdims=True)
        - xhat * jnp.mean(scaled * xhat, -1, keepdims=True)
    )


def feed_forward(
    low_ref, xhat_ref, rstd_ref, up_ref, ub_ref, down_ref, vec_ref, cot_ref,
    out_ref, gd_ref, gu_ref, d_resid_ref, small_ref, ubg_ref,
    act_ref, slope_ref, acc_ref, dffn_ref, dffn_t_ref, low_t_ref,
):
    tokens, width = low_ref.shape
    groups, hidden = up_ref.shape[0], up_ref.shape[2]
    step = min(CHUNK, hidden)
    per = hidden // step
    block = 256
    low_t_ref[...] = low_ref[...].T
    acc_ref[...] = jnp.zeros_like(acc_ref)

    @pl.loop(0, groups * per)
    def _(i):
        g = i // per
        at = pl.ds(pl.multiple_of((i % per) * step, step), step)

        @pl.loop(0, tokens // block)
        def _(b):
            rows = pl.ds(pl.multiple_of(b * block, block), block)
            u = mm(low_ref[rows, :], up_ref[g, :, at]) + ub_ref[g, :, at]
            square = u * u
            t = jnp.tanh(GELU_C * (u + 0.044715 * square * u))
            half = 0.5 * (1.0 + t)
            act = (u * half).astype(BF16)
            act_ref[g, rows, at] = act
            slope = half + (0.5 * GELU_C) * u * (1.0 - t * t) * (1.0 + 0.134145 * square)
            slope_ref[g, rows, at] = slope.astype(BF16)
            acc_ref[rows, :] += mm(act, down_ref[g, at, :])

    small_ref[...] = jnp.zeros_like(small_ref)
    attn_gain, attn_shift = vec_ref[0:1, :], vec_ref[1:2, :]
    down_bias = vec_ref[2:3, :]
    ffn_gain, ffn_shift = vec_ref[3:4, :], vec_ref[4:5, :]

    @pl.loop(0, tokens // block)
    def _(b):
        rows = pl.ds(pl.multiple_of(b * block, block), block)
        resid = xhat_ref[rows, :] * attn_gain + attn_shift + acc_ref[rows, :] + down_bias
        centred = resid - jnp.mean(resid, -1, keepdims=True)
        rstd = lax.rsqrt(jnp.mean(centred * centred, -1, keepdims=True) + EPS)
        xhat = centred * rstd
        out_ref[rows, :] = (xhat * ffn_gain + ffn_shift).astype(BF16)
        cot = cot_ref[rows, :].astype(F32)
        grad = norm_backward(xhat, rstd, ffn_gain, cot)
        acc_ref[rows, :] = grad
        dffn_ref[rows, :] = grad.astype(BF16)
        small_ref[3:4, :] += jnp.sum(grad, 0, keepdims=True)
        small_ref[4:5, :] += jnp.sum(cot * xhat, 0, keepdims=True)
        small_ref[5:6, :] += jnp.sum(cot, 0, keepdims=True)

    dffn_t_ref[...] = dffn_ref[...].T

    @pl.loop(0, groups * per)
    def _(i):
        g = i // per
        at = pl.ds(pl.multiple_of((i % per) * step, step), step)
        total = jnp.zeros((1, step), F32)
        for b in range(tokens // block):
            rows = slice(b * block, (b + 1) * block)
            d_upper = mm_t(dffn_ref[rows, :], down_ref[g, at, :]) * slope_ref[g, rows, at].astype(F32)
            total = total + jnp.sum(d_upper, 0, keepdims=True)
            d_low = d_upper.astype(BF16)
            slope_ref[g, rows, at] = d_low
            acc_ref[rows, :] += mm_t(d_low, up_ref[g, :, at])
        ubg_ref[g, :, at] = total
        for b in range(width // block):
            rows = slice(b * block, (b + 1) * block)
            gd_ref[g, rows, at] = mm(dffn_t_ref[rows, :], act_ref[g, :, at]).astype(BF16)
            gu_ref[g, rows, at] = mm(low_t_ref[rows, :], slope_ref[g, :, at]).astype(BF16)

    @pl.loop(0, tokens // block)
    def _(b):
        rows = pl.ds(pl.multiple_of(b * block, block), block)
        d_normed = acc_ref[rows, :]
        xhat = xhat_ref[rows, :]
        grad = norm_backward(xhat, rstd_ref[rows, :], attn_gain, d_normed)
        d_resid_ref[rows, :] = grad
        small_ref[0:1, :] += jnp.sum(grad, 0, keepdims=True)
        small_ref[1:2, :] += jnp.sum(d_normed * xhat, 0, keepdims=True)
        small_ref[2:3, :] += jnp.sum(d_normed, 0, keepdims=True)


def attention_backward(
    x_ref, d_resid_ref, w_ref, wo_ref, qkv_ref, p_ref, ctx_ref,
    in_ref, gq_ref, go_ref, bg_ref,
    dq_ref, dattn_t_ref, x_t_ref,
):
    seqs, length = p_ref.shape[0], p_ref.shape[2]
    groups, width = wo_ref.shape[0], wo_ref.shape[1]
    model = x_ref.shape[1]
    pairs = width // PAIR
    block = 256
    x_t_ref[...] = x_ref[...].T

    @pl.loop(0, seqs)
    def _(s):
        rows = pl.ds(pl.multiple_of(s * length, length), length)
        d_resid = d_resid_ref[rows, :]
        d_attn = d_resid.astype(BF16)
        dattn_t_ref[:, rows] = d_attn.T
        total = d_resid
        for g in range(groups):
            d_ctx = mm_t(d_attn, wo_ref[g]).astype(BF16)
            for p in range(pairs):
                at = slice(p * PAIR, (p + 1) * PAIR)
                q_at, k_at, v_at = (slice(o * width + p * PAIR, o * width + (p + 1) * PAIR) for o in range(3))
                value = qkv_ref[g, rows, v_at]
                q_pair = halves(qkv_ref[g, rows, q_at])
                k_pair = halves(qkv_ref[g, rows, k_at])
                c_pair = halves(d_ctx[:, at])
                dq = dk = dv = None
                for h in range(2):
                    low = p_ref[s, (g * pairs + p) * 2 + h]
                    probs = low.astype(F32)
                    d_probs = mm_t(c_pair[h], value)
                    inner = jnp.sum(probs * d_probs, -1, keepdims=True)
                    d_scores = (probs * (d_probs - inner)).astype(BF16)
                    dv_h = t_mm(low, c_pair[h])
                    dq_h = mm(d_scores, k_pair[h])
                    dk_h = t_mm(d_scores, q_pair[h])
                    dq = dq_h if dq is None else dq + dq_h
                    dk = dk_h if dk is None else dk + dk_h
                    dv = dv_h if dv is None else dv + dv_h
                dq_ref[g, rows, q_at] = (0.125 * dq).astype(BF16)
                dq_ref[g, rows, k_at] = dk.astype(BF16)
                dq_ref[g, rows, v_at] = dv.astype(BF16)
            total = total + mm_t(dq_ref[g, rows, :], w_ref[g])
        in_ref[rows, :] = total.astype(BF16)

    for g in range(groups):
        bg_ref[g] = jnp.sum(dq_ref[g].astype(F32), 0, keepdims=True)

        @pl.loop(0, model // block)
        def _(b):
            rows = pl.ds(pl.multiple_of(b * block, block), block)
            gq_ref[g, rows, :] = mm(x_t_ref[rows, :], dq_ref[g]).astype(BF16)
            go_ref[g, rows, :] = mm(dattn_t_ref[rows, :], ctx_ref[g]).astype(BF16)


def call(kernel, outs, scratch, flops, *args):
    shapes = [jax.ShapeDtypeStruct(s, d) for s, d in outs]
    moved = sum(a.size * a.dtype.itemsize for a in args) + sum(s.size * s.dtype.itemsize for s in shapes)
    vmem = pl.BlockSpec(memory_space=pltpu.VMEM)
    return pl.pallas_call(
        kernel,
        out_shape=shapes,
        in_specs=[vmem] * len(args),
        out_specs=[vmem] * len(shapes),
        scratch_shapes=[pltpu.VMEM(s, d) for s, d in scratch],
        compiler_params=pltpu.CompilerParams(vmem_limit_bytes=VMEM_LIMIT),
        cost_estimate=pl.CostEstimate(flops=flops, bytes_accessed=moved, transcendentals=0),
    )(*args)


def factors_of(n):
    found = []
    while n > 4 or (n > 1 and len(found) < 2):
        found.append(2)
        n //= 2
    return found + ([n] if n > 1 else [])


def swap(v):
    return lax.ppermute(v, "mp", [(0, 1), (1, 0)])


def shift_dp(v, n, stride, factor, k):
    def target(d):
        i = (d // stride) % factor
        return d + ((i + k) % factor - i) * stride

    return lax.ppermute(v, "dp", [(d, target(d)) for d in range(n)])


def with_peer(own, n):
    core = lax.axis_index("dp") % 2
    half = own.shape[0] // 2
    mine = swap(lax.dynamic_slice_in_dim(own, core * half, half, 0))
    other = shift_dp(mine, n, 1, 2, 1)
    first = core == 0
    peer = jnp.concatenate([jnp.where(first, mine, other), jnp.where(first, other, mine)], 0)
    return jnp.stack([own, peer])


def reduce_to_owner(grad, n):
    index = lax.axis_index("dp")
    rows = grad.shape[1] // n
    left = grad.reshape(2, n, rows, grad.shape[2])
    stride = 1
    for factor in factors_of(n):
        parts = left.reshape(2, left.shape[1] // factor, factor, rows, left.shape[3])
        i = (index // stride) % factor

        def pick(at):
            return lax.dynamic_index_in_dim(parts, at, 2, keepdims=False)

        total = pick(i).astype(F32)
        for k in range(1, factor):
            total = total + shift_dp(pick((i + k) % factor), n, stride, factor, k).astype(F32)
        left = total.astype(BF16)
        stride *= factor
    left = left.reshape(2, rows, left.shape[3])
    return left[0].astype(F32) + swap(left[1]).astype(F32)


def per_device(
    n, layer_input, doc_lengths, q_weight, q_bias, k_weight, v_weight, v_bias, out_weight, out_bias,
    attn_gain, attn_shift, up_weight, up_bias, down_weight, down_bias, ffn_gain, ffn_shift, cotangent,
):
    rows = doc_lengths.shape[0]
    tokens, model = layer_input.shape
    length = tokens // rows
    part = length // 2
    mine = rows * part
    width = q_weight.shape[1]
    hidden = up_weight.shape[1]
    heads = width // HD
    x_index = lax.axis_index("mp")

    ends = jnp.cumsum(doc_lengths, axis=-1, dtype=jnp.int32)
    start = jnp.sum(jnp.where(doc_lengths == part, ends - part, 0), -1)
    place = jnp.arange(length, dtype=jnp.int32)
    segment = jnp.sum((place[None, :, None] >= ends[:, None, :]).astype(jnp.int32), -1, dtype=jnp.int32)
    before = place[None, :part] < start[:, None]
    from_high = before != (x_index == 1)

    def take(v):
        v = v.reshape(rows, 2, part, model)
        return jnp.where(from_high[:, :, None], v[:, 1], v[:, 0]).reshape(mine, model)

    def give(own):
        own = own.reshape(rows, part, model)
        other = swap(own)
        low = jnp.where(from_high[:, :, None], other, own)
        high = jnp.where(from_high[:, :, None], own, other)
        return jnp.stack([low, high], 1).reshape(tokens, model)

    seg = jnp.where(from_high, segment[:, part:], segment[:, :part])

    w_qkv = with_peer(jnp.concatenate([q_weight, k_weight, v_weight], 1), n)
    w_out = with_peer(out_weight, n)
    w_up = with_peer(up_weight, n)
    w_down = with_peer(down_weight, n)
    own_bias = jnp.concatenate([q_bias, v_bias, up_bias])
    bias = jnp.stack([own_bias, swap(own_bias)]).astype(F32)[:, None, :]
    b_qkv = jnp.concatenate([bias[..., :width], jnp.zeros_like(bias[..., :width]), bias[..., width : 2 * width]], -1)
    b_up = bias[..., 2 * width :]
    vectors = jnp.stack([attn_gain, attn_shift, down_bias, ffn_gain, ffn_shift]).astype(F32)

    x = take(layer_input)
    cot = take(cotangent)
    qkv, probs, ctx, xhat, rstd, low = call(
        attention_forward,
        [
            ((2, mine, 3 * width), BF16),
            ((rows, 2 * heads, part, part), BF16),
            ((2, mine, width), BF16),
            ((mine, model), F32),
            ((mine, 1), F32),
            ((mine, model), BF16),
        ],
        [],
        2 * mine * model * 8 * width,
        x, w_qkv, b_qkv, w_out, seg[:, :, None], seg[:, None, :],
        out_bias.astype(F32)[None], vectors[0:1], vectors[1:2],
    )
    output, g_down, g_up, d_resid, small, up_bias_grad = call(
        feed_forward,
        [
            ((mine, model), BF16),
            ((2, model, hidden), BF16),
            ((2, model, hidden), BF16),
            ((mine, model), F32),
            ((8, model), F32),
            ((2, 1, hidden), F32),
        ],
        [
            ((2, mine, hidden), BF16),
            ((2, mine, hidden), BF16),
            ((mine, model), F32),
            ((mine, model), BF16),
            ((model, mine), BF16),
            ((model, mine), BF16),
        ],
        2 * mine * model * 2 * hidden * 6,
        low, xhat, rstd, w_up, b_up, w_down, vectors, cot,
    )
    layer_output = give(output)
    down_weight_grad = reduce_to_owner(g_down, n).T
    up_weight_grad = reduce_to_owner(g_up, n)
    grad_in, g_qkv, g_out, bias_grad = call(
        attention_backward,
        [
            ((mine, model), BF16),
            ((2, model, 3 * width), BF16),
            ((2, model, width), BF16),
            ((2, 1, 3 * width), F32),
        ],
        [((2, mine, 3 * width), BF16), ((model, mine), BF16), ((model, mine), BF16)],
        2 * mine * model * 16 * width,
        x, d_resid, w_qkv, w_out, qkv, probs, ctx,
    )
    input_grad = give(grad_in)
    g_attn = reduce_to_owner(jnp.concatenate([g_qkv, g_out], -1), n)
    sums = jnp.concatenate([bias_grad[:, 0, :width], bias_grad[:, 0, 2 * width :], up_bias_grad[:, 0]], -1)
    sums = jnp.where(x_index == 0, sums, sums[::-1])
    sums, small = lax.psum((sums, small), ("dp", "mp"))
    sums = lax.dynamic_index_in_dim(sums, x_index, 0, keepdims=False)
    return (
        layer_output,
        input_grad,
        g_attn[:, :width],
        sums[:width],
        g_attn[:, width : 2 * width],
        g_attn[:, 2 * width : 3 * width],
        sums[width : 2 * width],
        g_attn[:, 3 * width :].T,
        small[0],
        small[1],
        small[2],
        up_weight_grad,
        sums[2 * width :],
        down_weight_grad,
        small[3],
        small[4],
        small[5],
    )


def solution(mesh):
    in_specs = (
        P("dp", None), P("dp", None), P(None, "mp"), P("mp"), P(None, "mp"), P(None, "mp"), P("mp"),
        P("mp", None), P(), P(), P(), P(None, "mp"), P("mp"), P("mp", None), P(), P(), P(), P("dp", None),
    )
    out_specs = (
        P("dp", None), P("dp", None), P("dp", "mp"), P("mp"), P("dp", "mp"), P("dp", "mp"), P("mp"),
        P("mp", "dp"), P(), P(), P(), P("dp", "mp"), P("mp"), P("mp", "dp"), P(), P(), P(),
    )
    return jax.shard_map(
        functools.partial(per_device, mesh.shape["dp"]),
        mesh=mesh, in_specs=in_specs, out_specs=out_specs, check_vma=False,
    )
```

time: 919 us -> 432 us (0.47)
  waiting for transfers between devices: 571 us -> 139 us
  matrix products: 140 us -> 0 us
  Pallas kernels: 0 us -> 96 us
  starting transfers between devices: 0.88 us -> 28.9 us
  other arithmetic: 59.9 us -> 40.2 us
  local copies, waits for them, and re-layouts: 59.3 us -> 43 us
  blocking collectives: 61.8 us -> 78 us
  between operations: 15.3 us -> 1.32 us
    psum x4 -> x0, waiting for transfers between devices: 233 us -> none  [the longest x1 71.4 us: per_device(): lax.psum(matmul(context, out_weight).astype(jnp.bfloat16), 'mp')]
    unnamed x13 -> x0, waiting for transfers between devices: 179 us -> none
    reduce_scatter x3 -> x0, waiting for transfers between devices: 158 us -> none  [the longest x1 79.1 us: per_device(): lax.psum_scatter(up_weight_grad, 'dp', scatter_dimension=0, tiled=True)]
    dot_general x24 -> x0, matrix products: 140 us -> none  [the longest x6 34.3 us: inner_rows(): lax.dot_general(a, b, (((0,), (0,)), ((), ())), preferred_element_type=jn...]
    ppermute x0 -> x29, waiting for transfers between devices: none -> 139 us  [the longest x19 92.8 us: shift_dp(): return lax.ppermute(v, 'dp', [(d, target(d)) for d in range(n)])]
    pallas_call x0 -> x3, Pallas kernels: none -> 96 us  [call(): pl.pallas_call(kernel, out_shape=shapes, in_specs=[vmem] * len(args), out...]
    reduce_sum x11 -> x2, other arithmetic: 43.6 us -> 0.21 us  [the longest x1 0.12 us: per_device(): start = jnp.sum(jnp.where(doc_lengths == part, ends - part, 0), -1)]
    reshape x8 -> x0, local copies, waits for them, and re-layouts: 36.3 us -> none  [the longest x2 9.08 us: per_device(): key = key.reshape(rows, length, heads, HD)]
  transfers between devices with their start and end apart: 10 -> 29, of which waited for: 9 -> 9; matrix products, arithmetic and copies ran while one was open for 5% -> 15% of each run, Pallas kernels for 0% -> 11%
where the time goes in v1:
time: 432 us; the launch traced here: 427 us
  waiting for transfers between devices  139 us (32%)
  Pallas kernels  96 us (22%)
  blocking collectives  78 us (18%)
  local copies, waits for them, and re-layouts  43 us (10%)
  other arithmetic  40.2 us (9%)
  starting transfers between devices  28.9 us (7%)
    pallas_call x3, Pallas kernels, call(): pl.pallas_call(kernel, out_shape=shapes, in_specs=[vmem] * len(args), out...  96 us
    ppermute x19, waiting for transfers between devices, shift_dp(): return lax.ppermute(v, 'dp', [(d, target(d)) for d in range(n)])  92.8 us
    psum x1, blocking collectives, per_device(): sums, small = lax.psum((sums, small), ('dp', 'mp'))  78 us
    ppermute x10, waiting for transfers between devices, swap(): return lax.ppermute(v, 'mp', [(0, 1), (1, 0)])  46.4 us
    ppermute x19, starting transfers between devices, shift_dp(): return lax.ppermute(v, 'dp', [(d, target(d)) for d in range(n)])  16.7 us
    ppermute x10, starting transfers between devices, swap(): return lax.ppermute(v, 'mp', [(0, 1), (1, 0)])  12.2 us
    unnamed x71, local copies, waits for them, and re-layouts  11.2 us
    convert_element_type x9, other arithmetic, reduce_to_owner(): left = total.astype(BF16)  8.89 us
  transfers between devices with their start and end apart: 29, of which 9 were waited for; matrix products, arithmetic and copies ran while one was open for 15% of the time, Pallas kernels for 11%

profile of v1, /device:TPU:0, one launch (start us, length us, event | category | flops | bytes accessed | tf_op | source)
XLA Modules:
  0.0 426.8 jit_solution(12632071861205285189)
XLA Ops:
  4.3 3.0 collective-permute-start
  8.0 1.4 dynamic-update-slice
  9.4 1.4 dynamic-update-slice.1
  10.8 1.4 dynamic-update-slice.2
  12.3 2.1 collective-permute-start.2
  14.4 2.5 constant_dynamic-slice_fusion.11
  16.9 2.4 constant_dynamic-slice_fusion.10
  19.3 2.0 collective-permute-start.7
  23.5 4.2 fusion.9
  30.5 3.8 bitcast_select_fusion
  41.8 18.0 %collective-permute-done.5 = bf16[384,1536]{1,0:T(8,128)(2,1)} collective-permute-done((bf16[384,1536]{1,0:T(8,128)(2,1)}, bf16[384,1536]{1,0:T(8,128)(2,1)}, u32[]{:S(2)}, u32[]{:S(2)}) %collective-permute-start.5) | collective-permute-done | bytes 1179680 | tf_op jit(solution)/shard_map/ppermute | solution.py:259
  59.8 24.4 %collective-permute-done.7 = bf16[768,768]{1,0:T(8,128)(2,1)} collective-permute-done((bf16[768,768]{1,0:T(8,128)(2,1)}, bf16[768,768]{1,0:T(8,128)(2,1)}, u32[]{:S(2)}, u32[]{:S(2)}) %collective-permute-start.7) | collective-permute-done | bytes 1179680 | tf_op jit(solution)/shard_map/ppermute | solution.py:259
  84.2 1.3 broadcast_select_fusion.5
  85.7 2.1 pad_maximum_fusion.3.w_ref
  87.9 19.9 %shard_map.305 = (bf16[2,768,1152]{2,1,0:T(8,128)(2,1)}, bf16[3,12,256,256]{3,2,1,0:T(8,128)(2,1)}, bf16[2,768,384]{2,1,0:T(8,128)(2,1)}, f32[768,768]{1,0:T(8,1...) custom-call(bf16[768,768]{1,0:T(8,128)(2,1)} %get-tuple-element.99.x_ref, ...), custom_call_target="tpu_custom_call" | custom-call | flops 3623878656 | bytes 18902016 | tf_op jit(solution)/shard_map/pallas_call | solution.py:239
  107.7 1.4 broadcast_select_fusion.3
  109.3 1.5 copy-done
  110.8 2.6 pad_maximum_fusion.up_ref
  113.4 1.4 broadcast_select_fusion.1
  115.0 1.5 copy-done.1
  116.5 2.6 pad_maximum_fusion.1.down_ref
  119.1 47.0 %shard_map.306 = (bf16[768,768]{1,0:T(8,128)(2,1)}, bf16[2,768,1536]{2,1,0:T(8,128)(2,1)}, bf16[2,768,1536]{2,1,0:T(8,128)(2,1)}, f32[768,768]{1,0:T(8,128)}, f32[8,768]{1,0:T(8,128)}, /*index=5*/f32[2,1,1536]{2,1,0:T(1,128)}) custom-call(bf16[768,768]{1,0:T(8,128)(2,1)} %get-tuple-element.33.low_ref, f32[768,768]{1,0:T(8,128)} %get-tuple-element.34.xhat_ref, ...), custom_call_target="tpu_custom_call" | custom-call | flops 21743271936 | bytes 27199488 | tf_op jit(solution)/shard_map/pallas_call | solution.py:239
  166.1 3.4 dynamic-slice_bitcast_fusion
  170.0 1.7 dynamic-slice_bitcast_fusion.1
  171.7 29.2 %shard_map.307 = (bf16[768,768]{1,0:T(8,128)(2,1)}, bf16[2,768,1152]{2,1,0:T(8,128)(2,1)}, bf16[2,768,384]{2,1,0:T(8,128)(2,1)}, f32[2,1,1152]{2,1,0:T(1,128)}) custom-call(bf16[768,768]{1,0:T(8,128)(2,1)} %get-tuple-element.99.x_ref, f32[768,768]{1,0:T(8,128)} %get-tuple-element.37.d_resid_ref, bf16[2,768,1152]{2,1,0:T(8,128)(2,1)} %pad_maximum_fusion.3.w_ref, ...), custom_call_target="tpu_custom_call" | custom-call | flops 7247757312 | bytes 23602176 | tf_op jit(solution)/shard_map/pallas_call | solution.py:239
  200.8 1.8 collective-permute-start.10
  202.8 4.9 %pad_maximum_fusion.2 = bf16[2,768,1536]{2,1,0:T(8,128)(2,1)} fusion(bf16[2,768,384]{2,1,0:T(8,128)(2,1)} %get-tuple-element.43, bf16[2,768,1152]{2,1,0:T(8,128)(2,1)} %get-tuple-element.42), kind=kLoop, calls=%fused_computation.2 | loop fusion | flops 9437184 | bytes 9437184 | tf_op jit(solution)/shard_map/concatenate | solution.py:399
  208.3 3.3 dynamic-slice_bitcast_fusion.2
  211.7 78.0 %all-reduce = (f32[2,2304]{1,0:T(2,128)S(1)}, f32[8,768]{1,0:T(8,128)S(1)}) all-reduce(f32[2,2304]{1,0:T(2,128)S(1)} %broadcast_select_fusion.8, f32[8,768]{1,0:T(8,128)S(1)} %copy-done.8), channel_id=1, replica_groups=mesh['dp'=16,'mp'=2] {'dp','mp'}, use_global_device_ids=true, to_apply=%region_3.4 | all-reduce | flops 10752 | bytes 86016 | tf_op jit(solution)/shard_map/psum | solution.py:402
  292.8 2.4 select_bitcast_fusion.1
  295.5 1.6 copy.58
  297.2 1.6 copy.57
  299.5 2.8 fusion
  302.4 2.3 collective-permute-start.24
  304.7 2.4 fusion.1
  307.5 2.4 fusion.2
  310.0 1.9 collective-permute-start.12
  311.9 19.6 %collective-permute-done.24 = bf16[2,4,48,1536]{3,2,1,0:T(8,128)(2,1)S(1)} collective-permute-done((bf16[2,4,48,1536]{3,2,1,0:T(8,128)(2,1)S(1)}, bf16[2,4,48,1536]{3,2,1,0:T(8,128)(2,1)S(1)}, u32[]{:S(2)}, u32[]{:S(2)}) %collective-permute-start.24) | collective-permute-done | bytes 1179680 | tf_op jit(solution)/shard_map/ppermute | solution.py:267
  332.4 1.6 collective-permute-start.26
  334.1 1.8 collective-permute-start.27
  335.8 21.0 %collective-permute-done.18 = bf16[2,4,48,1536]{3,2,1,0:T(8,128)(2,1)S(1)} collective-permute-done((bf16[2,4,48,1536]{3,2,1,0:T(8,128)(2,1)S(1)}, bf16[2,4,48,1536]{3,2,1,0:T(8,128)(2,1)S(1)}, u32[]{:S(2)}, u32[]{:S(2)}) %collective-permute-start.18) | collective-permute-done | bytes 1179680 | tf_op jit(solution)/shard_map/ppermute | solution.py:267
  357.7 22.3 %collective-permute-done.12 = bf16[2,4,48,1536]{3,2,1,0:T(8,128)(2,1)S(1)} collective-permute-done((bf16[2,4,48,1536]{3,2,1,0:T(8,128)(2,1)S(1)}, bf16[2,4,48,1536]{3,2,1,0:T(8,128)(2,1)S(1)}, u32[]{:S(2)}, u32[]{:S(2)}) %collective-permute-start.12) | collective-permute-done | bytes 1179680 | tf_op jit(solution)/shard_map/ppermute | solution.py:267
  380.9 2.3 collective-permute-start.21
  383.2 2.2 collective-permute-start.14
  385.6 1.7 collective-permute-start.15
  387.3 16.6 %collective-permute-done.20 = bf16[2,1,48,1536]{3,2,1,0:T(8,128)(2,1)S(1)} collective-permute-done((bf16[2,1,48,1536]{3,2,1,0:T(8,128)(2,1)S(1)}, bf16[2,1,48,1536]{3,2,1,0:T(8,128)(2,1)S(1)}, u32[]{:S(2)}, u32[]{:S(2)}) %collective-permute-start.20) | collective-permute-done | bytes 294944 | tf_op jit(solution)/shard_map/ppermute | solution.py:267
  406.1 13.2 %collective-permute-done.14 = bf16[2,1,48,1536]{3,2,1,0:T(8,128)(2,1)S(1)} collective-permute-done((bf16[2,1,48,1536]{3,2,1,0:T(8,128)(2,1)S(1)}, bf16[2,1,48,1536]{3,2,1,0:T(8,128)(2,1)S(1)}, u32[]{:S(2)}, u32[]{:S(2)}) %collective-permute-start.14) | collective-permute-done | bytes 294944 | tf_op jit(solution)/shard_map/ppermute | solution.py:267
  421.3 4.0 collective-permute-done.16
  (176 shorter events, 31.7 us)
Async XLA Ops:
  1.9 5.4 %copy-start.3 = (bf16[384,768]{1,0:T(8,128)(2,1)S(1)}, bf16[384,768]{1,0:T(8,128)(2,1)}, u32[]{:S(2)}) copy-start(bf16[384,768]{1,0:T(8,128)(2,1)} %param.25) | copy-start | bytes 1769476
  1.9 6.1 %copy-start.24 = (bf16[384]{0:T(512)(128)(2,1)S(1)}, bf16[384]{0:T(512)(128)(2,1)}, u32[]{:S(2)}) copy-start(bf16[384]{0:T(512)(128)(2,1)} %param.21) | copy-start | bytes 2308
  1.9 7.5 %copy-start.25 = (bf16[384]{0:T(512)(128)(2,1)S(1)}, bf16[384]{0:T(512)(128)(2,1)}, u32[]{:S(2)}) copy-start(bf16[384]{0:T(512)(128)(2,1)} %param.24) | copy-start | bytes 2308
  1.9 8.9 %copy-start.16 = (bf16[1536]{0:T(1024)(128)(2,1)S(1)}, bf16[1536]{0:T(1024)(128)(2,1)}, u32[]{:S(2)}) copy-start(bf16[1536]{0:T(1024)(128)(2,1)} %param.30) | copy-start | bytes 9220
  4.3 33.5 %collective-permute-start = (bf16[384,1152]{1,0:T(8,128)(2,1)}, bf16[384,1152]{1,0:T(8,128)(2,1)}, u32[]{:S(2)}, u32[]{:S(2)}) collective-permute-start(bf16[384,1152]{1,0:T(8,128)(2,1)} %constant_dynamic-slice_fusion.13), channel_id=1, source_target_pairs={{0,1},{1,0},{2,3},{3,2},{4,5},{5,4},{6,7},{7,6},{8,9},{9,8},{10,11... | collective-permute-start | bytes 2654216 | tf_op jit(solution)/shard_map/ppermute | solution.py:259
  8.0 29.7 %collective-permute-start.3 = (bf16[192,768]{1,0:T(8,128)(2,1)}, bf16[192,768]{1,0:T(8,128)(2,1)}, u32[]{:S(2)}, u32[]{:S(2)}) collective-permute-start(bf16[192,768]{1,0:T(8,128)(2,1)} %constant_dynamic-slice_fusion.12), channel_id=1, source_target_pairs={{0,1},{1,0},{2,3},{3,2},{4,5},{5,4},{6,7},{7,6},{8,9},{9,8},{10,11... | collective-permute-start | bytes 884744 | tf_op jit(solution)/shard_map/ppermute | solution.py:259
  12.3 9.0 %copy-start.12 = (s32[3,8]{1,0:T(4,128)S(1)}, s32[3,8]{1,0:T(4,128)}, u32[]{:S(2)}) copy-start(s32[3,8]{1,0:T(4,128)} %param.19) | copy-start | bytes 292
  12.3 10.5 %copy-start.18 = (bf16[768]{0:T(1024)(128)(2,1)S(1)}, bf16[768]{0:T(1024)(128)(2,1)}, u32[]{:S(2)}) copy-start(bf16[768]{0:T(1024)(128)(2,1)} %param.27) | copy-start | bytes 4612
  12.3 10.5 %copy-start.19 = (bf16[768]{0:T(1024)(128)(2,1)S(1)}, bf16[768]{0:T(1024)(128)(2,1)}, u32[]{:S(2)}) copy-start(bf16[768]{0:T(1024)(128)(2,1)} %param.28) | copy-start | bytes 4612
  12.3 10.5 %copy-start.20 = (bf16[768]{0:T(1024)(128)(2,1)S(1)}, bf16[768]{0:T(1024)(128)(2,1)}, u32[]{:S(2)}) copy-start(bf16[768]{0:T(1024)(128)(2,1)} %param.32) | copy-start | bytes 4612
  12.3 10.5 %copy-start.21 = (bf16[768]{0:T(1024)(128)(2,1)S(1)}, bf16[768]{0:T(1024)(128)(2,1)}, u32[]{:S(2)}) copy-start(bf16[768]{0:T(1024)(128)(2,1)} %param.33) | copy-start | bytes 4612
  12.3 10.6 %copy-start.22 = (bf16[768]{0:T(1024)(128)(2,1)S(1)}, bf16[768]{0:T(1024)(128)(2,1)}, u32[]{:S(2)}) copy-start(bf16[768]{0:T(1024)(128)(2,1)} %param.34) | copy-start | bytes 4612
  12.3 24.7 %collective-permute-start.2 = (bf16[2304]{0:T(1024)(128)(2,1)}, bf16[2304]{0:T(1024)(128)(2,1)}, u32[]{:S(2)}, u32[]{:S(2)}) collective-permute-start(bf16[2304]{0:T(1024)(128)(2,1)} %dynamic-update-slice.2), channel_id=1, source_target_pairs={{0,1},{1,0},{2,3},{3,2},{4,5},{5,4},{6,7},{7,6},{8,9},{9,8},{10,11... | collective-permute-start | bytes 13832 | tf_op jit(solution)/shard_map/ppermute | solution.py:259
  16.9 42.9 %collective-permute-start.5 = (bf16[384,1536]{1,0:T(8,128)(2,1)}, bf16[384,1536]{1,0:T(8,128)(2,1)}, u32[]{:S(2)}, u32[]{:S(2)}) collective-permute-start(bf16[384,1536]{1,0:T(8,128)(2,1)} %constant_dynamic-slice_fusion.11), channel_id=1, source_target_pairs={{0,1},{1,0},{2,3},{3,2},{4,5},{5,4},{6,7},{7,6},{8,9},{9,8},{10,11... | collective-permute-start | bytes 3538952 | tf_op jit(solution)/shard_map/ppermute | solution.py:259
  19.3 64.9 %collective-permute-start.7 = (bf16[768,768]{1,0:T(8,128)(2,1)}, bf16[768,768]{1,0:T(8,128)(2,1)}, u32[]{:S(2)}, u32[]{:S(2)}) collective-permute-start(bf16[768,768]{1,0:T(8,128)(2,1)} %constant_dynamic-slice_fusion.10), channel_id=1, source_target_pairs={{0,1},{1,0},{2,3},{3,2},{4,5},{5,4},{6,7},{7,6},{8,9},{9,8},{10,11... | collective-permute-start | bytes 3538952 | tf_op jit(solution)/shard_map/ppermute | solution.py:259
  30.5 5.9 %copy-start.23 = (bf16[768]{0:T(1024)(128)(2,1)S(1)}, bf16[768]{0:T(1024)(128)(2,1)}, u32[]{:S(2)}) copy-start(bf16[768]{0:T(1024)(128)(2,1)} %param.26) | copy-start | bytes 4612
  37.7 1.9 collective-permute-start.4
  37.8 46.4 %collective-permute-start.1 = (bf16[384,1152]{1,0:T(8,128)(2,1)}, bf16[384,1152]{1,0:T(8,128)(2,1)S(1)}, u32[]{:S(2)}, u32[]{:S(2)}) collective-permute-start(bf16[384,1152]{1,0:T(8,128)(2,1)} %collective-permute-done), channel_id=1, source_target_pairs={{0,2},{2,0},{4,6},{6,4},{8,10},{10,8},{12,14},{14,12},{16,18},{18,... | collective-permute-start | bytes 2654216 | tf_op jit(solution)/shard_map/ppermute | solution.py:267
  59.8 48.0 %collective-permute-start.6 = (bf16[384,1536]{1,0:T(8,128)(2,1)}, bf16[384,1536]{1,0:T(8,128)(2,1)S(1)}, u32[]{:S(2)}, u32[]{:S(2)}) collective-permute-start(bf16[384,1536]{1,0:T(8,128)(2,1)} %collective-permute-done.5), channel_id=1, source_target_pairs={{0,2},{2,0},{4,6},{6,4},{8,10},{10,8},{12,14},{14,12},{16,18},{18,... | collective-permute-start | bytes 3538952 | tf_op jit(solution)/shard_map/ppermute | solution.py:267
  84.2 29.2 %collective-permute-start.8 = (bf16[768,768]{1,0:T(8,128)(2,1)}, bf16[768,768]{1,0:T(8,128)(2,1)S(1)}, u32[]{:S(2)}, u32[]{:S(2)}) collective-permute-start(bf16[768,768]{1,0:T(8,128)(2,1)} %collective-permute-done.7), channel_id=1, source_target_pairs={{0,2},{2,0},{4,6},{6,4},{8,10},{10,8},{12,14},{14,12},{16,18},{18,... | collective-permute-start | bytes 3538952 | tf_op jit(solution)/shard_map/ppermute | solution.py:267
  169.5 129.3 %collective-permute-start.23 = (bf16[2,8,48,1536]{3,2,1,0:T(8,128)(2,1)}, bf16[2,8,48,1536]{3,2,1,0:T(8,128)(2,1)}, u32[]{:S(2)}, u32[]{:S(2)}) collective-permute-start(bf16[2,8,48,1536]{3,2,1,0:T(8,128)(2,1)} %dynamic-slice_bitcast_fusion), channel_id=1, source_target_pairs={{0,2},{2,0},{4,6},{6,4},{8,10},{10,8},{12,14},{14,12},{16,18},{18,... | collective-permute-start | bytes 7077896 | tf_op jit(solution)/shard_map/ppermute | solution.py:267
  171.7 133.1 %collective-permute-start.17 = (bf16[2,8,48,1536]{3,2,1,0:T(8,128)(2,1)}, bf16[2,8,48,1536]{3,2,1,0:T(8,128)(2,1)}, u32[]{:S(2)}, u32[]{:S(2)}) collective-permute-start(bf16[2,8,48,1536]{3,2,1,0:T(8,128)(2,1)} %dynamic-slice_bitcast_fusion.1), channel_id=1, source_target_pairs={{0,2},{2,0},{4,6},{6,4},{8,10},{10,8},{12,14},{14,12},{16,18},{18,... | collective-permute-start | bytes 7077896 | tf_op jit(solution)/shard_map/ppermute | solution.py:267
  171.7 30.9 %copy-start.4 = (bf16[768,768]{1,0:T(8,128)(2,1)S(1)}, bf16[768,768]{1,0:T(8,128)(2,1)}, u32[]{:S(2)}) copy-start(bf16[768,768]{1,0:T(8,128)(2,1)} %get-tuple-element.36) | copy-start | bytes 3538948
  200.8 90.9 %collective-permute-start.10 = (bf16[3,256,768]{2,1,0:T(8,128)(2,1)}, bf16[3,256,768]{2,1,0:T(8,128)(2,1)S(1)}, u32[]{:S(2)}, u32[]{:S(2)}) collective-permute-start(bf16[3,256,768]{2,1,0:T(8,128)(2,1)} %bitcast.147), channel_id=1, source_target_pairs={{0,1},{1,0},{2,3},{3,2},{4,5},{5,4},{6,7},{7,6},{8,9},{9,8},{10,11... | collective-permute-start | bytes 3538952 | tf_op jit(solution)/shard_map/ppermute | solution.py:259
  202.6 89.2 %collective-permute-start.9 = (bf16[3,256,768]{2,1,0:T(8,128)(2,1)S(1)}, bf16[3,256,768]{2,1,0:T(8,128)(2,1)}, u32[]{:S(2)}, u32[]{:S(2)}) collective-permute-start(bf16[3,256,768]{2,1,0:T(8,128)(2,1)S(1)} %bitcast.145), channel_id=1, source_target_pairs={{0,1},{1,0},{2,3},{3,2},{4,5},{5,4},{6,7},{7,6},{8,9},{9,8},{10,11... | collective-permute-start | bytes 3538952 | tf_op jit(solution)/shard_map/ppermute | solution.py:259
  202.8 4.9 %copy-start.17 = (f32[2,1,1152]{2,1,0:T(1,128)S(1)}, f32[2,1,1152]{2,1,0:T(1,128)}, u32[]{:S(2)}) copy-start(f32[2,1,1152]{2,1,0:T(1,128)} %get-tuple-element.44) | copy-start | bytes 27652
  202.8 4.9 %copy-start.9 = (f32[2,1,1536]{2,1,0:T(1,128)S(1)}, f32[2,1,1536]{2,1,0:T(1,128)}, u32[]{:S(2)}) copy-start(f32[2,1,1536]{2,1,0:T(1,128)} %get-tuple-element.45) | copy-start | bytes 36868
  208.3 84.5 %copy-start.15 = (pred[3,256]{1,0:T(4,128)(4,1)S(1)}, pred[3,256]{1,0:T(4,128)(4,1)}, u32[]{:S(2)}) copy-start(pred[3,256]{1,0:T(4,128)(4,1)} %get-tuple-element.60) | copy-start | bytes 2308
  211.6 95.9 %collective-permute-start.11 = (bf16[2,8,48,1536]{3,2,1,0:T(8,128)(2,1)}, bf16[2,8,48,1536]{3,2,1,0:T(8,128)(2,1)}, u32[]{:S(2)}, u32[]{:S(2)}) collective-permute-start(bf16[2,8,48,1536]{3,2,1,0:T(8,128)(2,1)} %dynamic-slice_bitcast_fusion.2), channel_id=1, source_target_pairs={{0,2},{2,0},{4,6},{6,4},{8,10},{10,8},{12,14},{14,12},{16,18},{18,... | collective-permute-start | bytes 7077896 | tf_op jit(solution)/shard_map/ppermute | solution.py:267
  297.2 7.5 %slice-start.2 = ((s8[4718592]{0:T(1024)(128)(4,1)}), s8[4194304]{0:T(1024)(128)(4,1)S(1)}, s32[]{:S(2)}) async-start(s8[4718592]{0:T(1024)(128)(4,1)} %bitcast.133), calls=%async_computation.2 | async-start | bytes 8388608
  298.8 5.9 %slice-start.3 = ((s8[4718592]{0:T(1024)(128)(4,1)}), s8[524288]{0:T(1024)(128)(4,1)S(1)}, s32[]{:S(2)}) async-start(s8[4718592]{0:T(1024)(128)(4,1)} %bitcast.133), calls=%async_computation.3 | async-start | bytes 1048576
  302.3 5.2 %slice-start = ((s8[4718592]{0:T(1024)(128)(4,1)}), s8[4194304]{0:T(1024)(128)(4,1)S(1)}, s32[]{:S(2)}) async-start(s8[4718592]{0:T(1024)(128)(4,1)} %bitcast.120), calls=%async_computation | async-start | bytes 8388608
  302.4 5.1 %slice-start.1 = ((s8[4718592]{0:T(1024)(128)(4,1)}), s8[524288]{0:T(1024)(128)(4,1)S(1)}, s32[]{:S(2)}) async-start(s8[4718592]{0:T(1024)(128)(4,1)} %bitcast.120), calls=%async_computation.1 | async-start | bytes 1048576
  302.4 29.1 %collective-permute-start.24 = (bf16[2,4,48,1536]{3,2,1,0:T(8,128)(2,1)S(1)}, bf16[2,4,48,1536]{3,2,1,0:T(8,128)(2,1)S(1)}, u32[]{:S(2)}, u32[]{:S(2)}) collective-permute-start(bf16[2,4,48,1536]{3,2,1,0:T(8,128)(2,1)S(1)} %dynamic-slice_bitcast_fusion.3), channel_id=1, source_target_pairs={{0,4},{2,6},{4,0},{6,2},{8,12},{10,14},{12,8},{14,10},{16,20},{18,... | collective-permute-start | bytes 3538952 | tf_op jit(solution)/shard_map/ppermute | solution.py:267
  307.2 49.6 %collective-permute-start.18 = (bf16[2,4,48,1536]{3,2,1,0:T(8,128)(2,1)S(1)}, bf16[2,4,48,1536]{3,2,1,0:T(8,128)(2,1)S(1)}, u32[]{:S(2)}, u32[]{:S(2)}) collective-permute-start(bf16[2,4,48,1536]{3,2,1,0:T(8,128)(2,1)S(1)} %dynamic-slice_bitcast_fusion.4), channel_id=1, source_target_pairs={{0,4},{2,6},{4,0},{6,2},{8,12},{10,14},{12,8},{14,10},{16,20},{18,... | collective-permute-start | bytes 3538952 | tf_op jit(solution)/shard_map/ppermute | solution.py:267
  310.0 70.0 %collective-permute-start.12 = (bf16[2,4,48,1536]{3,2,1,0:T(8,128)(2,1)S(1)}, bf16[2,4,48,1536]{3,2,1,0:T(8,128)(2,1)S(1)}, u32[]{:S(2)}, u32[]{:S(2)}) collective-permute-start(bf16[2,4,48,1536]{3,2,1,0:T(8,128)(2,1)S(1)} %dynamic-slice_bitcast_fusion.5), channel_id=1, source_target_pairs={{0,4},{2,6},{4,0},{6,2},{8,12},{10,14},{12,8},{14,10},{16,20},{18,... | collective-permute-start | bytes 3538952 | tf_op jit(solution)/shard_map/ppermute | solution.py:267
  331.9 49.0 %collective-permute-start.25 = (bf16[2,1,48,1536]{3,2,1,0:T(8,128)(2,1)S(1)}, bf16[2,1,48,1536]{3,2,1,0:T(8,128)(2,1)S(1)}, u32[]{:S(2)}, u32[]{:S(2)}) collective-permute-start(bf16[2,1,48,1536]{3,2,1,0:T(8,128)(2,1)S(1)} %get-tuple-element.75), channel_id=1, source_target_pairs={{0,8},{2,10},{4,12},{6,14},{8,16},{10,18},{12,20},{14,22},{16,24},... | collective-permute-start | bytes 884744 | tf_op jit(solution)/shard_map/ppermute | solution.py:267
  332.4 50.8 %collective-permute-start.26 = (bf16[2,1,48,1536]{3,2,1,0:T(8,128)(2,1)S(1)}, bf16[2,1,48,1536]{3,2,1,0:T(8,128)(2,1)S(1)}, u32[]{:S(2)}, u32[]{:S(2)}) collective-permute-start(bf16[2,1,48,1536]{3,2,1,0:T(8,128)(2,1)S(1)} %get-tuple-element.77), channel_id=1, source_target_pairs={{0,16},{2,18},{4,20},{6,22},{8,24},{10,26},{12,28},{14,30},{16,0},... | collective-permute-start | bytes 884744 | tf_op jit(solution)/shard_map/ppermute | solution.py:267
  334.1 49.2 %collective-permute-start.27 = (bf16[2,1,48,1536]{3,2,1,0:T(8,128)(2,1)S(1)}, bf16[2,1,48,1536]{3,2,1,0:T(8,128)(2,1)S(1)}, u32[]{:S(2)}, u32[]{:S(2)}) collective-permute-start(bf16[2,1,48,1536]{3,2,1,0:T(8,128)(2,1)S(1)} %get-tuple-element.76), channel_id=1, source_target_pairs={{0,24},{2,26},{4,28},{6,30},{8,0},{10,2},{12,4},{14,6},{16,8},{18,... | collective-permute-start | bytes 884744 | tf_op jit(solution)/shard_map/ppermute | solution.py:267
  357.2 28.3 %collective-permute-start.19 = (bf16[2,1,48,1536]{3,2,1,0:T(8,128)(2,1)S(1)}, bf16[2,1,48,1536]{3,2,1,0:T(8,128)(2,1)S(1)}, u32[]{:S(2)}, u32[]{:S(2)}) collective-permute-start(bf16[2,1,48,1536]{3,2,1,0:T(8,128)(2,1)S(1)} %get-tuple-element.78), channel_id=1, source_target_pairs={{0,8},{2,10},{4,12},{6,14},{8,16},{10,18},{12,20},{14,22},{16,24},... | collective-permute-start | bytes 884744 | tf_op jit(solution)/shard_map/ppermute | solution.py:267
  380.0 23.9 %collective-permute-start.20 = (bf16[2,1,48,1536]{3,2,1,0:T(8,128)(2,1)S(1)}, bf16[2,1,48,1536]{3,2,1,0:T(8,128)(2,1)S(1)}, u32[]{:S(2)}, u32[]{:S(2)}) collective-permute-start(bf16[2,1,48,1536]{3,2,1,0:T(8,128)(2,1)S(1)} %get-tuple-element.80), channel_id=1, source_target_pairs={{0,16},{2,18},{4,20},{6,22},{8,24},{10,26},{12,28},{14,30},{16,0},... | collective-permute-start | bytes 884744 | tf_op jit(solution)/shard_map/ppermute | solution.py:267
  380.9 23.7 %collective-permute-start.21 = (bf16[2,1,48,1536]{3,2,1,0:T(8,128)(2,1)S(1)}, bf16[2,1,48,1536]{3,2,1,0:T(8,128)(2,1)S(1)}, u32[]{:S(2)}, u32[]{:S(2)}) collective-permute-start(bf16[2,1,48,1536]{3,2,1,0:T(8,128)(2,1)S(1)} %get-tuple-element.79), channel_id=1, source_target_pairs={{0,24},{2,26},{4,28},{6,30},{8,0},{10,2},{12,4},{14,6},{16,8},{18,... | collective-permute-start | bytes 884744 | tf_op jit(solution)/shard_map/ppermute | solution.py:267
  383.2 22.9 %collective-permute-start.13 = (bf16[2,1,48,1536]{3,2,1,0:T(8,128)(2,1)S(1)}, bf16[2,1,48,1536]{3,2,1,0:T(8,128)(2,1)S(1)}, u32[]{:S(2)}, u32[]{:S(2)}) collective-permute-start(bf16[2,1,48,1536]{3,2,1,0:T(8,128)(2,1)S(1)} %get-tuple-element.81), channel_id=1, source_target_pairs={{0,8},{2,10},{4,12},{6,14},{8,16},{10,18},{12,20},{14,22},{16,24},... | collective-permute-start | bytes 884744 | tf_op jit(solution)/shard_map/ppermute | solution.py:267
  383.2 36.1 %collective-permute-start.14 = (bf16[2,1,48,1536]{3,2,1,0:T(8,128)(2,1)S(1)}, bf16[2,1,48,1536]{3,2,1,0:T(8,128)(2,1)S(1)}, u32[]{:S(2)}, u32[]{:S(2)}) collective-permute-start(bf16[2,1,48,1536]{3,2,1,0:T(8,128)(2,1)S(1)} %get-tuple-element.83), channel_id=1, source_target_pairs={{0,16},{2,18},{4,20},{6,22},{8,24},{10,26},{12,28},{14,30},{16,0},... | collective-permute-start | bytes 884744 | tf_op jit(solution)/shard_map/ppermute | solution.py:267
  385.6 33.8 %collective-permute-start.15 = (bf16[2,1,48,1536]{3,2,1,0:T(8,128)(2,1)S(1)}, bf16[2,1,48,1536]{3,2,1,0:T(8,128)(2,1)S(1)}, u32[]{:S(2)}, u32[]{:S(2)}) collective-permute-start(bf16[2,1,48,1536]{3,2,1,0:T(8,128)(2,1)S(1)} %get-tuple-element.82), channel_id=1, source_target_pairs={{0,24},{2,26},{4,28},{6,30},{8,0},{10,2},{12,4},{14,6},{16,8},{18,... | collective-permute-start | bytes 884744 | tf_op jit(solution)/shard_map/ppermute | solution.py:267
  403.9 16.7 %collective-permute-start.28 = (bf16[48,1536]{1,0:T(8,128)(2,1)S(1)}, bf16[48,1536]{1,0:T(8,128)(2,1)S(1)}, u32[]{:S(2)}, u32[]{:S(2)}) collective-permute-start(bf16[48,1536]{1,0:T(8,128)(2,1)S(1)} %slice_bitcast_fusion), channel_id=1, source_target_pairs={{0,1},{1,0},{2,3},{3,2},{4,5},{5,4},{6,7},{7,6},{8,9},{9,8},{10,11... | collective-permute-start | bytes 442376 | tf_op jit(solution)/shard_map/ppermute | solution.py:259
  404.8 21.2 %collective-permute-start.22 = (bf16[48,1536]{1,0:T(8,128)(2,1)S(1)}, bf16[48,1536]{1,0:T(8,128)(2,1)S(1)}, u32[]{:S(2)}, u32[]{:S(2)}) collective-permute-start(bf16[48,1536]{1,0:T(8,128)(2,1)S(1)} %slice_bitcast_fusion.2), channel_id=1, source_target_pairs={{0,1},{1,0},{2,3},{3,2},{4,5},{5,4},{6,7},{7,6},{8,9},{9,8},{10,11... | collective-permute-start | bytes 442376 | tf_op jit(solution)/shard_map/ppermute | solution.py:259
  419.5 5.7 %collective-permute-start.16 = (bf16[48,1536]{1,0:T(8,128)(2,1)S(1)}, bf16[48,1536]{1,0:T(8,128)(2,1)S(1)}, u32[]{:S(2)}, u32[]{:S(2)}) collective-permute-start(bf16[48,1536]{1,0:T(8,128)(2,1)S(1)} %slice_bitcast_fusion.4), channel_id=1, source_target_pairs={{0,1},{1,0},{2,3},{3,2},{4,5},{5,4},{6,7},{7,6},{8,9},{9,8},{10,11... | collective-permute-start | bytes 442376 | tf_op jit(solution)/shard_map/ppermute | solution.py:259
  (13 other events, 29.3 us)

commit v2 on v1

--- a/solution.py
+++ b/solution.py
@@ -15,6 +15,7 @@
 BF16 = jnp.bfloat16
 CHUNK = 512
 VMEM_LIMIT = 60 * 1024 * 1024
+MESH = pl.DeviceIdType.MESH
 
 
 def mm(a, b):
@@ -91,8 +92,25 @@
     )
 
 
+def add_rows(dst, src, offset, step):
+    step = min(step, dst.shape[0])
+
+    @pl.loop(0, dst.shape[0] // step)
+    def _(i):
+        here = pl.ds(pl.multiple_of(i * step, step), step)
+        there = pl.ds(pl.multiple_of(offset + i * step, step), step)
+        dst[here, :] = (dst[here, :].astype(F32) + src[there, :].astype(F32)).astype(dst.dtype)
+
+
+def store_by_owner(dst, value, at, n):
+    rows = value.shape[0] // n
+    for d in range(n):
+        place = (d % 2) * (n // 2) + (d // 2 % 2) * (n // 4) + d // 4
+        dst[place * rows : (place + 1) * rows, at] = value[d * rows : (d + 1) * rows, :]
+
+
 def feed_forward(
-    low_ref, xhat_ref, rstd_ref, up_ref, ub_ref, down_ref, vec_ref, cot_ref,
+    n, low_ref, xhat_ref, rstd_ref, up_ref, ub_ref, down_ref, vec_ref, cot_ref,
     out_ref, gd_ref, gu_ref, d_resid_ref, small_ref, ubg_ref,
     act_ref, slope_ref, acc_ref, dffn_ref, dffn_t_ref, low_t_ref,
 ):
@@ -101,7 +119,13 @@
     step = min(CHUNK, hidden)
     per = hidden // step
     block = 256
-    low_t_ref[...] = low_ref[...].T
+    def put(dst, v):
+        if n:
+            store_by_owner(dst, v, slice(None), n)
+        else:
+            dst[...] = v
+
+    put(low_t_ref, low_ref[...].T)
     acc_ref[...] = jnp.zeros_like(acc_ref)
 
     @pl.loop(0, groups * per)
@@ -143,7 +167,7 @@
         small_ref[4:5, :] += jnp.sum(cot * xhat, 0, keepdims=True)
         small_ref[5:6, :] += jnp.sum(cot, 0, keepdims=True)
 
-    dffn_t_ref[...] = dffn_ref[...].T
+    put(dffn_t_ref, dffn_ref[...].T)
 
     @pl.loop(0, groups * per)
     def _(i):
@@ -175,74 +199,263 @@
         small_ref[2:3, :] += jnp.sum(d_normed, 0, keepdims=True)
 
 
+def backward_sequence(s, put, d_resid_ref, w_ref, wo_ref, qkv_ref, p_ref, in_ref, dq_ref):
+    length, groups, width = p_ref.shape[2], wo_ref.shape[0], wo_ref.shape[1]
+    pairs = width // PAIR
+    rows = pl.ds(pl.multiple_of(s * length, length), length)
+    d_resid = d_resid_ref[rows, :]
+    d_attn = d_resid.astype(BF16)
+    put(d_attn.T, rows)
+    total = d_resid
+    for g in range(groups):
+        d_ctx = mm_t(d_attn, wo_ref[g]).astype(BF16)
+        for p in range(pairs):
+            at = slice(p * PAIR, (p + 1) * PAIR)
+            q_at, k_at, v_at = (slice(o * width + p * PAIR, o * width + (p + 1) * PAIR) for o in range(3))
+            value = qkv_ref[g, rows, v_at]
+            q_pair = halves(qkv_ref[g, rows, q_at])
+            k_pair = halves(qkv_ref[g, rows, k_at])
+            c_pair = halves(d_ctx[:, at])
+            dq = dk = dv = None
+            for h in range(2):
+                low = p_ref[s, (g * pairs + p) * 2 + h]
+                probs = low.astype(F32)
+                d_probs = mm_t(c_pair[h], value)
+                inner = jnp.sum(probs * d_probs, -1, keepdims=True)
+                d_scores = (probs * (d_probs - inner)).astype(BF16)
+                dv_h = t_mm(low, c_pair[h])
+                dq_h = mm(d_scores, k_pair[h])
+                dk_h = t_mm(d_scores, q_pair[h])
+                dq = dq_h if dq is None else dq + dq_h
+                dk = dk_h if dk is None else dk + dk_h
+                dv = dv_h if dv is None else dv + dv_h
+            dq_ref[g, rows, q_at] = (0.125 * dq).astype(BF16)
+            dq_ref[g, rows, k_at] = dk.astype(BF16)
+            dq_ref[g, rows, v_at] = dv.astype(BF16)
+        total = total + mm_t(dq_ref[g, rows, :], w_ref[g])
+    in_ref[rows, :] = total.astype(BF16)
+
+
+def weight_products(g, x_t_ref, dattn_t_ref, dq_ref, ctx_ref, ga_ref):
+    block, wide = 256, dq_ref.shape[2]
+
+    @pl.loop(0, x_t_ref.shape[0] // block)
+    def _(b):
+        rows = pl.ds(pl.multiple_of(b * block, block), block)
+        ga_ref[g, rows, :wide] = mm(x_t_ref[rows, :], dq_ref[g]).astype(BF16)
+        ga_ref[g, rows, wide:] = mm(dattn_t_ref[rows, :], ctx_ref[g]).astype(BF16)
+
+
+def attention_backward_plain(
+    x_ref, d_resid_ref, w_ref, wo_ref, qkv_ref, p_ref, ctx_ref,
+    in_ref, ga_ref, bg_ref,
+    dq_ref, dattn_t_ref, x_t_ref,
+):
+    groups, width = wo_ref.shape[0], wo_ref.shape[1]
+    x_t_ref[...] = x_ref[...].T
+
+    def put(v, at):
+        dattn_t_ref[:, at] = v
+
+    @pl.loop(0, p_ref.shape[0])
+    def _(s):
+        backward_sequence(s, put, d_resid_ref, w_ref, wo_ref, qkv_ref, p_ref, in_ref, dq_ref)
+
+    for g in range(groups):
+        bg_ref[g] = jnp.sum(dq_ref[g].astype(F32), 0, keepdims=True)
+        weight_products(g, x_t_ref, dattn_t_ref, dq_ref, ctx_ref, ga_ref)
+
+
 def attention_backward(
-    x_ref, d_resid_ref, w_ref, wo_ref, qkv_ref, p_ref, ctx_ref,
-    in_ref, gq_ref, go_ref, bg_ref,
-    dq_ref, dattn_t_ref, x_t_ref,
+    n, x_ref, d_resid_ref, w_ref, wo_ref, qkv_ref, p_ref, ctx_ref, small_ref, ubg_ref, gd_ref, gu_ref, own_ref,
+    in_ref, in_peer_ref, out_peer_ref, rd_ref, ru_ref, ra_ref, sums_ref,
+    dq_ref, dattn_t_ref, x_t_ref, ga_ref, kept, half, quarter, owned, shard, tiny, tiny_1, tiny_2, tiny_x, tiny_z,
+    send, recv, send_z, recv_z, send_in, recv_in, local,
 ):
     seqs, length = p_ref.shape[0], p_ref.shape[2]
     groups, width = wo_ref.shape[0], wo_ref.shape[1]
     model = x_ref.shape[1]
-    pairs = width // PAIR
-    block = 256
-    x_t_ref[...] = x_ref[...].T
+    rows_own = model // n
+    depth = n // 4
+    index = lax.axis_index("dp")
+    x_index = lax.axis_index("mp")
+    core, line, rest = index % 2, index // 2 % 2, index // 4
+    to_core = {"dp": index + 1 - 2 * core}
+    to_line = {"dp": index + 2 - 4 * line}
+    to_x = {"mp": 1 - x_index}
+
+    def to_rest(k):
+        return {"dp": (rest + k) % depth * 4 + index % 4}
+
+    barrier = pltpu.get_barrier_semaphore()
+    peers = [to_core, to_line, to_x] + [to_rest(k) for k in range(1, depth)]
+    for peer in peers:
+        pl.semaphore_signal(barrier, inc=1, device_id=peer, device_id_type=MESH)
+    pl.semaphore_wait(barrier, len(peers))
+
+    def remote(src, dst, s, r, device):
+        return pltpu.make_async_remote_copy(
+            src_ref=src, dst_ref=dst, send_sem=s, recv_sem=r, device_id=device, device_id_type=MESH
+        )
+
+    n_half, n_quarter = model // 2, model // 4
+    sources = (gd_ref, gu_ref, ga_ref)
+
+    def by_core(t):
+        there = pl.ds(pl.multiple_of((1 - core) * n_half, n_half), n_half)
+        return remote(sources[t].at[:, there, :], half.at[t], send.at[0, t], recv.at[0, t], to_core)
+
+    def by_line(t):
+        there = pl.ds(pl.multiple_of((1 - line) * n_quarter, n_quarter), n_quarter)
+        return remote(half.at[t, :, there, :], quarter.at[t], send.at[1, t], recv.at[1, t], to_line)
+
+    def by_x(t):
+        return remote(quarter.at[t, 1], owned.at[t], send.at[2, t], recv.at[2, t], to_x)
+
+    def by_rest(t, k):
+        there = pl.ds(pl.multiple_of((rest + k) % depth * rows_own, rows_own), rows_own)
+        return remote(
+            owned.at[t, there, :], shard.at[t, k - 1], send_z.at[t, k - 1], recv_z.at[t, k - 1], to_rest(k)
+        )
+
+    def keep(t):
+        here = pl.ds(pl.multiple_of(core * n_half, n_half), n_half)
+        return pltpu.make_async_copy(sources[t].at[:, here, :], kept.at[t], local.at[t])
+
+    def after_core(t):
+        by_core(t).wait_recv()
+        if t < 2:
+            keep(t).wait()
+        for g in range(groups):
+            if t < 2:
+                add_rows(half.at[t, g], kept.at[t, g], 0, 96)
+            else:
+                add_rows(half.at[t, g], ga_ref.at[g], core * n_half, 96)
+        by_line(t).start()
+
+    def after_line(t):
+        by_line(t).wait_recv()
+        for g in range(groups):
+            add_rows(quarter.at[t, g], half.at[t, g], line * n_quarter, 96)
+        by_x(t).start()
+
+    def after_x(t):
+        by_x(t).wait_recv()
+        add_rows(owned.at[t], quarter.at[t, 0], 0, 96)
+        for k in range(1, depth):
+            by_rest(t, k).start()
+
+    def after_rest(t, out):
+        total = owned[t, pl.ds(pl.multiple_of(rest * rows_own, rows_own), rows_own), :].astype(F32)
+        for k in range(1, depth):
+            by_rest(t, k).wait_recv()
+            total = total + shard[t, k - 1].astype(F32)
+        out[...] = total
+
+    def send_output():
+        return remote(own_ref, out_peer_ref, send.at[3, 0], recv.at[3, 0], to_x)
+
+    def send_input(s):
+        rows = pl.ds(pl.multiple_of(s * length, length), length)
+        return remote(in_ref.at[rows, :], in_peer_ref.at[rows, :], send_in.at[s], recv_in.at[s], to_x)
+
+    for t in range(2):
+        by_core(t).start()
+        keep(t).start()
+    send_output().start()
+    store_by_owner(x_t_ref, x_ref[...].T, slice(None), n)
 
     @pl.loop(0, seqs)
     def _(s):
-        rows = pl.ds(pl.multiple_of(s * length, length), length)
-        d_resid = d_resid_ref[rows, :]
-        d_attn = d_resid.astype(BF16)
-        dattn_t_ref[:, rows] = d_attn.T
-        total = d_resid
-        for g in range(groups):
-            d_ctx = mm_t(d_attn, wo_ref[g]).astype(BF16)
-            for p in range(pairs):
-                at = slice(p * PAIR, (p + 1) * PAIR)
-                q_at, k_at, v_at = (slice(o * width + p * PAIR, o * width + (p + 1) * PAIR) for o in range(3))
-                value = qkv_ref[g, rows, v_at]
-                q_pair = halves(qkv_ref[g, rows, q_at])
-                k_pair = halves(qkv_ref[g, rows, k_at])
-                c_pair = halves(d_ctx[:, at])
-                dq = dk = dv = None
-                for h in range(2):
-                    low = p_ref[s, (g * pairs + p) * 2 + h]
-                    probs = low.astype(F32)
-                    d_probs = mm_t(c_pair[h], value)
-                    inner = jnp.sum(probs * d_probs, -1, keepdims=True)
-                    d_scores = (probs * (d_probs - inner)).astype(BF16)
-                    dv_h = t_mm(low, c_pair[h])
-                    dq_h = mm(d_scores, k_pair[h])
-                    dk_h = t_mm(d_scores, q_pair[h])
-                    dq = dq_h if dq is None else dq + dq_h
-                    dk = dk_h if dk is None else dk + dk_h
-                    dv = dv_h if dv is None else dv + dv_h
-                dq_ref[g, rows, q_at] = (0.125 * dq).astype(BF16)
-                dq_ref[g, rows, k_at] = dk.astype(BF16)
-                dq_ref[g, rows, v_at] = dv.astype(BF16)
-            total = total + mm_t(dq_ref[g, rows, :], w_ref[g])
-        in_ref[rows, :] = total.astype(BF16)
+        backward_sequence(
+            s, lambda v, at: store_by_owner(dattn_t_ref, v, at, n),
+            d_resid_ref, w_ref, wo_ref, qkv_ref, p_ref, in_ref, dq_ref,
+        )
+        send_input(s).start()
+
+        for t in range(2):
+
+            @pl.when(s == min(t, seqs - 1))
+            def _():
+                after_core(t)
 
     for g in range(groups):
-        bg_ref[g] = jnp.sum(dq_ref[g].astype(F32), 0, keepdims=True)
-
-        @pl.loop(0, model // block)
-        def _(b):
-            rows = pl.ds(pl.multiple_of(b * block, block), block)
-            gq_ref[g, rows, :] = mm(x_t_ref[rows, :], dq_ref[g]).astype(BF16)
-            go_ref[g, rows, :] = mm(dattn_t_ref[rows, :], ctx_ref[g]).astype(BF16)
-
-
-def call(kernel, outs, scratch, flops, *args):
+        column = jnp.sum(dq_ref[g].astype(F32), 0, keepdims=True)
+        tiny[g] = jnp.zeros_like(tiny[g])
+        tiny[g, 0:1, :width] = column[:, :width]
+        tiny[g, 0:1, width:] = column[:, 2 * width :]
+        tiny[g, 1:2, :] = ubg_ref[g, :, :model]
+        tiny[g, 2:3, :] = ubg_ref[g, :, model:]
+
+        weight_products(g, x_t_ref, dattn_t_ref, dq_ref, ctx_ref, ga_ref)
+
+    tiny[2] = small_ref[...]
+
+    tiny_core = remote(tiny, tiny_1, send.at[3, 1], recv.at[3, 1], to_core)
+    tiny_line = remote(tiny_1, tiny_2, send.at[3, 2], recv.at[3, 2], to_line)
+    tiny_over = remote(tiny_2.at[1:3], tiny_x, send.at[4, 0], recv.at[4, 0], to_x)
+
+    def tiny_rest(k):
+        return remote(tiny_x, tiny_z.at[k - 1], send_z.at[3, k - 1], recv_z.at[3, k - 1], to_rest(k))
+
+    by_core(2).start()
+    tiny_core.start()
+    after_line(0)
+    after_core(2)
+    tiny_core.wait_recv()
+    tiny_1[...] += tiny[...]
+    tiny_line.start()
+    after_line(1)
+    after_x(0)
+    tiny_line.wait_recv()
+    tiny_2[...] += tiny_1[...]
+    tiny_over.start()
+    after_x(1)
+    after_rest(0, rd_ref)
+    tiny_over.wait_recv()
+    tiny_x[0] += tiny_2[0]
+    tiny_x[1] += tiny_2[2]
+    for k in range(1, depth):
+        tiny_rest(k).start()
+    after_line(2)
+    after_rest(1, ru_ref)
+    after_x(2)
+    total = tiny_x[...]
+    for k in range(1, depth):
+        tiny_rest(k).wait_recv()
+        total = total + tiny_z[k - 1]
+    sums_ref[...] = total
+    after_rest(2, ra_ref)
+    for s in range(seqs):
+        send_input(s).wait_recv()
+        send_input(s).wait_send()
+    send_output().wait()
+    for t in range(3):
+        by_core(t).wait_send()
+        by_line(t).wait_send()
+        by_x(t).wait_send()
+        for k in range(1, depth):
+            by_rest(t, k).wait_send()
+    tiny_core.wait_send()
+    tiny_line.wait_send()
+    tiny_over.wait_send()
+    for k in range(1, depth):
+        tiny_rest(k).wait_send()
+
+
+def call(kernel, outs, scratch, flops, *args, far=(), far_out=(), collective=None):
     shapes = [jax.ShapeDtypeStruct(s, d) for s, d in outs]
     moved = sum(a.size * a.dtype.itemsize for a in args) + sum(s.size * s.dtype.itemsize for s in shapes)
     vmem = pl.BlockSpec(memory_space=pltpu.VMEM)
     return pl.pallas_call(
         kernel,
         out_shape=shapes,
-        in_specs=[vmem] * len(args),
-        out_specs=[vmem] * len(shapes),
-        scratch_shapes=[pltpu.VMEM(s, d) for s, d in scratch],
-        compiler_params=pltpu.CompilerParams(vmem_limit_bytes=VMEM_LIMIT),
+        in_specs=[pl.BlockSpec(memory_space=pl.ANY) if i in far else vmem for i in range(len(args))],
+        out_specs=[pl.BlockSpec(memory_space=pl.ANY) if i in far_out else vmem for i in range(len(shapes))],
+        scratch_shapes=[pltpu.VMEM(*s) if isinstance(s, tuple) else s for s in scratch],
+        compiler_params=pltpu.CompilerParams(
+            vmem_limit_bytes=VMEM_LIMIT, collective_id=collective, has_side_effects=collective is not None
+        ),
         cost_estimate=pl.CostEstimate(flops=flops, bytes_accessed=moved, transcendentals=0),
     )(*args)
 
@@ -323,9 +536,8 @@
         v = v.reshape(rows, 2, part, model)
         return jnp.where(from_high[:, :, None], v[:, 1], v[:, 0]).reshape(mine, model)
 
-    def give(own):
-        own = own.reshape(rows, part, model)
-        other = swap(own)
+    def give(own, other):
+        own, other = own.reshape(rows, part, model), other.reshape(rows, part, model)
         low = jnp.where(from_high[:, :, None], other, own)
         high = jnp.where(from_high[:, :, None], own, other)
         return jnp.stack([low, high], 1).reshape(tokens, model)
@@ -359,8 +571,9 @@
         x, w_qkv, b_qkv, w_out, seg[:, :, None], seg[:, None, :],
         out_bias.astype(F32)[None], vectors[0:1], vectors[1:2],
     )
+    remote = (model // n) % 16 == 0 and n % 4 == 0 and n > 4 and hidden == 2 * model and 4 * width == hidden
     output, g_down, g_up, d_resid, small, up_bias_grad = call(
-        feed_forward,
+        functools.partial(feed_forward, n if remote else 0),
         [
             ((mine, model), BF16),
             ((2, model, hidden), BF16),
@@ -380,27 +593,50 @@
         2 * mine * model * 2 * hidden * 6,
         low, xhat, rstd, w_up, b_up, w_down, vectors, cot,
     )
-    layer_output = give(output)
-    down_weight_grad = reduce_to_owner(g_down, n).T
-    up_weight_grad = reduce_to_owner(g_up, n)
-    grad_in, g_qkv, g_out, bias_grad = call(
-        attention_backward,
-        [
-            ((mine, model), BF16),
-            ((2, model, 3 * width), BF16),
-            ((2, model, width), BF16),
-            ((2, 1, 3 * width), F32),
-        ],
-        [((2, mine, 3 * width), BF16), ((model, mine), BF16), ((model, mine), BF16)],
-        2 * mine * model * 16 * width,
-        x, d_resid, w_qkv, w_out, qkv, probs, ctx,
-    )
-    input_grad = give(grad_in)
-    g_attn = reduce_to_owner(jnp.concatenate([g_qkv, g_out], -1), n)
-    sums = jnp.concatenate([bias_grad[:, 0, :width], bias_grad[:, 0, 2 * width :], up_bias_grad[:, 0]], -1)
-    sums = jnp.where(x_index == 0, sums, sums[::-1])
-    sums, small = lax.psum((sums, small), ("dp", "mp"))
-    sums = lax.dynamic_index_in_dim(sums, x_index, 0, keepdims=False)
+    scratch = [((2, mine, 3 * width), BF16), ((model, mine), BF16), ((model, mine), BF16)]
+    flops = 2 * mine * model * 16 * width
+    if remote:
+        depth = n // 4
+        dma = pltpu.SemaphoreType.DMA
+        grad_in, grad_in_peer, output_peer, g_down, g_up, g_attn, sums = call(
+            functools.partial(attention_backward, n),
+            [((mine, model), BF16)] * 3 + [((model // n, hidden), F32)] * 3 + [((2, 8, model), F32)],
+            scratch + [
+                ((2, model, hidden), BF16),
+                ((2, 2, model // 2, hidden), BF16),
+                ((3, 2, model // 2, hidden), BF16),
+                ((3, 2, model // 4, hidden), BF16),
+                ((3, model // 4, hidden), BF16),
+                ((3, depth - 1, model // n, hidden), BF16),
+                ((3, 8, model), F32),
+                ((3, 8, model), F32),
+                ((3, 8, model), F32),
+                ((2, 8, model), F32),
+                ((depth - 1, 2, 8, model), F32),
+                dma((5, 3)), dma((5, 3)), dma((4, depth - 1)), dma((4, depth - 1)), dma((rows,)), dma((rows,)), dma((2,)),
+            ],
+            flops,
+            x, d_resid, w_qkv, w_out, qkv, probs, ctx, small, up_bias_grad, g_down, g_up, output,
+            far=(9, 10, 11), far_out=(1, 2), collective=0,
+        )
+        sums, small = sums[0, :3].reshape(-1), sums[1]
+    else:
+        output_peer = swap(output)
+        grad_in, g_attn, bias_grad = call(
+            attention_backward_plain,
+            [((mine, model), BF16), ((2, model, 4 * width), BF16), ((2, 1, 3 * width), F32)],
+            scratch, flops, x, d_resid, w_qkv, w_out, qkv, probs, ctx,
+        )
+        grad_in_peer = swap(grad_in)
+        g_down, g_up, g_attn = (reduce_to_owner(v, n) for v in (g_down, g_up, g_attn))
+        sums = jnp.concatenate([bias_grad[:, 0, :width], bias_grad[:, 0, 2 * width :], up_bias_grad[:, 0]], -1)
+        sums = jnp.where(x_index == 0, sums, sums[::-1])
+        sums, small = lax.psum((sums, small), ("dp", "mp"))
+        sums = lax.dynamic_index_in_dim(sums, x_index, 0, keepdims=False)
+    layer_output = give(output, output_peer)
+    input_grad = give(grad_in, grad_in_peer)
+    down_weight_grad = g_down.T
+    up_weight_grad = g_up
     return (
         layer_output,
         input_grad,

time: 432 us -> 313 us (0.72)
  Pallas kernels: 96 us -> 192 us
  waiting for transfers between devices: 139 us -> 56.7 us
  blocking collectives: 78 us -> 0 us
  starting transfers between devices: 28.9 us -> 6.77 us
  other arithmetic: 40.2 us -> 23.2 us
  local copies, waits for them, and re-layouts: 43 us -> 31.6 us
    pallas_call x3, Pallas kernels: 96 us -> 192 us  [call(): pl.pallas_call(kernel, out_shape=shapes, in_specs=[pl.BlockSpec(memory_sp...]
    ppermute x19 -> x4, waiting for transfers between devices: 92.8 us -> 0.01 us  [shift_dp(): return lax.ppermute(v, 'dp', [(d, target(d)) for d in range(n)])]
    psum x1 -> x0, blocking collectives: 78 us -> none  [per_device(): sums, small = lax.psum((sums, small), ('dp', 'mp'))]
    ppermute x19 -> x4, starting transfers between devices: 16.7 us -> 0.65 us  [shift_dp(): return lax.ppermute(v, 'dp', [(d, target(d)) for d in range(n)])]
    ppermute x10 -> x5, waiting for transfers between devices: 46.4 us -> 56.7 us  [swap(): return lax.ppermute(v, 'mp', [(0, 1), (1, 0)])]
    squeeze x12 -> x0, local copies, waits for them, and re-layouts: 8.91 us -> none  [the longest x9 8.88 us: pick(): return lax.dynamic_index_in_dim(parts, at, 2, keepdims=False)]
    convert_element_type x9 -> x0, other arithmetic: 8.89 us -> none  [reduce_to_owner(): left = total.astype(BF16)]
    ppermute x10 -> x5, starting transfers between devices: 12.2 us -> 6.12 us  [swap(): return lax.ppermute(v, 'mp', [(0, 1), (1, 0)])]
  transfers between devices with their start and end apart: 29 -> 9, of which waited for: 9 -> 1; matrix products, arithmetic and copies ran while one was open for 15% -> 9% of each run, Pallas kernels for 11% -> 6%
where the time goes in v2:
time: 313 us; the launch traced here: 312 us
  Pallas kernels  192 us (61%)
  waiting for transfers between devices  56.7 us (18%)
  local copies, waits for them, and re-layouts  31.6 us (10%)
  other arithmetic  23.2 us (7%)
  starting transfers between devices  6.77 us (2%)
    pallas_call x3, Pallas kernels, call(): pl.pallas_call(kernel, out_shape=shapes, in_specs=[pl.BlockSpec(memory_sp...  192 us
    ppermute x5, waiting for transfers between devices, swap(): return lax.ppermute(v, 'mp', [(0, 1), (1, 0)])  56.7 us
    another operation x8, other arithmetic, with_peer(): return jnp.stack([own, peer])  8.97 us
    unnamed x50, local copies, waits for them, and re-layouts  7.52 us
  transfers between devices with their start and end apart: 9, of which 1 were waited for; matrix products, arithmetic and copies ran while one was open for 9% of the time, Pallas kernels for 6%

profile of v2, /device:TPU:0, one launch (start us, length us, event | category | flops | bytes accessed | tf_op | source)
XLA Modules:
  0.0 311.7 jit_solution(9426637756472880516)
XLA Ops:
  0.7 1.6 dynamic-update-slice
  2.3 1.4 dynamic-update-slice.1
  3.7 1.4 dynamic-update-slice.2
  5.2 3.0 collective-permute-start.2
  8.1 1.7 constant_dynamic-slice_fusion.2
  9.8 2.4 constant_dynamic-slice_fusion.1
  12.2 2.0 collective-permute-start.5
  14.2 1.1 constant_dynamic-slice_fusion
  16.0 0.5 copy-done.7
  16.6 1.0 constant_dynamic-slice_fusion.3
  17.6 1.1 collective-permute-start
  19.7 0.6 fusion.4
  20.2 2.6 fusion.1
  23.0 2.2 bitcast_select_fusion
  25.2 0.6 slice_select_fusion
  25.9 0.7 stack.76
  26.6 1.3 convert_element_type.19.vec_ref
  27.9 1.3 reshape.220.bo_ref
  29.2 0.6 broadcast_in_dim.59.seg_r_ref
  29.7 0.9 copy.51.seg_c_ref
  30.7 0.7 stack.77
  31.5 56.7 %collective-permute-done = bf16[384,1152]{1,0:T(8,128)(2,1)} collective-permute-done((bf16[384,1152]{1,0:T(8,128)(2,1)}, bf16[384,1152]{1,0:T(8,128)(2,1)}, u32[]{:S(2)}, u32[]{:S(2)}) %collective-permute-start) | collective-permute-done | bytes 884768 | tf_op jit(solution)/shard_map/ppermute | solution.py:472
  88.1 0.6 pad_maximum_fusion.7.b_ref
  88.7 0.6 fusion.ub_ref
  89.4 1.0 broadcast_select_fusion.11
  90.5 1.1 pad_maximum_fusion.5.wo_ref
  91.6 0.5 collective-permute-start.6
  92.2 1.3 broadcast_select_fusion.9
  93.7 2.2 pad_maximum_fusion.2.w_ref
  95.9 19.9 %shard_map.305 = (bf16[2,768,1152]{2,1,0:T(8,128)(2,1)}, bf16[3,12,256,256]{3,2,1,0:T(8,128)(2,1)}, bf16[2,768,384]{2,1,0:T(8,128)(2,1)}, f32[768,768]{1,0:T(8,1...) custom-call(bf16[768,768]{1,0:T(8,128)(2,1)} %get-tuple-element.92.x_ref, ...), custom_call_target="tpu_custom_call" | custom-call | flops 3623878656 | bytes 18902016 | tf_op jit(solution)/shard_map/pallas_call | solution.py:450
  115.8 1.4 broadcast_select_fusion.3
  117.4 1.8 broadcast_select_fusion.1
  119.4 1.5 copy-done.1
  120.9 2.6 pad_maximum_fusion.1.down_ref
  123.5 2.5 pad_maximum_fusion.up_ref
  126.0 47.0 %shard_map.306 = (bf16[768,768]{1,0:T(8,128)(2,1)}, bf16[2,768,1536]{2,1,0:T(8,128)(2,1)}, bf16[2,768,1536]{2,1,0:T(8,128)(2,1)}, f32[768,768]{1,0:T(8,128)}, f32[8,768]{1,0:T(8,128)}, /*index=5*/f32[2,1,1536]{2,1,0:T(1,128)}) custom-call(bf16[768,768]{1,0:T(8,128)(2,1)} %get-tuple-element.36.low_ref, f32[768,768]{1,0:T(8,128)} %get-tuple-element.37.xhat_ref, ...), custom_call_target="tpu_custom_call" | custom-call | flops 21743271936 | bytes 27199488 | tf_op jit(solution)/shard_map/pallas_call | solution.py:450
  173.0 125.5 %shard_map.307 = (bf16[768,768]{1,0:T(8,128)(2,1)}, bf16[768,768]{1,0:T(8,128)(2,1)}, bf16[768,768]{1,0:T(8,128)(2,1)}, f32[48,1536]{1,0:T(8,128)}, f32[48,1536]...) custom-call(bf16[768,768]{1,0:T(8,128)(2,1)} %get-tuple-element.92.x_ref, ...), custom_call_target="tpu_custom_call" | custom-call | flops 7247757312 | bytes 32821248 | tf_op jit(solution)/shard_map/pallas_call | solution.py:450
  298.6 1.3 slice.119
  299.9 0.7 slice.110
  300.7 1.7 slice_reduce_fusion
  302.4 2.4 broadcast_select_fusion.5
  305.0 1.6 copy.55
  306.6 0.6 slice.120
  307.2 0.6 fusion.3
  307.8 0.7 slice_bitcast_fusion
  308.8 1.6 copy.54
  310.3 0.7 copy.67
  311.0 0.7 copy.68
  (85 shorter events, 2.9 us)
Async XLA Ops:
  0.7 13.6 %copy-start = (bf16[1536,768]{1,0:T(8,128)(2,1)S(1)}, bf16[1536,768]{1,0:T(8,128)(2,1)}, u32[]{:S(2)}) copy-start(bf16[1536,768]{1,0:T(8,128)(2,1)} %param.31) | copy-start | bytes 7077892
  5.2 25.5 %collective-permute-start.2 = (bf16[2304]{0:T(1024)(128)(2,1)}, bf16[2304]{0:T(1024)(128)(2,1)}, u32[]{:S(2)}, u32[]{:S(2)}) collective-permute-start(bf16[2304]{0:T(1024)(128)(2,1)} %dynamic-update-slice.2), channel_id=1, source_target_pairs={{0,1},{1,0},{2,3},{3,2},{4,5},{5,4},{6,7},{7,6},{8,9},{9,8},{10,11... | collective-permute-start | bytes 13832 | tf_op jit(solution)/shard_map/ppermute | solution.py:472
  9.8 21.6 %collective-permute-start.3 = (bf16[192,768]{1,0:T(8,128)(2,1)}, bf16[192,768]{1,0:T(8,128)(2,1)}, u32[]{:S(2)}, u32[]{:S(2)}) collective-permute-start(bf16[192,768]{1,0:T(8,128)(2,1)} %constant_dynamic-slice_fusion.2), channel_id=1, source_target_pairs={{0,1},{1,0},{2,3},{3,2},{4,5},{5,4},{6,7},{7,6},{8,9},{9,8},{10,11... | collective-permute-start | bytes 884744 | tf_op jit(solution)/shard_map/ppermute | solution.py:472
  12.2 79.4 %collective-permute-start.5 = (bf16[384,1536]{1,0:T(8,128)(2,1)}, bf16[384,1536]{1,0:T(8,128)(2,1)S(1)}, u32[]{:S(2)}, u32[]{:S(2)}) collective-permute-start(bf16[384,1536]{1,0:T(8,128)(2,1)} %constant_dynamic-slice_fusion.1), channel_id=1, source_target_pairs={{0,1},{1,0},{2,3},{3,2},{4,5},{5,4},{6,7},{7,6},{8,9},{9,8},{10,11... | collective-permute-start | bytes 3538952 | tf_op jit(solution)/shard_map/ppermute | solution.py:472
  14.2 1.3 copy-start.5
  14.2 1.7 copy-start.6
  15.3 1.1 copy-start.7
  15.3 76.8 %collective-permute-start.7 = (bf16[768,768]{1,0:T(8,128)(2,1)}, bf16[768,768]{1,0:T(8,128)(2,1)}, u32[]{:S(2)}, u32[]{:S(2)}) collective-permute-start(bf16[768,768]{1,0:T(8,128)(2,1)} %constant_dynamic-slice_fusion), channel_id=1, source_target_pairs={{0,1},{1,0},{2,3},{3,2},{4,5},{5,4},{6,7},{7,6},{8,9},{9,8},{10,11... | collective-permute-start | bytes 3538952 | tf_op jit(solution)/shard_map/ppermute | solution.py:472
  16.5 2.3 copy-start.13
  16.5 2.6 copy-start.17
  16.5 2.6 copy-start.18
  16.6 2.5 copy-start.19
  16.6 2.5 copy-start.20
  16.6 2.5 copy-start.21
  17.6 70.5 %collective-permute-start = (bf16[384,1152]{1,0:T(8,128)(2,1)}, bf16[384,1152]{1,0:T(8,128)(2,1)}, u32[]{:S(2)}, u32[]{:S(2)}) collective-permute-start(bf16[384,1152]{1,0:T(8,128)(2,1)} %constant_dynamic-slice_fusion.3), channel_id=1, source_target_pairs={{0,1},{1,0},{2,3},{3,2},{4,5},{5,4},{6,7},{7,6},{8,9},{9,8},{10,11... | collective-permute-start | bytes 2654216 | tf_op jit(solution)/shard_map/ppermute | solution.py:472
  19.0 0.5 copy-start.14
  19.6 3.3 %copy-start.11 = (bf16[5,768]{1,0:T(8,128)(2,1)}, bf16[5,768]{1,0:T(8,128)(2,1)S(1)}, u32[]{:S(2)}) copy-start(bf16[5,768]{1,0:T(8,128)(2,1)S(1)} %stack.87) | copy-start | bytes 23044
  23.0 2.2 copy-start.15
  25.2 65.2 %copy-start.4 = (bf16[384,768]{1,0:T(8,128)(2,1)S(1)}, bf16[384,768]{1,0:T(8,128)(2,1)}, u32[]{:S(2)}) copy-start(bf16[384,768]{1,0:T(8,128)(2,1)} %param.25) | copy-start | bytes 1769476
  31.4 58.0 %collective-permute-start.4 = (bf16[192,768]{1,0:T(8,128)(2,1)}, bf16[192,768]{1,0:T(8,128)(2,1)S(1)}, u32[]{:S(2)}, u32[]{:S(2)}) collective-permute-start(bf16[192,768]{1,0:T(8,128)(2,1)} %collective-permute-done.3), channel_id=1, source_target_pairs={{0,2},{2,0},{4,6},{6,4},{8,10},{10,8},{12,14},{14,12},{16,18},{18,... | collective-permute-start | bytes 884744 | tf_op jit(solution)/shard_map/ppermute | solution.py:480
  88.1 4.1 %collective-permute-start.1 = (bf16[384,1152]{1,0:T(8,128)(2,1)}, bf16[384,1152]{1,0:T(8,128)(2,1)S(1)}, u32[]{:S(2)}, u32[]{:S(2)}) collective-permute-start(bf16[384,1152]{1,0:T(8,128)(2,1)} %collective-permute-done), channel_id=1, source_target_pairs={{0,2},{2,0},{4,6},{6,4},{8,10},{10,8},{12,14},{14,12},{16,18},{18,... | collective-permute-start | bytes 2654216 | tf_op jit(solution)/shard_map/ppermute | solution.py:480
  91.6 24.2 %collective-permute-start.6 = (bf16[384,1536]{1,0:T(8,128)(2,1)S(1)}, bf16[384,1536]{1,0:T(8,128)(2,1)}, u32[]{:S(2)}, u32[]{:S(2)}) collective-permute-start(bf16[384,1536]{1,0:T(8,128)(2,1)S(1)} %collective-permute-done.5), channel_id=1, source_target_pairs={{0,2},{2,0},{4,6},{6,4},{8,10},{10,8},{12,14},{14,12},{16,18},{18,... | collective-permute-start | bytes 3538952 | tf_op jit(solution)/shard_map/ppermute | solution.py:480
  92.1 25.3 %collective-permute-start.8 = (bf16[768,768]{1,0:T(8,128)(2,1)}, bf16[768,768]{1,0:T(8,128)(2,1)}, u32[]{:S(2)}, u32[]{:S(2)}) collective-permute-start(bf16[768,768]{1,0:T(8,128)(2,1)} %collective-permute-done.7), channel_id=1, source_target_pairs={{0,2},{2,0},{4,6},{6,4},{8,10},{10,8},{12,14},{14,12},{16,18},{18,... | collective-permute-start | bytes 3538952 | tf_op jit(solution)/shard_map/ppermute | solution.py:480
  119.2 1.7 copy-start.1
  120.9 2.6 copy-start.2
  173.0 129.4 %copy-start.3 = (bf16[768,768]{1,0:T(8,128)(2,1)S(1)}, bf16[768,768]{1,0:T(8,128)(2,1)}, u32[]{:S(2)}) copy-start(bf16[768,768]{1,0:T(8,128)(2,1)} %get-tuple-element.47.own_ref) | copy-start | bytes 3538948
  173.0 129.4 %copy-start.16 = (pred[3,256]{1,0:T(4,128)(4,1)S(1)}, pred[3,256]{1,0:T(4,128)(4,1)}, u32[]{:S(2)}) copy-start(pred[3,256]{1,0:T(4,128)(4,1)} %get-tuple-element.62) | copy-start | bytes 2308
  305.0 1.6 copy-start.12
  305.0 2.8 copy-start.10
  308.7 1.6 copy-start.9
  308.7 2.3 copy-start.8

commit v3 on v2

--- a/solution.py
+++ b/solution.py
@@ -14,7 +14,7 @@
 F32 = jnp.float32
 BF16 = jnp.bfloat16
 CHUNK = 512
-VMEM_LIMIT = 60 * 1024 * 1024
+VMEM_LIMIT = 67043328
 MESH = pl.DeviceIdType.MESH
 
 
@@ -110,7 +110,7 @@
 
 
 def feed_forward(
-    n, low_ref, xhat_ref, rstd_ref, up_ref, ub_ref, down_ref, vec_ref, cot_ref,
+    low_ref, xhat_ref, rstd_ref, up_ref, ub_ref, down_ref, vec_ref, cot_ref,
     out_ref, gd_ref, gu_ref, d_resid_ref, small_ref, ubg_ref,
     act_ref, slope_ref, acc_ref, dffn_ref, dffn_t_ref, low_t_ref,
 ):
@@ -119,13 +119,7 @@
     step = min(CHUNK, hidden)
     per = hidden // step
     block = 256
-    def put(dst, v):
-        if n:
-            store_by_owner(dst, v, slice(None), n)
-        else:
-            dst[...] = v
-
-    put(low_t_ref, low_ref[...].T)
+    low_t_ref[...] = low_ref[...].T
     acc_ref[...] = jnp.zeros_like(acc_ref)
 
     @pl.loop(0, groups * per)
@@ -167,7 +161,7 @@
         small_ref[4:5, :] += jnp.sum(cot * xhat, 0, keepdims=True)
         small_ref[5:6, :] += jnp.sum(cot, 0, keepdims=True)
 
-    put(dffn_t_ref, dffn_ref[...].T)
+    dffn_t_ref[...] = dffn_ref[...].T
 
     @pl.loop(0, groups * per)
     def _(i):
@@ -266,15 +260,23 @@
         weight_products(g, x_t_ref, dattn_t_ref, dq_ref, ctx_ref, ga_ref)
 
 
-def attention_backward(
-    n, x_ref, d_resid_ref, w_ref, wo_ref, qkv_ref, p_ref, ctx_ref, small_ref, ubg_ref, gd_ref, gu_ref, own_ref,
-    in_ref, in_peer_ref, out_peer_ref, rd_ref, ru_ref, ra_ref, sums_ref,
-    dq_ref, dattn_t_ref, x_t_ref, ga_ref, kept, half, quarter, owned, shard, tiny, tiny_1, tiny_2, tiny_x, tiny_z,
-    send, recv, send_z, recv_z, send_in, recv_in, local,
+def whole_layer(
+    n, x_ref, cot_ref, seg_c_ref, seg_r_ref, bias_ref, vec_ref, wq_hbm, wk_hbm, wv_hbm, wo_hbm, up_hbm, down_hbm,
+    out_ref, out_peer_ref, in_ref, in_peer_ref, rd_ref, ru_ref, ra_ref, rb_ref, sums_ref,
+    w_ref, wo_ref, up_ref, down_ref, bias_2, qkv_ref, p_ref, ctx_ref, xhat_ref, rstd_ref, low_ref, act_ref, slope_ref,
+    acc_ref, dffn_ref, t_low_ref, t_grad_ref, small_ref, *rest_refs,
 ):
-    seqs, length = p_ref.shape[0], p_ref.shape[2]
-    groups, width = wo_ref.shape[0], wo_ref.shape[1]
-    model = x_ref.shape[1]
+    ways = ("line", "x", "line", "x")
+    half, mid, owned, shard = rest_refs[0:4], rest_refs[4:8], rest_refs[8:12], rest_refs[12:16]
+    tiny, tiny_1, tiny_2, tiny_x, tiny_z = rest_refs[16:21]
+    send, recv, send_z, recv_z, send_in, recv_in, g_send, g_recv, g_local = rest_refs[21:]
+    seqs, length = seg_c_ref.shape[0], seg_c_ref.shape[1]
+    groups, width, model = wo_ref.shape
+    hidden = up_ref.shape[2]
+    pairs = width // PAIR
+    tokens = seqs * length
+    step = hidden // 3
+    block = 256
     rows_own = model // n
     depth = n // 4
     index = lax.axis_index("dp")
@@ -298,142 +300,410 @@
             src_ref=src, dst_ref=dst, send_sem=s, recv_sem=r, device_id=device, device_id_type=MESH
         )
 
+    def columns(c):
+        return pl.ds(pl.multiple_of(c * step, step), step)
+
+    def ends_of(kind, c, piece):
+        if kind < 3:
+            size = model // 4
+            rows = pl.ds(pl.multiple_of(piece * size, size), size)
+            return (wq_hbm, wk_hbm, wv_hbm)[kind].at[rows, :], w_ref.at[1, rows, kind * width : (kind + 1) * width]
+        if kind == 3:
+            size = width // 4
+            rows = pl.ds(pl.multiple_of(piece * size, size), size)
+            return wo_hbm.at[rows, :], wo_ref.at[1, rows, :]
+        if kind == 4:
+            size = model // 4
+            rows = pl.ds(pl.multiple_of(piece * size, size), size)
+            return up_hbm.at[rows, columns(c)], up_ref.at[1, rows, columns(c)]
+        size = step // 4
+        rows = pl.ds(pl.multiple_of(c * step + piece * size, size), size)
+        return down_hbm.at[rows, :], down_ref.at[1, rows, :]
+
+    def slot(kind, c):
+        return kind if kind < 4 else (4 + c if kind == 4 else 7 + c)
+
+    def over_x(kind, c=0):
+        src, dst = ends_of(kind, c, 2 * line + core)
+        i = slot(kind, c)
+        return remote(src, dst, g_send.at[0, i], g_recv.at[0, i], to_x)
+
+    def pass_on(kind, c, hop):
+        at = ends_of(kind, c, 2 * (1 - line) + core if hop == 3 else 2 * line + core)[1]
+        i = slot(kind, c)
+        return remote(at, at, g_send.at[hop, i], g_recv.at[hop, i], to_line if hop == 2 else to_core)
+
+    def first_hop(kind, c=0):
+        over_x(kind, c).wait_recv()
+        pass_on(kind, c, 2).start()
+        pass_on(kind, c, 1).start()
+
+    def second_hop(kind, c=0):
+        pass_on(kind, c, 2).wait_recv()
+        pass_on(kind, c, 3).start()
+
+    def complete(kind, c=0):
+        pass_on(kind, c, 1).wait_recv()
+        pass_on(kind, c, 3).wait_recv()
+
+    def sent(kind, c=0):
+        over_x(kind, c).wait_send()
+        for hop in (1, 2, 3):
+            pass_on(kind, c, hop).wait_send()
+
+    bias_over = remote(bias_ref, bias_2, send.at[4, 0], recv.at[4, 0], to_x)
+    bias_over.start()
+    for kind in range(4):
+        over_x(kind).start()
+    for c in range(3):
+        over_x(4, c).start()
+        over_x(5, c).start()
+    own_copies = [
+        pltpu.make_async_copy(src, dst, g_local.at[i])
+        for i, (src, dst) in enumerate(
+            [(w, w_ref.at[0, :, o * width : (o + 1) * width]) for o, w in enumerate((wq_hbm, wk_hbm, wv_hbm))]
+            + [(wo_hbm, wo_ref.at[0]), (up_hbm, up_ref.at[0]), (down_hbm, down_ref.at[0])]
+        )
+    ]
+    for copy in own_copies:
+        copy.start()
+
     n_half, n_quarter = model // 2, model // 4
-    sources = (gd_ref, gu_ref, ga_ref)
+    cut = hidden // 2
+    sources = (act_ref, slope_ref, up_ref.at[:, :, :cut], up_ref.at[:, :, cut:])
 
     def by_core(t):
         there = pl.ds(pl.multiple_of((1 - core) * n_half, n_half), n_half)
-        return remote(sources[t].at[:, there, :], half.at[t], send.at[0, t], recv.at[0, t], to_core)
-
-    def by_line(t):
+        return remote(sources[t].at[:, there, :], half[t], send.at[0, t], recv.at[0, t], to_core)
+
+    def by_first(t):
+        if ways[t] == "line":
+            there = pl.ds(pl.multiple_of((1 - line) * n_quarter, n_quarter), n_quarter)
+            return remote(half[t].at[:, there, :], mid[t], send.at[1, t], recv.at[1, t], to_line)
+        return remote(half[t].at[1], mid[t], send.at[1, t], recv.at[1, t], to_x)
+
+    def by_second(t):
+        if ways[t] == "line":
+            return remote(mid[t].at[1], owned[t], send.at[2, t], recv.at[2, t], to_x)
         there = pl.ds(pl.multiple_of((1 - line) * n_quarter, n_quarter), n_quarter)
-        return remote(half.at[t, :, there, :], quarter.at[t], send.at[1, t], recv.at[1, t], to_line)
-
-    def by_x(t):
-        return remote(quarter.at[t, 1], owned.at[t], send.at[2, t], recv.at[2, t], to_x)
+        return remote(mid[t].at[there, :], owned[t], send.at[2, t], recv.at[2, t], to_line)
 
     def by_rest(t, k):
         there = pl.ds(pl.multiple_of((rest + k) % depth * rows_own, rows_own), rows_own)
-        return remote(
-            owned.at[t, there, :], shard.at[t, k - 1], send_z.at[t, k - 1], recv_z.at[t, k - 1], to_rest(k)
-        )
-
-    def keep(t):
-        here = pl.ds(pl.multiple_of(core * n_half, n_half), n_half)
-        return pltpu.make_async_copy(sources[t].at[:, here, :], kept.at[t], local.at[t])
+        return remote(owned[t].at[there, :], shard[t].at[k - 1], send_z.at[t, k - 1], recv_z.at[t, k - 1], to_rest(k))
 
     def after_core(t):
         by_core(t).wait_recv()
-        if t < 2:
-            keep(t).wait()
         for g in range(groups):
-            if t < 2:
-                add_rows(half.at[t, g], kept.at[t, g], 0, 96)
-            else:
-                add_rows(half.at[t, g], ga_ref.at[g], core * n_half, 96)
-        by_line(t).start()
-
-    def after_line(t):
-        by_line(t).wait_recv()
-        for g in range(groups):
-            add_rows(quarter.at[t, g], half.at[t, g], line * n_quarter, 96)
-        by_x(t).start()
-
-    def after_x(t):
-        by_x(t).wait_recv()
-        add_rows(owned.at[t], quarter.at[t, 0], 0, 96)
+            add_rows(half[t].at[g], sources[t].at[g], core * n_half, 96)
+        by_first(t).start()
+
+    def after_first(t):
+        by_first(t).wait_recv()
+        if ways[t] == "line":
+            for g in range(groups):
+                add_rows(mid[t].at[g], half[t].at[g], line * n_quarter, 96)
+        else:
+            add_rows(mid[t], half[t].at[0], 0, 96)
+        by_second(t).start()
+
+    def after_second(t):
+        by_second(t).wait_recv()
+        if ways[t] == "line":
+            add_rows(owned[t], mid[t].at[0], 0, 96)
+        else:
+            add_rows(owned[t], mid[t], line * n_quarter, 96)
         for k in range(1, depth):
             by_rest(t, k).start()
 
     def after_rest(t, out):
-        total = owned[t, pl.ds(pl.multiple_of(rest * rows_own, rows_own), rows_own), :].astype(F32)
+        total = owned[t][pl.ds(pl.multiple_of(rest * rows_own, rows_own), rows_own), :].astype(F32)
         for k in range(1, depth):
             by_rest(t, k).wait_recv()
-            total = total + shard[t, k - 1].astype(F32)
+            total = total + shard[t][k - 1].astype(F32)
         out[...] = total
 
-    def send_output():
-        return remote(own_ref, out_peer_ref, send.at[3, 0], recv.at[3, 0], to_x)
+    def send_output(b):
+        rows = pl.ds(pl.multiple_of(b * length, length), length)
+        return remote(out_ref.at[rows, :], out_peer_ref.at[rows, :], send_in.at[1, b], recv_in.at[1, b], to_x)
 
     def send_input(s):
         rows = pl.ds(pl.multiple_of(s * length, length), length)
-        return remote(in_ref.at[rows, :], in_peer_ref.at[rows, :], send_in.at[s], recv_in.at[s], to_x)
-
-    for t in range(2):
-        by_core(t).start()
-        keep(t).start()
-    send_output().start()
-    store_by_owner(x_t_ref, x_ref[...].T, slice(None), n)
+        return remote(in_ref.at[rows, :], in_peer_ref.at[rows, :], send_in.at[0, s], recv_in.at[0, s], to_x)
+
+    attn_gain, attn_shift, down_bias = vec_ref[0:1, :], vec_ref[1:2, :], vec_ref[2:3, :]
+    ffn_gain, ffn_shift, out_bias = vec_ref[3:4, :], vec_ref[4:5, :], vec_ref[5:6, :]
+
+    def attend(s, g, biases):
+        rows = pl.ds(pl.multiple_of(s * length, length), length)
+        x = x_ref[rows, :]
+        mask = seg_c_ref[s] == seg_r_ref[s]
+        y = mm(x, w_ref[g])
+        query = (0.125 * (y[:, :width] + biases[0:1, :width])).astype(BF16)
+        key = y[:, width : 2 * width].astype(BF16)
+        value = (y[:, 2 * width :] + biases[0:1, width : 2 * width]).astype(BF16)
+        qkv_ref[g, rows, :width] = query
+        qkv_ref[g, rows, width : 2 * width] = key
+        qkv_ref[g, rows, 2 * width :] = value
+        parts = []
+        for p in range(pairs):
+            at = slice(p * PAIR, (p + 1) * PAIR)
+            k = key[:, at]
+            both = None
+            for h, (q, v) in enumerate(zip(halves(query[:, at]), halves(value[:, at]))):
+                scores = jnp.where(mask, mm_t(q, k), -1000000000.0)
+                expo = jnp.exp(scores - jnp.max(scores, -1, keepdims=True))
+                probs = (expo * (1.0 / jnp.sum(expo, -1, keepdims=True))).astype(BF16)
+                p_ref[s, (g * pairs + p) * 2 + h] = probs
+                part = mm(probs, v)
+                both = part if both is None else both + part
+            parts.append(both.astype(BF16))
+        ctx = jnp.concatenate(parts, 1)
+        ctx_ref[g, rows, :] = ctx
+        return mm(ctx, wo_ref[g])
+
+    for copy in own_copies[:4]:
+        copy.wait()
+
+    @pl.loop(0, seqs)
+    def _(s):
+        rows = pl.ds(pl.multiple_of(s * length, length), length)
+        acc_ref[rows, :] = x_ref[rows, :].astype(F32) + out_bias + attend(s, 0, bias_ref)
+        for kind in range(3):
+
+            @pl.when(s == min(kind, seqs - 1))
+            def _():
+                first_hop(kind)
+
+    first_hop(3)
+    for kind in range(4):
+        second_hop(kind)
+    for kind in range(4):
+        complete(kind)
+    bias_over.wait()
+
+    @pl.loop(0, seqs)
+    def _(s):
+        rows = pl.ds(pl.multiple_of(s * length, length), length)
+        attn = acc_ref[rows, :] + attend(s, 1, bias_2)
+        centred = attn - jnp.mean(attn, -1, keepdims=True)
+        rstd = lax.rsqrt(jnp.mean(centred * centred, -1, keepdims=True) + EPS)
+        xhat = centred * rstd
+        xhat_ref[rows, :] = xhat
+        rstd_ref[rows, :] = rstd
+        low_ref[rows, :] = (xhat * attn_gain + attn_shift).astype(BF16)
+
+        @pl.when(s == min(1, seqs - 1))
+        def _():
+            first_hop(4, 0)
+            first_hop(5, 0)
+
+    for copy in own_copies[4:]:
+        copy.wait()
+    store_by_owner(t_low_ref, low_ref[...].T, slice(None), n)
+
+    def expand(c, g, biases):
+        at = columns(c)
+        bias_at = pl.ds(pl.multiple_of(2 * width + c * step, 128), step)
+
+        @pl.loop(0, tokens // block)
+        def _(b):
+            rows = pl.ds(pl.multiple_of(b * block, block), block)
+            u = mm(low_ref[rows, :], up_ref[g, :, at]) + biases[0:1, bias_at]
+            square = u * u
+            t = jnp.tanh(GELU_C * (u + 0.044715 * square * u))
+            gate = 0.5 * (1.0 + t)
+            act = (u * gate).astype(BF16)
+            act_ref[g, rows, at] = act
+            slope = gate + (0.5 * GELU_C) * u * (1.0 - t * t) * (1.0 + 0.134145 * square)
+            slope_ref[g, rows, at] = slope.astype(BF16)
+            acc_ref[rows, :] += mm(act, down_ref[g, at, :])
+
+    acc_ref[...] = jnp.zeros_like(acc_ref)
+
+    @pl.loop(0, 3)
+    def _(c):
+        expand(c, 0, bias_ref)
+
+        @pl.when(c == 0)
+        def _():
+            first_hop(4, 1)
+            first_hop(5, 1)
+
+        @pl.when(c == 1)
+        def _():
+            second_hop(4, 0)
+            second_hop(5, 0)
+
+        @pl.when(c == 2)
+        def _():
+            first_hop(4, 2)
+            first_hop(5, 2)
+            second_hop(4, 1)
+            second_hop(5, 1)
+
+    @pl.loop(0, 3)
+    def _(c):
+        @pl.when(c == 2)
+        def _():
+            second_hop(4, 2)
+            second_hop(5, 2)
+
+        complete(4, c)
+        complete(5, c)
+        expand(c, 1, bias_2)
+
+    small_ref[...] = jnp.zeros_like(small_ref)
+
+    @pl.loop(0, seqs)
+    def _(b):
+        rows = pl.ds(pl.multiple_of(b * length, length), length)
+        resid = xhat_ref[rows, :] * attn_gain + attn_shift + acc_ref[rows, :] + down_bias
+        centred = resid - jnp.mean(resid, -1, keepdims=True)
+        rstd = lax.rsqrt(jnp.mean(centred * centred, -1, keepdims=True) + EPS)
+        xhat = centred * rstd
+        out_ref[rows, :] = (xhat * ffn_gain + ffn_shift).astype(BF16)
+        cot = cot_ref[rows, :].astype(F32)
+        grad = norm_backward(xhat, rstd, ffn_gain, cot)
+        acc_ref[rows, :] = grad
+        dffn_ref[rows, :] = grad.astype(BF16)
+        small_ref[3:4, :] += jnp.sum(grad, 0, keepdims=True)
+        small_ref[4:5, :] += jnp.sum(cot * xhat, 0, keepdims=True)
+        small_ref[5:6, :] += jnp.sum(cot, 0, keepdims=True)
+        send_output(b).start()
+
+    store_by_owner(t_grad_ref, dffn_ref[...].T, slice(None), n)
+
+    def product(left, place, g, at):
+        made = [
+            mm(left[b * block : (b + 1) * block, :], place[g, :, at]).astype(BF16) for b in range(model // block)
+        ]
+        for b, value in enumerate(made):
+            place[g, b * block : (b + 1) * block, at] = value
+
+    tiny[...] = jnp.zeros_like(tiny)
+    for g in range(groups):
+
+        @pl.loop(0, 3)
+        def _(c):
+            product(t_grad_ref, act_ref, g, columns(c))
+
+    by_core(0).start()
+    for g in range(groups):
+
+        @pl.loop(0, 3)
+        def _(c):
+            at = columns(c)
+            total = jnp.zeros((1, step), F32)
+            for b in range(tokens // block):
+                rows = slice(b * block, (b + 1) * block)
+                d_upper = mm_t(dffn_ref[rows, :], down_ref[g, at, :]) * slope_ref[g, rows, at].astype(F32)
+                total = total + jnp.sum(d_upper, 0, keepdims=True)
+                d_low = d_upper.astype(BF16)
+                slope_ref[g, rows, at] = d_low
+                acc_ref[rows, :] += mm_t(d_low, up_ref[g, :, at])
+            tiny[3 + g, 0:1, at] = total
+            product(t_low_ref, slope_ref, g, at)
+            if g == 0:
+
+                @pl.when(c == 1)
+                def _():
+                    after_core(0)
+
+    by_core(1).start()
+
+    @pl.loop(0, seqs)
+    def _(b):
+        rows = pl.ds(pl.multiple_of(b * length, length), length)
+        d_normed = acc_ref[rows, :]
+        xhat = xhat_ref[rows, :]
+        grad = norm_backward(xhat, rstd_ref[rows, :], attn_gain, d_normed)
+        acc_ref[rows, :] = grad
+        small_ref[0:1, :] += jnp.sum(grad, 0, keepdims=True)
+        small_ref[1:2, :] += jnp.sum(d_normed * xhat, 0, keepdims=True)
+        small_ref[2:3, :] += jnp.sum(d_normed, 0, keepdims=True)
+
+    store_by_owner(t_low_ref, x_ref[...].T, slice(None), n)
 
     @pl.loop(0, seqs)
     def _(s):
         backward_sequence(
-            s, lambda v, at: store_by_owner(dattn_t_ref, v, at, n),
-            d_resid_ref, w_ref, wo_ref, qkv_ref, p_ref, in_ref, dq_ref,
+            s, lambda v, at: store_by_owner(t_grad_ref, v, at, n),
+            acc_ref, w_ref, wo_ref, qkv_ref, p_ref, in_ref, qkv_ref,
         )
         send_input(s).start()
 
-        for t in range(2):
-
-            @pl.when(s == min(t, seqs - 1))
-            def _():
-                after_core(t)
-
+        @pl.when(s == 0)
+        def _():
+            after_core(1)
+
+        @pl.when(s == min(1, seqs - 1))
+        def _():
+            after_first(0)
+
+        @pl.when(s == min(2, seqs - 1))
+        def _():
+            after_second(0)
+
+    for kind in range(4):
+        sent(kind)
+    for c in range(3):
+        sent(4, c)
+        sent(5, c)
     for g in range(groups):
-        column = jnp.sum(dq_ref[g].astype(F32), 0, keepdims=True)
-        tiny[g] = jnp.zeros_like(tiny[g])
+        weight_products(g, t_low_ref, t_grad_ref, qkv_ref, ctx_ref, up_ref)
+    by_core(2).start()
+    by_core(3).start()
+    for g in range(groups):
+        column = jnp.sum(qkv_ref[g].astype(F32), 0, keepdims=True)
         tiny[g, 0:1, :width] = column[:, :width]
-        tiny[g, 0:1, width:] = column[:, 2 * width :]
-        tiny[g, 1:2, :] = ubg_ref[g, :, :model]
-        tiny[g, 2:3, :] = ubg_ref[g, :, model:]
-
-        weight_products(g, x_t_ref, dattn_t_ref, dq_ref, ctx_ref, ga_ref)
-
-    tiny[2] = small_ref[...]
-
-    tiny_core = remote(tiny, tiny_1, send.at[3, 1], recv.at[3, 1], to_core)
+        tiny[g, 0:1, width : 2 * width] = column[:, 2 * width :]
+        tiny[g, 1:2, :] = tiny[3 + g, 0:1, :]
+    tiny[2, :, :model] = small_ref[...]
+
+    tiny_core = remote(tiny.at[0:3], tiny_1, send.at[3, 1], recv.at[3, 1], to_core)
     tiny_line = remote(tiny_1, tiny_2, send.at[3, 2], recv.at[3, 2], to_line)
-    tiny_over = remote(tiny_2.at[1:3], tiny_x, send.at[4, 0], recv.at[4, 0], to_x)
+    tiny_over = remote(tiny_2.at[1:3], tiny_x, send.at[3, 3], recv.at[3, 3], to_x)
 
     def tiny_rest(k):
-        return remote(tiny_x, tiny_z.at[k - 1], send_z.at[3, k - 1], recv_z.at[3, k - 1], to_rest(k))
-
-    by_core(2).start()
+        return remote(tiny_x, tiny_z.at[k - 1], send_z.at[4, k - 1], recv_z.at[4, k - 1], to_rest(k))
+
     tiny_core.start()
-    after_line(0)
     after_core(2)
+    after_core(3)
     tiny_core.wait_recv()
-    tiny_1[...] += tiny[...]
+    tiny_1[...] += tiny[0:3]
     tiny_line.start()
-    after_line(1)
-    after_x(0)
+    after_first(1)
+    after_first(2)
     tiny_line.wait_recv()
     tiny_2[...] += tiny_1[...]
     tiny_over.start()
-    after_x(1)
+    after_first(3)
     after_rest(0, rd_ref)
+    after_second(1)
     tiny_over.wait_recv()
     tiny_x[0] += tiny_2[0]
     tiny_x[1] += tiny_2[2]
     for k in range(1, depth):
         tiny_rest(k).start()
-    after_line(2)
+    after_second(2)
+    after_second(3)
     after_rest(1, ru_ref)
-    after_x(2)
     total = tiny_x[...]
     for k in range(1, depth):
         tiny_rest(k).wait_recv()
         total = total + tiny_z[k - 1]
     sums_ref[...] = total
     after_rest(2, ra_ref)
+    after_rest(3, rb_ref)
     for s in range(seqs):
-        send_input(s).wait_recv()
-        send_input(s).wait_send()
-    send_output().wait()
-    for t in range(3):
+        send_output(s).wait()
+        send_input(s).wait()
+    for t in range(4):
         by_core(t).wait_send()
-        by_line(t).wait_send()
-        by_x(t).wait_send()
+        by_first(t).wait_send()
+        by_second(t).wait_send()
         for k in range(1, depth):
             by_rest(t, k).wait_send()
     tiny_core.wait_send()
@@ -544,83 +814,113 @@
 
     seg = jnp.where(from_high, segment[:, part:], segment[:, :part])
 
-    w_qkv = with_peer(jnp.concatenate([q_weight, k_weight, v_weight], 1), n)
-    w_out = with_peer(out_weight, n)
-    w_up = with_peer(up_weight, n)
-    w_down = with_peer(down_weight, n)
-    own_bias = jnp.concatenate([q_bias, v_bias, up_bias])
-    bias = jnp.stack([own_bias, swap(own_bias)]).astype(F32)[:, None, :]
-    b_qkv = jnp.concatenate([bias[..., :width], jnp.zeros_like(bias[..., :width]), bias[..., width : 2 * width]], -1)
-    b_up = bias[..., 2 * width :]
-    vectors = jnp.stack([attn_gain, attn_shift, down_bias, ffn_gain, ffn_shift]).astype(F32)
-
     x = take(layer_input)
     cot = take(cotangent)
-    qkv, probs, ctx, xhat, rstd, low = call(
-        attention_forward,
-        [
-            ((2, mine, 3 * width), BF16),
-            ((rows, 2 * heads, part, part), BF16),
-            ((2, mine, width), BF16),
-            ((mine, model), F32),
-            ((mine, 1), F32),
-            ((mine, model), BF16),
-        ],
-        [],
-        2 * mine * model * 8 * width,
-        x, w_qkv, b_qkv, w_out, seg[:, :, None], seg[:, None, :],
-        out_bias.astype(F32)[None], vectors[0:1], vectors[1:2],
+    own_bias = jnp.concatenate([q_bias, v_bias, up_bias])
+    remote = (
+        (model // n) % 16 == 0 and n % 4 == 0 and n > 4
+        and hidden == 2 * model and 4 * width == hidden and hidden % 384 == 0 and rows >= 3
     )
-    remote = (model // n) % 16 == 0 and n % 4 == 0 and n > 4 and hidden == 2 * model and 4 * width == hidden
-    output, g_down, g_up, d_resid, small, up_bias_grad = call(
-        functools.partial(feed_forward, n if remote else 0),
-        [
-            ((mine, model), BF16),
-            ((2, model, hidden), BF16),
-            ((2, model, hidden), BF16),
-            ((mine, model), F32),
-            ((8, model), F32),
-            ((2, 1, hidden), F32),
-        ],
-        [
-            ((2, mine, hidden), BF16),
-            ((2, mine, hidden), BF16),
-            ((mine, model), F32),
-            ((mine, model), BF16),
-            ((model, mine), BF16),
-            ((model, mine), BF16),
-        ],
-        2 * mine * model * 2 * hidden * 6,
-        low, xhat, rstd, w_up, b_up, w_down, vectors, cot,
-    )
-    scratch = [((2, mine, 3 * width), BF16), ((model, mine), BF16), ((model, mine), BF16)]
-    flops = 2 * mine * model * 16 * width
     if remote:
         depth = n // 4
         dma = pltpu.SemaphoreType.DMA
-        grad_in, grad_in_peer, output_peer, g_down, g_up, g_attn, sums = call(
-            functools.partial(attention_backward, n),
-            [((mine, model), BF16)] * 3 + [((model // n, hidden), F32)] * 3 + [((2, 8, model), F32)],
-            scratch + [
+        wide = (hidden, hidden, model, model)
+        quarter = model // 4
+        vectors = jnp.stack([attn_gain, attn_shift, down_bias, ffn_gain, ffn_shift, out_bias]).astype(F32)
+        output, output_peer, grad_in, grad_in_peer, g_down, g_up, g_first, g_last, sums = call(
+            functools.partial(whole_layer, n),
+            [((mine, model), BF16)] * 4
+            + [((model // n, c), F32) for c in wide]
+            + [((2, 8, hidden), F32)],
+            [
+                ((2, model, 3 * width), BF16),
+                ((2, width, model), BF16),
                 ((2, model, hidden), BF16),
-                ((2, 2, model // 2, hidden), BF16),
-                ((3, 2, model // 2, hidden), BF16),
-                ((3, 2, model // 4, hidden), BF16),
-                ((3, model // 4, hidden), BF16),
-                ((3, depth - 1, model // n, hidden), BF16),
-                ((3, 8, model), F32),
-                ((3, 8, model), F32),
-                ((3, 8, model), F32),
-                ((2, 8, model), F32),
-                ((depth - 1, 2, 8, model), F32),
-                dma((5, 3)), dma((5, 3)), dma((4, depth - 1)), dma((4, depth - 1)), dma((rows,)), dma((rows,)), dma((2,)),
+                ((2, hidden, model), BF16),
+                ((1, 2 * width + hidden), F32),
+                ((2, mine, 3 * width), BF16),
+                ((rows, 2 * heads, part, part), BF16),
+                ((2, mine, width), BF16),
+                ((mine, model), F32),
+                ((mine, 1), F32),
+                ((mine, model), BF16),
+                ((2, model, hidden), BF16),
+                ((2, model, hidden), BF16),
+                ((mine, model), F32),
+                ((mine, model), BF16),
+                ((model, mine), BF16),
+                ((model, mine), BF16),
+                ((8, model), F32),
+            ]
+            + [((2, model // 2, c), BF16) for c in wide]
+            + [((2, quarter, c) if i % 2 == 0 else (2 * quarter, c), BF16) for i, c in enumerate(wide)]
+            + [((quarter, c), BF16) for c in wide]
+            + [((depth - 1, model // n, c), BF16) for c in wide]
+            + [
+                ((5, 8, hidden), F32),
+                ((3, 8, hidden), F32),
+                ((3, 8, hidden), F32),
+                ((2, 8, hidden), F32),
+                ((depth - 1, 2, 8, hidden), F32),
+                dma((5, 4)), dma((5, 4)), dma((5, depth - 1)), dma((5, depth - 1)), dma((2, rows)), dma((2, rows)),
+                dma((4, 10)), dma((4, 10)), dma((6,)),
             ],
-            flops,
-            x, d_resid, w_qkv, w_out, qkv, probs, ctx, small, up_bias_grad, g_down, g_up, output,
-            far=(9, 10, 11), far_out=(1, 2), collective=0,
+            2 * mine * model * (24 * width + 12 * hidden),
+            x, cot, seg[:, :, None], seg[:, None, :], own_bias.astype(F32)[None], vectors,
+            q_weight, k_weight, v_weight, out_weight, up_weight, down_weight,
+            far=(6, 7, 8, 9, 10, 11), far_out=(1, 3), collective=0,
         )
-        sums, small = sums[0, :3].reshape(-1), sums[1]
+        g_attn = jnp.concatenate([g_first, g_last], -1)
+        small = sums[1, :, :model]
+        sums = jnp.concatenate([sums[0, 0, : 2 * width], sums[0, 1]])
     else:
+        w_qkv = with_peer(jnp.concatenate([q_weight, k_weight, v_weight], 1), n)
+        w_out = with_peer(out_weight, n)
+        w_up = with_peer(up_weight, n)
+        w_down = with_peer(down_weight, n)
+        bias = jnp.stack([own_bias, swap(own_bias)]).astype(F32)[:, None, :]
+        b_qkv = jnp.concatenate([bias[..., :width], jnp.zeros_like(bias[..., :width]), bias[..., width : 2 * width]], -1)
+        b_up = bias[..., 2 * width :]
+        vectors = jnp.stack([attn_gain, attn_shift, down_bias, ffn_gain, ffn_shift]).astype(F32)
+
+        qkv, probs, ctx, xhat, rstd, low = call(
+            attention_forward,
+            [
+                ((2, mine, 3 * width), BF16),
+                ((rows, 2 * heads, part, part), BF16),
+                ((2, mine, width), BF16),
+                ((mine, model), F32),
+                ((mine, 1), F32),
+                ((mine, model), BF16),
+            ],
+            [],
+            2 * mine * model * 8 * width,
+            x, w_qkv, b_qkv, w_out, seg[:, :, None], seg[:, None, :],
+            out_bias.astype(F32)[None], vectors[0:1], vectors[1:2],
+        )
+        output, g_down, g_up, d_resid, small, up_bias_grad = call(
+            feed_forward,
+            [
+                ((mine, model), BF16),
+                ((2, model, hidden), BF16),
+                ((2, model, hidden), BF16),
+                ((mine, model), F32),
+                ((8, model), F32),
+                ((2, 1, hidden), F32),
+            ],
+            [
+                ((2, mine, hidden), BF16),
+                ((2, mine, hidden), BF16),
+                ((mine, model), F32),
+                ((mine, model), BF16),
+                ((model, mine), BF16),
+                ((model, mine), BF16),
+            ],
+            2 * mine * model * 2 * hidden * 6,
+            low, xhat, rstd, w_up, b_up, w_down, vectors, cot,
+        )
+        scratch = [((2, mine, 3 * width), BF16), ((model, mine), BF16), ((model, mine), BF16)]
+        flops = 2 * mine * model * 16 * width
         output_peer = swap(output)
         grad_in, g_attn, bias_grad = call(
             attention_backward_plain,

time: 313 us -> 255 us (0.81)
  waiting for transfers between devices: 56.7 us -> 0 us
  Pallas kernels: 192 us -> 223 us
  other arithmetic: 23.2 us -> 9.03 us
  local copies, waits for them, and re-layouts: 31.6 us -> 20.9 us
  starting transfers between devices: 6.77 us -> 0 us
    ppermute x9 -> x0, waiting for transfers between devices: 56.7 us -> none  [the longest x5 56.7 us: swap(): return lax.ppermute(v, 'mp', [(0, 1), (1, 0)])]
    pallas_call x3 -> x1, Pallas kernels: 192 us -> 223 us  [call(): pl.pallas_call(kernel, out_shape=shapes, in_specs=[pl.BlockSpec(memory_sp...]
    another operation x8 -> x0, other arithmetic: 8.97 us -> none  [with_peer(): return jnp.stack([own, peer])]
    ppermute x9 -> x0, starting transfers between devices: 6.77 us -> none  [the longest x5 6.12 us: swap(): return lax.ppermute(v, 'mp', [(0, 1), (1, 0)])]
    dynamic_slice x4 -> x0, local copies, waits for them, and re-layouts: 6.15 us -> none  [with_peer(): mine = swap(lax.dynamic_slice_in_dim(own, core * half, half, 0))]
    unnamed x50 -> x10, local copies, waits for them, and re-layouts: 7.52 us -> 1.44 us
    select_n x4 -> x0, other arithmetic: 5.59 us -> none  [with_peer(): jnp.where(first, mine, other)]
  transfers between devices with their start and end apart: 9 -> 0, of which waited for: 1 -> 0; matrix products, arithmetic and copies ran while one was open for 9% -> 0% of each run, Pallas kernels for 6% -> 0%
where the time goes in v3:
time: 255 us; the launch traced here: 253 us
  Pallas kernels  223 us (87%)
  local copies, waits for them, and re-layouts  20.9 us (8%)
  other arithmetic  9.03 us (4%)
    pallas_call x1, Pallas kernels, call(): pl.pallas_call(kernel, out_shape=shapes, in_specs=[pl.BlockSpec(memory_sp...  223 us

profile of v3, /device:TPU:0, one launch (start us, length us, event | category | flops | bytes accessed | tf_op | source)
XLA Modules:
  0.0 253.3 jit_solution(6966572478275246347)
XLA Ops:
  0.7 0.7 concatenate.16
  1.3 0.7 concatenate.17
  2.0 0.9 reduce_window_sum.11
  2.9 0.8 select_reduce_fusion
  3.7 0.7 stack.36
  4.4 0.7 stack.31
  5.1 0.7 stack.32
  5.7 0.7 stack.33
  6.4 0.7 stack.34
  7.1 0.7 stack.35
  7.9 0.1 lt.27
  8.0 0.1 convert_reduce_fusion
  8.1 0.6 slice_select_fusion
  8.7 0.6 broadcast_in_dim.50.seg_r_ref
  9.3 0.7 concatenate.18
  10.0 0.6 maximum_convert_fusion.bias_ref
  10.6 0.6 convert_element_type.18.vec_ref
  11.2 1.0 copy.46.seg_c_ref
  12.1 2.6 %fusion = (bf16[3,1,256,768]{3,2,1,0:T(8,128)(2,1)S(1)}, bf16[3,1,256,768]{3,2,1,0:T(8,128)(2,1)S(1)}, bf16[3,1,256,768]{3,2,1,0:T(8,128)(2,1)S(1)}, bf16[3,1,256,768]{3,2,1,0:T(8,128)(2,1)S(1)}) fusion(bf16[3,2,256,768]{3,2,1,0:T(8,128)(2,1)} %bitcast.30, bf16[3,2,256,768]{3,2,1,0:T(8,128)(2,1)} %bitcast.31), kind=kLoop, calls=%fused_computation.26 | loop fusion | bytes 9437184 | tf_op jit(solution)/shard_map/slice | solution.py:807
  14.8 2.2 bitcast_select_fusion
  17.0 222.7 %shard_map.305 = (bf16[768,768]{1,0:T(8,128)(2,1)}, bf16[768,768]{1,0:T(8,128)(2,1)}, bf16[768,768]{1,0:T(8,128)(2,1)}, bf16[768,768]{1,0:T(8,128)(2,1)}, f32[48...) custom-call(bf16[768,768]{1,0:T(8,128)(2,1)} %get-tuple-element.60.x_re, ...), custom_call_target="tpu_custom_call" | custom-call | flops 32614907904 | bytes 15172608 | tf_op jit(solution)/shard_map/pallas_call | solution.py:720
  239.7 2.8 %broadcast_select_fusion.1 = (bf16[3,1,256,768]{3,2,0,1:T(8,128)(2,1)S(1)}, bf16[3,1,256,768]{3,2,0,1:T(8,128)(2,1)S(1)}, bf16[3,1,256,768]{3,2,0,1:T(8,128)(2,1)S(1)}, bf16[3,1,256,768]{3,2,0,1:T(8,128)(2,1)S(1)}) fusion(bf16[3,1,256,768]{3,2,0,1:T(8,128)(2,1)} %bitcast.35, bf16[3,1,256,768]{3,2,0,1:T(8,128)(2,1)} %bitcast.34, ...), kind=kLoop, calls=%fused_computation.5 | loop fusion | flops 2359296 | bytes 9437952 | tf_op jit(solution)/shard_map/jit(_where)/select_n | solution.py:811
  242.5 0.2 pad_maximum_fusion.1
  242.7 0.0 copy-start.3
  242.7 0.0 copy-start.2
  242.7 1.6 copy.48
  244.3 1.3 slice_reduce_fusion.7
  245.6 1.4 slice_reduce_fusion
  247.0 1.7 slice_reduce_fusion.1
  248.8 0.0 copy-done.3
  248.8 0.7 fusion.2
  249.4 0.0 copy-done.2
  249.4 0.7 slice_bitcast_fusion
  250.1 0.2 pad_maximum_fusion
  250.3 0.0 copy-start.1
  250.3 0.0 copy-start
  250.3 1.6 copy.47
  251.9 0.0 copy-done.1
  251.9 0.7 copy.55
  252.6 0.0 copy-done
  252.6 0.7 copy.56
  (7 shorter events, 0.1 us)
Async XLA Ops:
  242.7 6.1 %copy-start.3 = (f32[48,768]{1,0:T(8,128)S(1)}, f32[48,768]{1,0:T(8,128)}, u32[]{:S(2)}) copy-start(f32[48,768]{1,0:T(8,128)} %get-tuple-element.30) | copy-start | bytes 442372
  242.7 6.7 %copy-start.2 = (f32[48,768]{1,0:T(8,128)S(1)}, f32[48,768]{1,0:T(8,128)}, u32[]{:S(2)}) copy-start(f32[48,768]{1,0:T(8,128)} %get-tuple-element.32) | copy-start | bytes 442372
  250.3 1.6 copy-start.1
  250.3 2.3 copy-start

commit v4 on v3

--- a/solution.py
+++ b/solution.py
@@ -260,16 +260,18 @@
         weight_products(g, x_t_ref, dattn_t_ref, dq_ref, ctx_ref, ga_ref)
 
 
+WAYS = ("yzx", "yxz", "yxz", "xyz")
+
+
 def whole_layer(
     n, x_ref, cot_ref, seg_c_ref, seg_r_ref, bias_ref, vec_ref, wq_hbm, wk_hbm, wv_hbm, wo_hbm, up_hbm, down_hbm,
     out_ref, out_peer_ref, in_ref, in_peer_ref, rd_ref, ru_ref, ra_ref, rb_ref, sums_ref,
     w_ref, wo_ref, up_ref, down_ref, bias_2, qkv_ref, p_ref, ctx_ref, xhat_ref, rstd_ref, low_ref, act_ref, slope_ref,
     acc_ref, dffn_ref, t_low_ref, t_grad_ref, small_ref, *rest_refs,
 ):
-    ways = ("line", "x", "line", "x")
     half, mid, owned, shard = rest_refs[0:4], rest_refs[4:8], rest_refs[8:12], rest_refs[12:16]
-    tiny, tiny_1, tiny_2, tiny_x, tiny_z = rest_refs[16:21]
-    send, recv, send_z, recv_z, send_in, recv_in, g_send, g_recv, g_local = rest_refs[21:]
+    tiny, tiny_1, tiny_2, tiny_x, tiny_z, last = rest_refs[16:22]
+    send, recv, send_z, recv_z, send_in, recv_in, g_send, g_recv, g_local = rest_refs[22:]
     seqs, length = seg_c_ref.shape[0], seg_c_ref.shape[1]
     groups, width, model = wo_ref.shape
     hidden = up_ref.shape[2]
@@ -376,21 +378,42 @@
         there = pl.ds(pl.multiple_of((1 - core) * n_half, n_half), n_half)
         return remote(sources[t].at[:, there, :], half[t], send.at[0, t], recv.at[0, t], to_core)
 
+    def quarter_of(place):
+        return pl.ds(pl.multiple_of(place * n_quarter, n_quarter), n_quarter)
+
+    def own_rows(place):
+        return pl.ds(pl.multiple_of(place * rows_own, rows_own), rows_own)
+
     def by_first(t):
-        if ways[t] == "line":
-            there = pl.ds(pl.multiple_of((1 - line) * n_quarter, n_quarter), n_quarter)
-            return remote(half[t].at[:, there, :], mid[t], send.at[1, t], recv.at[1, t], to_line)
-        return remote(half[t].at[1], mid[t], send.at[1, t], recv.at[1, t], to_x)
+        if WAYS[t] == "xyz":
+            return remote(half[t].at[1], mid[t], send.at[1, t], recv.at[1, t], to_x)
+        return remote(half[t].at[:, quarter_of(1 - line), :], mid[t], send.at[1, t], recv.at[1, t], to_line)
 
     def by_second(t):
-        if ways[t] == "line":
-            return remote(mid[t].at[1], owned[t], send.at[2, t], recv.at[2, t], to_x)
-        there = pl.ds(pl.multiple_of((1 - line) * n_quarter, n_quarter), n_quarter)
-        return remote(mid[t].at[there, :], owned[t], send.at[2, t], recv.at[2, t], to_line)
+        if WAYS[t] == "xyz":
+            return remote(mid[t].at[quarter_of(1 - line), :], owned[t], send.at[2, t], recv.at[2, t], to_line)
+        if WAYS[t] == "yzx":
+            return remote(owned[t].at[1], last, send.at[2, t], recv.at[2, t], to_x)
+        return remote(mid[t].at[1], owned[t], send.at[2, t], recv.at[2, t], to_x)
 
     def by_rest(t, k):
-        there = pl.ds(pl.multiple_of((rest + k) % depth * rows_own, rows_own), rows_own)
-        return remote(owned[t].at[there, :], shard[t].at[k - 1], send_z.at[t, k - 1], recv_z.at[t, k - 1], to_rest(k))
+        there = own_rows((rest + k) % depth)
+        source = mid[t].at[:, there, :] if WAYS[t] == "yzx" else owned[t].at[there, :]
+        return remote(source, shard[t].at[k - 1], send_z.at[t, k - 1], recv_z.at[t, k - 1], to_rest(k))
+
+    def start_rest(t):
+        for k in range(1, depth):
+            by_rest(t, k).start()
+
+    def rest_sum(t):
+        if WAYS[t] == "yzx":
+            total = mid[t][:, own_rows(rest), :].astype(F32)
+        else:
+            total = owned[t][own_rows(rest), :].astype(F32)
+        for k in range(1, depth):
+            by_rest(t, k).wait_recv()
+            total = total + shard[t][k - 1].astype(F32)
+        return total
 
     def after_core(t):
         by_core(t).wait_recv()
@@ -400,28 +423,36 @@
 
     def after_first(t):
         by_first(t).wait_recv()
-        if ways[t] == "line":
+        if WAYS[t] == "xyz":
+            add_rows(mid[t], half[t].at[0], 0, 96)
+        else:
             for g in range(groups):
                 add_rows(mid[t].at[g], half[t].at[g], line * n_quarter, 96)
+        if WAYS[t] == "yzx":
+            start_rest(t)
         else:
-            add_rows(mid[t], half[t].at[0], 0, 96)
-        by_second(t).start()
-
-    def after_second(t):
+            by_second(t).start()
+
+    def after_second(t, out):
+        if WAYS[t] == "yzx":
+            total = rest_sum(t)
+            out[...] = total[0]
+            owned[t][...] = total.astype(BF16)
+            by_second(t).start()
+            return
         by_second(t).wait_recv()
-        if ways[t] == "line":
+        if WAYS[t] == "xyz":
+            add_rows(owned[t], mid[t], line * n_quarter, 96)
+        else:
             add_rows(owned[t], mid[t].at[0], 0, 96)
+        start_rest(t)
+
+    def finish(t, out):
+        if WAYS[t] == "yzx":
+            by_second(t).wait_recv()
+            out[...] += last[...].astype(F32)
         else:
-            add_rows(owned[t], mid[t], line * n_quarter, 96)
-        for k in range(1, depth):
-            by_rest(t, k).start()
-
-    def after_rest(t, out):
-        total = owned[t][pl.ds(pl.multiple_of(rest * rows_own, rows_own), rows_own), :].astype(F32)
-        for k in range(1, depth):
-            by_rest(t, k).wait_recv()
-            total = total + shard[t][k - 1].astype(F32)
-        out[...] = total
+            out[...] = rest_sum(t)
 
     def send_output(b):
         rows = pl.ds(pl.multiple_of(b * length, length), length)
@@ -527,31 +558,31 @@
 
         @pl.when(c == 0)
         def _():
+            second_hop(4, 0)
+            second_hop(5, 0)
+
+        @pl.when(c == 1)
+        def _():
             first_hop(4, 1)
             first_hop(5, 1)
 
-        @pl.when(c == 1)
+    @pl.loop(0, 3)
+    def _(c):
+        complete(4, c)
+        complete(5, c)
+        expand(c, 1, bias_2)
+
+        @pl.when(c == 0)
         def _():
-            second_hop(4, 0)
-            second_hop(5, 0)
-
-        @pl.when(c == 2)
-        def _():
+            second_hop(4, 1)
+            second_hop(5, 1)
             first_hop(4, 2)
             first_hop(5, 2)
-            second_hop(4, 1)
-            second_hop(5, 1)
-
-    @pl.loop(0, 3)
-    def _(c):
-        @pl.when(c == 2)
+
+        @pl.when(c == 1)
         def _():
             second_hop(4, 2)
             second_hop(5, 2)
-
-        complete(4, c)
-        complete(5, c)
-        expand(c, 1, bias_2)
 
     small_ref[...] = jnp.zeros_like(small_ref)
 
@@ -641,10 +672,6 @@
         def _():
             after_first(0)
 
-        @pl.when(s == min(2, seqs - 1))
-        def _():
-            after_second(0)
-
     for kind in range(4):
         sent(kind)
     for c in range(3):
@@ -675,28 +702,29 @@
     tiny_1[...] += tiny[0:3]
     tiny_line.start()
     after_first(1)
-    after_first(2)
+    after_second(0, rd_ref)
     tiny_line.wait_recv()
     tiny_2[...] += tiny_1[...]
     tiny_over.start()
     after_first(3)
-    after_rest(0, rd_ref)
-    after_second(1)
+    after_first(2)
+    after_second(1, ru_ref)
     tiny_over.wait_recv()
     tiny_x[0] += tiny_2[0]
     tiny_x[1] += tiny_2[2]
     for k in range(1, depth):
         tiny_rest(k).start()
-    after_second(2)
-    after_second(3)
-    after_rest(1, ru_ref)
+    finish(0, rd_ref)
+    after_second(3, rb_ref)
+    after_second(2, ra_ref)
+    finish(1, ru_ref)
     total = tiny_x[...]
     for k in range(1, depth):
         tiny_rest(k).wait_recv()
         total = total + tiny_z[k - 1]
     sums_ref[...] = total
-    after_rest(2, ra_ref)
-    after_rest(3, rb_ref)
+    finish(3, rb_ref)
+    finish(2, ra_ref)
     for s in range(seqs):
         send_output(s).wait()
         send_input(s).wait()
@@ -853,15 +881,16 @@
                 ((8, model), F32),
             ]
             + [((2, model // 2, c), BF16) for c in wide]
-            + [((2, quarter, c) if i % 2 == 0 else (2 * quarter, c), BF16) for i, c in enumerate(wide)]
-            + [((quarter, c), BF16) for c in wide]
-            + [((depth - 1, model // n, c), BF16) for c in wide]
+            + [((2 * quarter, c) if w == "xyz" else (2, quarter, c), BF16) for w, c in zip(WAYS, wide)]
+            + [((2, model // n, c) if w == "yzx" else (quarter, c), BF16) for w, c in zip(WAYS, wide)]
+            + [((depth - 1,) + (2,) * (w == "yzx") + (model // n, c), BF16) for w, c in zip(WAYS, wide)]
             + [
                 ((5, 8, hidden), F32),
                 ((3, 8, hidden), F32),
                 ((3, 8, hidden), F32),
                 ((2, 8, hidden), F32),
                 ((depth - 1, 2, 8, hidden), F32),
+                ((model // n, hidden), BF16),
                 dma((5, 4)), dma((5, 4)), dma((5, depth - 1)), dma((5, depth - 1)), dma((2, rows)), dma((2, rows)),
                 dma((4, 10)), dma((4, 10)), dma((6,)),
             ],

time: 255 us -> 222 us (0.87)
  Pallas kernels: 223 us -> 190 us
    pallas_call x1, Pallas kernels: 223 us -> 190 us  [call(): pl.pallas_call(kernel, out_shape=shapes, in_specs=[pl.BlockSpec(memory_sp...]
where the time goes in v4:
time: 222 us; the launch traced here: 221 us
  Pallas kernels  190 us (86%)
  local copies, waits for them, and re-layouts  20.9 us (9%)
  other arithmetic  9.03 us (4%)
    pallas_call x1, Pallas kernels, call(): pl.pallas_call(kernel, out_shape=shapes, in_specs=[pl.BlockSpec(memory_sp...  190 us

profile of v4, /device:TPU:0, one launch (start us, length us, event | category | flops | bytes accessed | tf_op | source)
XLA Modules:
  0.0 221.1 jit_solution(10516815760562421340)
XLA Ops:
  0.7 0.7 concatenate.16
  1.3 0.7 concatenate.17
  2.0 0.9 reduce_window_sum.11
  2.9 0.8 select_reduce_fusion
  3.7 0.7 stack.36
  4.4 0.7 stack.31
  5.1 0.7 stack.32
  5.7 0.7 stack.33
  6.4 0.7 stack.34
  7.1 0.7 stack.35
  7.9 0.1 lt.27
  8.0 0.1 convert_reduce_fusion
  8.1 0.6 slice_select_fusion
  8.7 0.6 broadcast_in_dim.50.seg_r_ref
  9.3 0.7 concatenate.18
  10.0 0.6 maximum_convert_fusion.bias_ref
  10.6 0.6 convert_element_type.18.vec_ref
  11.2 1.0 copy.46.seg_c_ref
  12.1 2.6 %fusion = (bf16[3,1,256,768]{3,2,1,0:T(8,128)(2,1)S(1)}, bf16[3,1,256,768]{3,2,1,0:T(8,128)(2,1)S(1)}, bf16[3,1,256,768]{3,2,1,0:T(8,128)(2,1)S(1)}, bf16[3,1,256,768]{3,2,1,0:T(8,128)(2,1)S(1)}) fusion(bf16[3,2,256,768]{3,2,1,0:T(8,128)(2,1)} %bitcast.30, bf16[3,2,256,768]{3,2,1,0:T(8,128)(2,1)} %bitcast.31), kind=kLoop, calls=%fused_computation.26 | loop fusion | bytes 9437184 | tf_op jit(solution)/shard_map/slice | solution.py:835
  14.8 2.2 %bitcast_select_fusion = (bf16[768,768]{1,0:T(8,128)(2,1)}, bf16[768,768]{1,0:T(8,128)(2,1)}) fusion(bf16[3,1,256,768]{3,2,1,0:T(8,128)(2,1)S(1)} %get-tuple-element.50, bf16[3,1,256,768]{3,2,1,0:T(8,128)(2,1)S(1)} %get-tuple-element.49, pred[768]{0:T(1024)(128)(4,1)S(1)} %compare_compare_fusion, bf16[3,1,256,768]{3,2,1,0:T(8,128)(2,1)S(1)} %get-tuple-element.61, ...), kind=kLoop, calls=%fused_computation.2 | loop fusion | flops 1179648 | bytes 7078656 | tf_op jit(solution)/shard_map/jit(_where)/select_n | solution.py:835
  17.0 190.4 %shard_map.305 = (bf16[768,768]{1,0:T(8,128)(2,1)}, bf16[768,768]{1,0:T(8,128)(2,1)}, bf16[768,768]{1,0:T(8,128)(2,1)}, bf16[768,768]{1,0:T(8,128)(2,1)}, f32[48...) custom-call(bf16[768,768]{1,0:T(8,128)(2,1)} %get-tuple-element.60.x_re, ...), custom_call_target="tpu_custom_call" | custom-call | flops 32614907904 | bytes 15172608 | tf_op jit(solution)/shard_map/pallas_call | solution.py:748
  207.5 2.8 %broadcast_select_fusion.1 = (bf16[3,1,256,768]{3,2,0,1:T(8,128)(2,1)S(1)}, bf16[3,1,256,768]{3,2,0,1:T(8,128)(2,1)S(1)}, bf16[3,1,256,768]{3,2,0,1:T(8,128)(2,1)S(1)}, bf16[3,1,256,768]{3,2,0,1:T(8,128)(2,1)S(1)}) fusion(bf16[3,1,256,768]{3,2,0,1:T(8,128)(2,1)} %bitcast.35, bf16[3,1,256,768]{3,2,0,1:T(8,128)(2,1)} %bitcast.34, ...), kind=kLoop, calls=%fused_computation.5 | loop fusion | flops 2359296 | bytes 9437952 | tf_op jit(solution)/shard_map/jit(_where)/select_n | solution.py:839
  210.2 0.2 pad_maximum_fusion.1
  210.5 0.0 copy-start.3
  210.5 0.0 copy-start.2
  210.5 1.6 copy.48
  212.0 1.3 slice_reduce_fusion.7
  213.4 1.4 slice_reduce_fusion
  214.8 1.7 slice_reduce_fusion.1
  216.5 0.0 copy-done.3
  216.5 0.7 fusion.2
  217.2 0.0 copy-done.2
  217.2 0.7 slice_bitcast_fusion
  217.9 0.2 pad_maximum_fusion
  218.1 0.0 copy-start.1
  218.1 0.0 copy-start
  218.1 1.6 copy.47
  219.7 0.0 copy-done.1
  219.7 0.7 copy.55
  220.4 0.0 copy-done
  220.4 0.7 copy.56
  (7 shorter events, 0.1 us)
Async XLA Ops:
  210.5 6.1 %copy-start.3 = (f32[48,768]{1,0:T(8,128)S(1)}, f32[48,768]{1,0:T(8,128)}, u32[]{:S(2)}) copy-start(f32[48,768]{1,0:T(8,128)} %get-tuple-element.30) | copy-start | bytes 442372
  210.5 6.7 %copy-start.2 = (f32[48,768]{1,0:T(8,128)S(1)}, f32[48,768]{1,0:T(8,128)}, u32[]{:S(2)}) copy-start(f32[48,768]{1,0:T(8,128)} %get-tuple-element.32) | copy-start | bytes 442372
  218.1 1.6 copy-start.1
  218.1 2.3 %copy-start = (f32[48,1536]{1,0:T(8,128)S(1)}, f32[48,1536]{1,0:T(8,128)}, u32[]{:S(2)}) copy-start(f32[48,1536]{1,0:T(8,128)} %get-tuple-element.34) | copy-start | bytes 884740

commit v5 on v4

--- a/solution.py
+++ b/solution.py
@@ -524,10 +524,17 @@
         rstd_ref[rows, :] = rstd
         low_ref[rows, :] = (xhat * attn_gain + attn_shift).astype(BF16)
 
-        @pl.when(s == min(1, seqs - 1))
+        @pl.when(s == 0)
         def _():
             first_hop(4, 0)
+
+        @pl.when(s == 1)
+        def _():
             first_hop(5, 0)
+
+        @pl.when(s == 2)
+        def _():
+            first_hop(4, 1)
 
     for copy in own_copies[4:]:
         copy.wait()
@@ -559,12 +566,16 @@
         @pl.when(c == 0)
         def _():
             second_hop(4, 0)
-            second_hop(5, 0)
 
         @pl.when(c == 1)
         def _():
-            first_hop(4, 1)
+            second_hop(5, 0)
             first_hop(5, 1)
+
+        @pl.when(c == 2)
+        def _():
+            second_hop(4, 1)
+            first_hop(4, 2)
 
     @pl.loop(0, 3)
     def _(c):
@@ -574,10 +585,8 @@
 
         @pl.when(c == 0)
         def _():
-            second_hop(4, 1)
+            first_hop(5, 2)
             second_hop(5, 1)
-            first_hop(4, 2)
-            first_hop(5, 2)
 
         @pl.when(c == 1)
         def _():
@@ -672,57 +681,56 @@
         def _():
             after_first(0)
 
-    for kind in range(4):
-        sent(kind)
-    for c in range(3):
-        sent(4, c)
-        sent(5, c)
-    for g in range(groups):
-        weight_products(g, t_low_ref, t_grad_ref, qkv_ref, ctx_ref, up_ref)
-    by_core(2).start()
-    by_core(3).start()
+    tiny_core = remote(tiny.at[0:3], tiny_1, send.at[3, 1], recv.at[3, 1], to_core)
+    tiny_line = remote(tiny_1, tiny_2, send.at[3, 2], recv.at[3, 2], to_line)
+    tiny_over = remote(tiny_2.at[1:3], tiny_x, send.at[3, 3], recv.at[3, 3], to_x)
+
+    def tiny_rest(k):
+        return remote(tiny_x, tiny_z.at[k - 1], send_z.at[4, k - 1], recv_z.at[4, k - 1], to_rest(k))
+
     for g in range(groups):
         column = jnp.sum(qkv_ref[g].astype(F32), 0, keepdims=True)
         tiny[g, 0:1, :width] = column[:, :width]
         tiny[g, 0:1, width : 2 * width] = column[:, 2 * width :]
         tiny[g, 1:2, :] = tiny[3 + g, 0:1, :]
     tiny[2, :, :model] = small_ref[...]
-
-    tiny_core = remote(tiny.at[0:3], tiny_1, send.at[3, 1], recv.at[3, 1], to_core)
-    tiny_line = remote(tiny_1, tiny_2, send.at[3, 2], recv.at[3, 2], to_line)
-    tiny_over = remote(tiny_2.at[1:3], tiny_x, send.at[3, 3], recv.at[3, 3], to_x)
-
-    def tiny_rest(k):
-        return remote(tiny_x, tiny_z.at[k - 1], send_z.at[4, k - 1], recv_z.at[4, k - 1], to_rest(k))
-
+    for kind in range(4):
+        sent(kind)
+    for c in range(3):
+        sent(4, c)
+        sent(5, c)
     tiny_core.start()
-    after_core(2)
-    after_core(3)
+    for g in range(groups):
+        weight_products(g, t_low_ref, t_grad_ref, qkv_ref, ctx_ref, up_ref)
+    by_core(2).start()
+    by_core(3).start()
     tiny_core.wait_recv()
     tiny_1[...] += tiny[0:3]
     tiny_line.start()
-    after_first(1)
-    after_second(0, rd_ref)
+    after_core(2)
+    after_core(3)
     tiny_line.wait_recv()
     tiny_2[...] += tiny_1[...]
     tiny_over.start()
+    after_first(1)
+    after_second(0, rd_ref)
     after_first(3)
-    after_first(2)
-    after_second(1, ru_ref)
     tiny_over.wait_recv()
     tiny_x[0] += tiny_2[0]
     tiny_x[1] += tiny_2[2]
     for k in range(1, depth):
         tiny_rest(k).start()
+    after_first(2)
+    after_second(1, ru_ref)
+    after_second(3, rb_ref)
     finish(0, rd_ref)
-    after_second(3, rb_ref)
     after_second(2, ra_ref)
-    finish(1, ru_ref)
     total = tiny_x[...]
     for k in range(1, depth):
         tiny_rest(k).wait_recv()
         total = total + tiny_z[k - 1]
     sums_ref[...] = total
+    finish(1, ru_ref)
     finish(3, rb_ref)
     finish(2, ra_ref)
     for s in range(seqs):

time: 222 us -> 204 us (0.919)
  Pallas kernels: 190 us -> 173 us
    pallas_call x1, Pallas kernels: 190 us -> 173 us  [call(): pl.pallas_call(kernel, out_shape=shapes, in_specs=[pl.BlockSpec(memory_sp...]
where the time goes in v5:
time: 204 us
  Pallas kernels  173 us (85%)
  local copies, waits for them, and re-layouts  20.9 us (10%)
  other arithmetic  9.03 us (4%)
    pallas_call x1, Pallas kernels, call(): pl.pallas_call(kernel, out_shape=shapes, in_specs=[pl.BlockSpec(memory_sp...  173 us
    another operation x7, local copies, waits for them, and re-layouts, per_device(): jnp.stack([attn_gain, attn_shift, down_bias, ffn_gain, ffn_shift, out_bias])  4.15 us

profile of v5, /device:TPU:0, one launch (start us, length us, event | category | flops | bytes accessed | tf_op | source)
XLA Modules:
  0.0 203.7 jit_solution(18243054417620309725)
XLA Ops:
  0.7 0.7 concatenate.16
  1.3 0.7 concatenate.17
  2.0 0.9 reduce_window_sum.11
  2.9 0.8 select_reduce_fusion
  3.7 0.7 stack.36
  4.4 0.7 stack.31
  5.1 0.7 stack.32
  5.7 0.7 stack.33
  6.4 0.7 stack.34
  7.1 0.7 stack.35
  7.9 0.1 lt.27
  8.0 0.1 convert_reduce_fusion
  8.1 0.6 slice_select_fusion
  8.7 0.6 broadcast_in_dim.50.seg_r_ref
  9.3 0.7 concatenate.18
  10.0 0.6 maximum_convert_fusion.bias_ref
  10.6 0.6 convert_element_type.18.vec_ref
  11.2 1.0 copy.46.seg_c_ref
  12.1 2.6 %fusion = (bf16[3,1,256,768]{3,2,1,0:T(8,128)(2,1)S(1)}, bf16[3,1,256,768]{3,2,1,0:T(8,128)(2,1)S(1)}, bf16[3,1,256,768]{3,2,1,0:T(8,128)(2,1)S(1)}, bf16[3,1,256,768]{3,2,1,0:T(8,128)(2,1)S(1)}) fusion(bf16[3,2,256,768]{3,2,1,0:T(8,128)(2,1)} %bitcast.30, bf16[3,2,256,768]{3,2,1,0:T(8,128)(2,1)} %bitcast.31), kind=kLoop, calls=%fused_computation.26 | loop fusion | bytes 9437184 | tf_op jit(solution)/shard_map/slice | solution.py:843
  14.8 2.2 %bitcast_select_fusion = (bf16[768,768]{1,0:T(8,128)(2,1)}, bf16[768,768]{1,0:T(8,128)(2,1)}) fusion(bf16[3,1,256,768]{3,2,1,0:T(8,128)(2,1)S(1)} %get-tuple-element.50, bf16[3,1,256,768]{3,2,1,0:T(8,128)(2,1)S(1)} %get-tuple-element.49, pred[768]{0:T(1024)(128)(4,1)S(1)} %compare_compare_fusion, bf16[3,1,256,768]{3,2,1,0:T(8,128)(2,1)S(1)} %get-tuple-element.61, ...), kind=kLoop, calls=%fused_computation.2 | loop fusion | flops 1179648 | bytes 7078656 | tf_op jit(solution)/shard_map/jit(_where)/select_n | solution.py:843
  17.0 173.1 %shard_map.305 = (bf16[768,768]{1,0:T(8,128)(2,1)}, bf16[768,768]{1,0:T(8,128)(2,1)}, bf16[768,768]{1,0:T(8,128)(2,1)}, bf16[768,768]{1,0:T(8,128)(2,1)}, f32[48...) custom-call(bf16[768,768]{1,0:T(8,128)(2,1)} %get-tuple-element.60.x_re, ...), custom_call_target="tpu_custom_call" | custom-call | flops 32614907904 | bytes 15172608 | tf_op jit(solution)/shard_map/pallas_call | solution.py:756
  190.1 2.8 %broadcast_select_fusion.1 = (bf16[3,1,256,768]{3,2,0,1:T(8,128)(2,1)S(1)}, bf16[3,1,256,768]{3,2,0,1:T(8,128)(2,1)S(1)}, bf16[3,1,256,768]{3,2,0,1:T(8,128)(2,1)S(1)}, bf16[3,1,256,768]{3,2,0,1:T(8,128)(2,1)S(1)}) fusion(bf16[3,1,256,768]{3,2,0,1:T(8,128)(2,1)} %bitcast.35, bf16[3,1,256,768]{3,2,0,1:T(8,128)(2,1)} %bitcast.34, ...), kind=kLoop, calls=%fused_computation.5 | loop fusion | flops 2359296 | bytes 9437952 | tf_op jit(solution)/shard_map/jit(_where)/select_n | solution.py:847
  192.9 0.2 pad_maximum_fusion.1
  193.1 0.0 copy-start.3
  193.1 0.0 copy-start.2
  193.1 1.6 copy.48
  194.7 1.3 slice_reduce_fusion.7
  196.0 1.4 slice_reduce_fusion
  197.4 1.7 slice_reduce_fusion.1
  199.1 0.0 copy-done.3
  199.1 0.7 fusion.2
  199.8 0.0 copy-done.2
  199.8 0.7 slice_bitcast_fusion
  200.5 0.2 pad_maximum_fusion
  200.7 0.0 copy-start.1
  200.7 0.0 copy-start
  200.7 1.6 copy.47
  202.3 0.0 copy-done.1
  202.3 0.7 copy.55
  203.0 0.0 copy-done
  203.0 0.7 copy.56
  (7 shorter events, 0.1 us)
Async XLA Ops:
  193.1 6.1 %copy-start.3 = (f32[48,768]{1,0:T(8,128)S(1)}, f32[48,768]{1,0:T(8,128)}, u32[]{:S(2)}) copy-start(f32[48,768]{1,0:T(8,128)} %get-tuple-element.30) | copy-start | bytes 442372
  193.1 6.7 %copy-start.2 = (f32[48,768]{1,0:T(8,128)S(1)}, f32[48,768]{1,0:T(8,128)}, u32[]{:S(2)}) copy-start(f32[48,768]{1,0:T(8,128)} %get-tuple-element.32) | copy-start | bytes 442372
  200.7 1.6 copy-start.1
  200.7 2.3 %copy-start = (f32[48,1536]{1,0:T(8,128)S(1)}, f32[48,1536]{1,0:T(8,128)}, u32[]{:S(2)}) copy-start(f32[48,1536]{1,0:T(8,128)} %get-tuple-element.34) | copy-start | bytes 884740

commit v6 on v5

--- a/solution.py
+++ b/solution.py
@@ -264,14 +264,16 @@
 
 
 def whole_layer(
-    n, x_ref, cot_ref, seg_c_ref, seg_r_ref, bias_ref, vec_ref, wq_hbm, wk_hbm, wv_hbm, wo_hbm, up_hbm, down_hbm,
-    out_ref, out_peer_ref, in_ref, in_peer_ref, rd_ref, ru_ref, ra_ref, rb_ref, sums_ref,
+    n, doc_ref, x_hbm, cot_hbm, vec_ref, wq_hbm, wk_hbm, wv_hbm, wo_hbm, up_hbm, down_hbm,
+    output_hbm, input_hbm, rd_ref, ru_ref, ra_ref, rb_ref, sums_ref,
+    x_ref, cot_ref, seg_c_ref, seg_r_ref, out_ref, out_peer_ref, in_peer_ref,
     w_ref, wo_ref, up_ref, down_ref, bias_2, qkv_ref, p_ref, ctx_ref, xhat_ref, rstd_ref, low_ref, act_ref, slope_ref,
-    acc_ref, dffn_ref, t_low_ref, t_grad_ref, small_ref, *rest_refs,
+    acc_ref, t_low_ref, t_grad_ref, small_ref, *rest_refs,
 ):
+    in_ref, dffn_ref = cot_ref, low_ref
     half, mid, owned, shard = rest_refs[0:4], rest_refs[4:8], rest_refs[8:12], rest_refs[12:16]
     tiny, tiny_1, tiny_2, tiny_x, tiny_z, last = rest_refs[16:22]
-    send, recv, send_z, recv_z, send_in, recv_in, g_send, g_recv, g_local = rest_refs[22:]
+    send, recv, send_z, recv_z, send_in, recv_in, g_send, g_recv, g_local, raw, done = rest_refs[22:]
     seqs, length = seg_c_ref.shape[0], seg_c_ref.shape[1]
     groups, width, model = wo_ref.shape
     hidden = up_ref.shape[2]
@@ -353,6 +355,7 @@
         for hop in (1, 2, 3):
             pass_on(kind, c, hop).wait_send()
 
+    bias_ref = vec_ref.at[:, 6 * model :]
     bias_over = remote(bias_ref, bias_2, send.at[4, 0], recv.at[4, 0], to_x)
     bias_over.start()
     for kind in range(4):
@@ -367,8 +370,56 @@
             + [(wo_hbm, wo_ref.at[0]), (up_hbm, up_ref.at[0]), (down_hbm, down_ref.at[0])]
         )
     ]
-    for copy in own_copies:
+    raw_copies = [
+        pltpu.make_async_copy(
+            source.at[(2 * r + h) * length : (2 * r + h + 1) * length, :],
+            act_ref.at[i, r * length : (r + 1) * length, h * model : (h + 1) * model],
+            raw.at[i, 2 * r + h],
+        )
+        for i, source in enumerate((x_hbm, cot_hbm))
+        for r in range(seqs)
+        for h in range(2)
+    ]
+    for copy in raw_copies[: 2 * seqs] + own_copies + raw_copies[2 * seqs :]:
         copy.start()
+
+    def starts(s):
+        ends, end, start = [], 0, 0
+        for d in range(doc_ref.shape[1]):
+            size = doc_ref[s, d]
+            end = end + size
+            ends.append(end)
+            start = start + jnp.where(size == length, end - length, 0)
+        return start, ends
+
+    def from_high(s, shape, dim):
+        place = lax.broadcasted_iota(jnp.int32, shape, dim)
+        return (place < starts(s)[0]).astype(jnp.int32) != x_index
+
+    def segments(s, shape, dim):
+        place = lax.broadcasted_iota(jnp.int32, shape, dim)
+        place = jnp.where(from_high(s, shape, dim), place + length, place)
+        segment = jnp.zeros(shape, jnp.int32)
+        for end in starts(s)[1]:
+            segment = segment + (place >= end).astype(jnp.int32)
+        return segment
+
+    def choose(s, i, dst):
+        rows = pl.ds(pl.multiple_of(s * length, length), length)
+        high = from_high(s, (length, model), 0)
+        first, second = act_ref[i, rows, :model].astype(F32), act_ref[i, rows, model:].astype(F32)
+        dst[rows, :] = jnp.where(high, second, first).astype(BF16)
+
+    def put_back(s, i, own, other):
+        rows = pl.ds(pl.multiple_of(s * length, length), length)
+        high = from_high(s, (length, model), 0)
+        a, b = own[rows, :].astype(F32), other[rows, :].astype(F32)
+        down_ref[i, pl.ds(pl.multiple_of(2 * s * length, length), length), :] = jnp.where(high, b, a).astype(BF16)
+        down_ref[i, pl.ds(pl.multiple_of((2 * s + 1) * length, length), length), :] = jnp.where(high, a, b).astype(BF16)
+
+    def put_out(s, i):
+        rows = pl.ds(pl.multiple_of(2 * s * length, length), 2 * length)
+        return pltpu.make_async_copy(down_ref.at[i, rows, :], (output_hbm, input_hbm)[i].at[rows, :], done.at[i, s])
 
     n_half, n_quarter = model // 2, model // 4
     cut = hidden // 2
@@ -462,8 +513,9 @@
         rows = pl.ds(pl.multiple_of(s * length, length), length)
         return remote(in_ref.at[rows, :], in_peer_ref.at[rows, :], send_in.at[0, s], recv_in.at[0, s], to_x)
 
-    attn_gain, attn_shift, down_bias = vec_ref[0:1, :], vec_ref[1:2, :], vec_ref[2:3, :]
-    ffn_gain, ffn_shift, out_bias = vec_ref[3:4, :], vec_ref[4:5, :], vec_ref[5:6, :]
+    attn_gain, attn_shift, down_bias, ffn_gain, ffn_shift, out_bias = (
+        vec_ref[:, i * model : (i + 1) * model] for i in range(6)
+    )
 
     def attend(s, g, biases):
         rows = pl.ds(pl.multiple_of(s * length, length), length)
@@ -493,18 +545,28 @@
         ctx_ref[g, rows, :] = ctx
         return mm(ctx, wo_ref[g])
 
-    for copy in own_copies[:4]:
+    for copy in raw_copies[: 2 * seqs] + own_copies[:4]:
         copy.wait()
 
     @pl.loop(0, seqs)
     def _(s):
         rows = pl.ds(pl.multiple_of(s * length, length), length)
+        choose(s, 0, x_ref)
+        seg_c_ref[s] = segments(s, (length, 1), 0)
+        seg_r_ref[s] = segments(s, (1, length), 1)
         acc_ref[rows, :] = x_ref[rows, :].astype(F32) + out_bias + attend(s, 0, bias_ref)
         for kind in range(3):
 
             @pl.when(s == min(kind, seqs - 1))
             def _():
                 first_hop(kind)
+
+    for copy in raw_copies[2 * seqs :]:
+        copy.wait()
+
+    @pl.loop(0, seqs)
+    def _(s):
+        choose(s, 1, cot_ref)
 
     first_hop(3)
     for kind in range(4):
@@ -709,6 +771,16 @@
     tiny_line.start()
     after_core(2)
     after_core(3)
+    for i, (one, own, other) in enumerate(
+        ((send_output, out_ref, out_peer_ref), (send_input, in_ref, in_peer_ref))
+    ):
+
+        @pl.loop(0, seqs)
+        def _(s):
+            one(s).wait_recv()
+            put_back(s, i, own, other)
+            put_out(s, i).start()
+
     tiny_line.wait_recv()
     tiny_2[...] += tiny_1[...]
     tiny_over.start()
@@ -734,8 +806,10 @@
     finish(3, rb_ref)
     finish(2, ra_ref)
     for s in range(seqs):
-        send_output(s).wait()
-        send_input(s).wait()
+        send_output(s).wait_send()
+        send_input(s).wait_send()
+        for i in range(2):
+            put_out(s, i).wait()
     for t in range(4):
         by_core(t).wait_send()
         by_first(t).wait_send()
@@ -749,14 +823,17 @@
         tiny_rest(k).wait_send()
 
 
-def call(kernel, outs, scratch, flops, *args, far=(), far_out=(), collective=None):
+def call(kernel, outs, scratch, flops, *args, scalar=(), far=(), far_out=(), collective=None):
     shapes = [jax.ShapeDtypeStruct(s, d) for s, d in outs]
     moved = sum(a.size * a.dtype.itemsize for a in args) + sum(s.size * s.dtype.itemsize for s in shapes)
     vmem = pl.BlockSpec(memory_space=pltpu.VMEM)
     return pl.pallas_call(
         kernel,
         out_shape=shapes,
-        in_specs=[pl.BlockSpec(memory_space=pl.ANY) if i in far else vmem for i in range(len(args))],
+        in_specs=[
+            pl.BlockSpec(memory_space=pltpu.SMEM if i in scalar else pl.ANY if i in far else pltpu.VMEM)
+            for i in range(len(args))
+        ],
         out_specs=[pl.BlockSpec(memory_space=pl.ANY) if i in far_out else vmem for i in range(len(shapes))],
         scratch_shapes=[pltpu.VMEM(*s) if isinstance(s, tuple) else s for s in scratch],
         compiler_params=pltpu.CompilerParams(
@@ -831,44 +908,31 @@
     heads = width // HD
     x_index = lax.axis_index("mp")
 
-    ends = jnp.cumsum(doc_lengths, axis=-1, dtype=jnp.int32)
-    start = jnp.sum(jnp.where(doc_lengths == part, ends - part, 0), -1)
-    place = jnp.arange(length, dtype=jnp.int32)
-    segment = jnp.sum((place[None, :, None] >= ends[:, None, :]).astype(jnp.int32), -1, dtype=jnp.int32)
-    before = place[None, :part] < start[:, None]
-    from_high = before != (x_index == 1)
-
-    def take(v):
-        v = v.reshape(rows, 2, part, model)
-        return jnp.where(from_high[:, :, None], v[:, 1], v[:, 0]).reshape(mine, model)
-
-    def give(own, other):
-        own, other = own.reshape(rows, part, model), other.reshape(rows, part, model)
-        low = jnp.where(from_high[:, :, None], other, own)
-        high = jnp.where(from_high[:, :, None], own, other)
-        return jnp.stack([low, high], 1).reshape(tokens, model)
-
-    seg = jnp.where(from_high, segment[:, part:], segment[:, :part])
-
-    x = take(layer_input)
-    cot = take(cotangent)
-    own_bias = jnp.concatenate([q_bias, v_bias, up_bias])
     remote = (
         (model // n) % 16 == 0 and n % 4 == 0 and n > 4
-        and hidden == 2 * model and 4 * width == hidden and hidden % 384 == 0 and rows >= 3
+        and hidden == 2 * model and 4 * width == hidden and hidden % 384 == 0 and rows >= 3 and mine == model
     )
     if remote:
         depth = n // 4
         dma = pltpu.SemaphoreType.DMA
         wide = (hidden, hidden, model, model)
         quarter = model // 4
-        vectors = jnp.stack([attn_gain, attn_shift, down_bias, ffn_gain, ffn_shift, out_bias]).astype(F32)
-        output, output_peer, grad_in, grad_in_peer, g_down, g_up, g_first, g_last, sums = call(
+        vectors = jnp.concatenate(
+            [attn_gain, attn_shift, down_bias, ffn_gain, ffn_shift, out_bias, q_bias, v_bias, up_bias]
+        ).astype(F32)[None]
+        layer_output, input_grad, g_down, g_up, g_first, g_last, sums = call(
             functools.partial(whole_layer, n),
-            [((mine, model), BF16)] * 4
+            [((tokens, model), BF16)] * 2
             + [((model // n, c), F32) for c in wide]
             + [((2, 8, hidden), F32)],
             [
+                ((mine, model), BF16),
+                ((mine, model), BF16),
+                ((rows, part, 1), jnp.int32),
+                ((rows, 1, part), jnp.int32),
+                ((mine, model), BF16),
+                ((mine, model), BF16),
+                ((mine, model), BF16),
                 ((2, model, 3 * width), BF16),
                 ((2, width, model), BF16),
                 ((2, model, hidden), BF16),
@@ -883,7 +947,6 @@
                 ((2, model, hidden), BF16),
                 ((2, model, hidden), BF16),
                 ((mine, model), F32),
-                ((mine, model), BF16),
                 ((model, mine), BF16),
                 ((model, mine), BF16),
                 ((8, model), F32),
@@ -900,17 +963,38 @@
                 ((depth - 1, 2, 8, hidden), F32),
                 ((model // n, hidden), BF16),
                 dma((5, 4)), dma((5, 4)), dma((5, depth - 1)), dma((5, depth - 1)), dma((2, rows)), dma((2, rows)),
-                dma((4, 10)), dma((4, 10)), dma((6,)),
+                dma((4, 10)), dma((4, 10)), dma((6,)), dma((2, 2 * rows)), dma((2, rows)),
             ],
             2 * mine * model * (24 * width + 12 * hidden),
-            x, cot, seg[:, :, None], seg[:, None, :], own_bias.astype(F32)[None], vectors,
+            doc_lengths, layer_input, cotangent, vectors,
             q_weight, k_weight, v_weight, out_weight, up_weight, down_weight,
-            far=(6, 7, 8, 9, 10, 11), far_out=(1, 3), collective=0,
+            scalar=(0,), far=(1, 2, 4, 5, 6, 7, 8, 9), far_out=(0, 1), collective=0,
         )
         g_attn = jnp.concatenate([g_first, g_last], -1)
         small = sums[1, :, :model]
         sums = jnp.concatenate([sums[0, 0, : 2 * width], sums[0, 1]])
     else:
+        ends = jnp.cumsum(doc_lengths, axis=-1, dtype=jnp.int32)
+        start = jnp.sum(jnp.where(doc_lengths == part, ends - part, 0), -1)
+        place = jnp.arange(length, dtype=jnp.int32)
+        segment = jnp.sum((place[None, :, None] >= ends[:, None, :]).astype(jnp.int32), -1, dtype=jnp.int32)
+        before = place[None, :part] < start[:, None]
+        from_high = before != (x_index == 1)
+
+        def take(v):
+            v = v.reshape(rows, 2, part, model)
+            return jnp.where(from_high[:, :, None], v[:, 1], v[:, 0]).reshape(mine, model)
+
+        def give(own, other):
+            own, other = own.reshape(rows, part, model), other.reshape(rows, part, model)
+            low = jnp.where(from_high[:, :, None], other, own)
+            high = jnp.where(from_high[:, :, None], own, other)
+            return jnp.stack([low, high], 1).reshape(tokens, model)
+
+        seg = jnp.where(from_high, segment[:, part:], segment[:, :part])
+        x = take(layer_input)
+        cot = take(cotangent)
+        own_bias = jnp.concatenate([q_bias, v_bias, up_bias])
         w_qkv = with_peer(jnp.concatenate([q_weight, k_weight, v_weight], 1), n)
         w_out = with_peer(out_weight, n)
         w_up = with_peer(up_weight, n)
@@ -970,8 +1054,8 @@
         sums = jnp.where(x_index == 0, sums, sums[::-1])
         sums, small = lax.psum((sums, small), ("dp", "mp"))
         sums = lax.dynamic_index_in_dim(sums, x_index, 0, keepdims=False)
-    layer_output = give(output, output_peer)
-    input_grad = give(grad_in, grad_in_peer)
+        layer_output = give(output, output_peer)
+        input_grad = give(grad_in, grad_in_peer)
     down_weight_grad = g_down.T
     up_weight_grad = g_up
     return (

time: 204 us -> 192 us (0.941)
  other arithmetic: 9.03 us -> 0.64 us
  local copies, waits for them, and re-layouts: 20.9 us -> 18.6 us
    unnamed x10 -> x18, local copies, waits for them, and re-layouts: 1.44 us -> 11.7 us
    another operation x9 -> x0, local copies, waits for them, and re-layouts: 7.27 us -> none  [the longest x7 4.15 us: per_device(): jnp.stack([attn_gain, attn_shift, down_bias, ffn_gain, ffn_shift, out_bias])]
    select_n x3 -> x0, other arithmetic: 5.62 us -> none  [the longest x1 2.78 us: give(): low = jnp.where(from_high[:, :, None], other, own)]
    slice x3 -> x0, local copies, waits for them, and re-layouts: 3.31 us -> none  [the longest x1 2.65 us: take(): v[:, 1]]
where the time goes in v6:
time: 192 us
  Pallas kernels  172 us (90%)
  local copies, waits for them, and re-layouts  18.6 us (10%)
    pallas_call x1, Pallas kernels, call(): pl.pallas_call(kernel, out_shape=shapes, in_specs=[pl.BlockSpec(memory_sp...  172 us
    unnamed x18, local copies, waits for them, and re-layouts  11.7 us

profile of v6, /device:TPU:0, one launch (start us, length us, event | category | flops | bytes accessed | tf_op | source)
XLA Modules:
  0.0 191.8 jit_solution(1313991787342347704)
XLA Ops:
  0.7 0.7 constant_dynamic-update-slice_fusion.8
  1.3 0.7 constant_dynamic-update-slice_fusion.7
  2.0 0.7 constant_dynamic-update-slice_fusion.6
  2.7 0.7 constant_dynamic-update-slice_fusion.5
  3.4 0.7 constant_dynamic-update-slice_fusion.4
  4.1 0.7 constant_dynamic-update-slice_fusion.3
  4.8 0.7 constant_dynamic-update-slice_fusion.2
  5.5 0.7 constant_dynamic-update-slice_fusion.1
  6.2 0.7 constant_dynamic-update-slice_fusion
  6.9 0.6 convert_element_type.10.vec_ref
  7.5 171.9 %shard_map.305 = (bf16[1536,768]{1,0:T(8,128)(2,1)}, bf16[1536,768]{1,0:T(8,128)(2,1)}, f32[48,1536]{1,0:T(8,128)}, f32[48,1536]{1,0:T(8,128)}, f32[48,768]{1,0:...) custom-call(s32[3,8]{1,0:T(4,128)} %doc_ref.1, bf16[1536,768]{1,0:T(8,128)(2,1)} %x_hbm.1, bf16[1536,768]{1,0:T(8,128)(2,1)} %cot_hbm.1, ...), custom_call_target="tpu_custom_call" | custom-call | flops 32614907904 | bytes 17525856 | tf_op jit(solution)/shard_map/pallas_call | solution.py:830
  179.4 1.7 slice_bitcast_fusion
  181.1 1.7 slice_reduce_fusion.1
  182.8 1.3 slice_reduce_fusion.7
  184.1 1.4 slice_reduce_fusion
  185.6 0.0 copy-start
  185.6 3.4 %copy.47 = bf16[1536,768]{1,0:T(8,128)(2,1)} copy(bf16[1536,768]{1,0:T(8,128)(2,1)} %get-tuple-element.62) | data formatting | bytes 4718592
  188.9 0.0 copy-done
  188.9 0.0 copy-start.2
  188.9 0.0 copy-start.1
  188.9 1.4 copy.48
  190.3 0.0 copy-done.2
  190.3 0.7 copy.49
  191.1 0.0 copy-done.1
  191.1 0.7 copy.50
Async XLA Ops:
  185.6 3.4 %copy-start = (bf16[1536,768]{1,0:T(8,128)(2,1)S(1)}, bf16[1536,768]{1,0:T(8,128)(2,1)}, u32[]{:S(2)}) copy-start(bf16[1536,768]{1,0:T(8,128)(2,1)} %get-tuple-element.63) | copy-start | bytes 7077892
  188.9 1.4 copy-start.2
  188.9 2.1 %copy-start.1 = (f32[48,1536]{1,0:T(8,128)S(1)}, f32[48,1536]{1,0:T(8,128)}, u32[]{:S(2)}) copy-start(f32[48,1536]{1,0:T(8,128)} %get-tuple-element.30) | copy-start | bytes 884740

commit v7 on v6

--- a/solution.py
+++ b/solution.py
@@ -92,20 +92,10 @@
     )
 
 
-def add_rows(dst, src, offset, step):
-    step = min(step, dst.shape[0])
-
-    @pl.loop(0, dst.shape[0] // step)
-    def _(i):
-        here = pl.ds(pl.multiple_of(i * step, step), step)
-        there = pl.ds(pl.multiple_of(offset + i * step, step), step)
-        dst[here, :] = (dst[here, :].astype(F32) + src[there, :].astype(F32)).astype(dst.dtype)
-
-
 def store_by_owner(dst, value, at, n):
     rows = value.shape[0] // n
     for d in range(n):
-        place = (d % 2) * (n // 2) + (d // 2 % 2) * (n // 4) + d // 4
+        place = d % 2 * 8 + d // 2 % 2 * 4 + d // 4 % 2 * 2 + d // 8
         dst[place * rows : (place + 1) * rows, at] = value[d * rows : (d + 1) * rows, :]
 
 
@@ -260,20 +250,16 @@
         weight_products(g, x_t_ref, dattn_t_ref, dq_ref, ctx_ref, ga_ref)
 
 
-WAYS = ("yzx", "yxz", "yxz", "xyz")
-
-
 def whole_layer(
     n, doc_ref, x_hbm, cot_hbm, vec_ref, wq_hbm, wk_hbm, wv_hbm, wo_hbm, up_hbm, down_hbm,
-    output_hbm, input_hbm, rd_ref, ru_ref, ra_ref, rb_ref, sums_ref,
+    output_hbm, input_hbm, rd_ref, ru_ref, ra_ref, sums_ref,
     x_ref, cot_ref, seg_c_ref, seg_r_ref, out_ref, out_peer_ref, in_peer_ref,
     w_ref, wo_ref, up_ref, down_ref, bias_2, qkv_ref, p_ref, ctx_ref, xhat_ref, rstd_ref, low_ref, act_ref, slope_ref,
     acc_ref, t_low_ref, t_grad_ref, small_ref, *rest_refs,
 ):
     in_ref, dffn_ref = cot_ref, low_ref
-    half, mid, owned, shard = rest_refs[0:4], rest_refs[4:8], rest_refs[8:12], rest_refs[12:16]
-    tiny, tiny_1, tiny_2, tiny_x, tiny_z, last = rest_refs[16:22]
-    send, recv, send_z, recv_z, send_in, recv_in, g_send, g_recv, g_local, raw, done = rest_refs[22:]
+    level_0, level_1, level_2, level_3, level_4, tiny, tiny_1, tiny_2, tiny_x, tiny_z = rest_refs[:10]
+    send, recv, send_0, recv_0, send_z, recv_z, send_in, recv_in, g_send, g_recv, g_local, raw, done = rest_refs[10:]
     seqs, length = seg_c_ref.shape[0], seg_c_ref.shape[1]
     groups, width, model = wo_ref.shape
     hidden = up_ref.shape[2]
@@ -289,6 +275,10 @@
     to_core = {"dp": index + 1 - 2 * core}
     to_line = {"dp": index + 2 - 4 * line}
     to_x = {"mp": 1 - x_index}
+
+    near, far = rest % 2, rest // 2
+    to_near = {"dp": index + 4 - 8 * near}
+    to_far = {"dp": index + 8 - 16 * far}
 
     def to_rest(k):
         return {"dp": (rest + k) % depth * 4 + index % 4}
@@ -356,7 +346,7 @@
             pass_on(kind, c, hop).wait_send()
 
     bias_ref = vec_ref.at[:, 6 * model :]
-    bias_over = remote(bias_ref, bias_2, send.at[4, 0], recv.at[4, 0], to_x)
+    bias_over = remote(bias_ref, bias_2, send.at[3, 0], recv.at[3, 0], to_x)
     bias_over.start()
     for kind in range(4):
         over_x(kind).start()
@@ -421,89 +411,76 @@
         rows = pl.ds(pl.multiple_of(2 * s * length, length), 2 * length)
         return pltpu.make_async_copy(down_ref.at[i, rows, :], (output_hbm, input_hbm)[i].at[rows, :], done.at[i, s])
 
-    n_half, n_quarter = model // 2, model // 4
     cut = hidden // 2
-    sources = (act_ref, slope_ref, up_ref.at[:, :, :cut], up_ref.at[:, :, cut:])
-
-    def by_core(t):
-        there = pl.ds(pl.multiple_of((1 - core) * n_half, n_half), n_half)
-        return remote(sources[t].at[:, there, :], half[t], send.at[0, t], recv.at[0, t], to_core)
-
-    def quarter_of(place):
-        return pl.ds(pl.multiple_of(place * n_quarter, n_quarter), n_quarter)
-
-    def own_rows(place):
+    size = model // 8
+    sources = (act_ref, slope_ref, up_ref)
+
+    def source(t, where, block):
+        rows = pl.ds(pl.multiple_of((where * 4 + block) * size, size), size)
+        return sources[t // 2].at[:, rows, t % 2 * cut : (t % 2 + 1) * cut]
+
+    def by_core(t, block):
+        return remote(
+            source(t, 1 - core, block), level_0.at[t, :, block // 2, block % 2],
+            send_0.at[t, block], recv_0.at[t, block], to_core,
+        )
+
+    def start_core(t):
+        for block in range(4):
+            by_core(t, block).start()
+
+    def by_first(t):
+        if t % 2 == 0:
+            return remote(level_0.at[t, :, 1 - line], level_1.at[t], send.at[1, t], recv.at[1, t], to_line)
+        return remote(level_0.at[t, :, :, 1 - near], level_1.at[t], send.at[1, t], recv.at[1, t], to_near)
+
+    def by_second(t):
+        if t % 2 == 0:
+            return remote(level_1.at[t, :, 1 - near], level_2.at[t], send.at[2, t], recv.at[2, t], to_near)
+        return remote(level_1.at[t, :, 1 - line], level_2.at[t], send.at[2, t], recv.at[2, t], to_line)
+
+    def by_x(t):
+        return remote(level_2.at[t, 1], level_3.at[t], send.at[0, t], recv.at[0, t], to_x)
+
+    def far_rows(place):
         return pl.ds(pl.multiple_of(place * rows_own, rows_own), rows_own)
 
-    def by_first(t):
-        if WAYS[t] == "xyz":
-            return remote(half[t].at[1], mid[t], send.at[1, t], recv.at[1, t], to_x)
-        return remote(half[t].at[:, quarter_of(1 - line), :], mid[t], send.at[1, t], recv.at[1, t], to_line)
-
-    def by_second(t):
-        if WAYS[t] == "xyz":
-            return remote(mid[t].at[quarter_of(1 - line), :], owned[t], send.at[2, t], recv.at[2, t], to_line)
-        if WAYS[t] == "yzx":
-            return remote(owned[t].at[1], last, send.at[2, t], recv.at[2, t], to_x)
-        return remote(mid[t].at[1], owned[t], send.at[2, t], recv.at[2, t], to_x)
-
-    def by_rest(t, k):
-        there = own_rows((rest + k) % depth)
-        source = mid[t].at[:, there, :] if WAYS[t] == "yzx" else owned[t].at[there, :]
-        return remote(source, shard[t].at[k - 1], send_z.at[t, k - 1], recv_z.at[t, k - 1], to_rest(k))
-
-    def start_rest(t):
-        for k in range(1, depth):
-            by_rest(t, k).start()
-
-    def rest_sum(t):
-        if WAYS[t] == "yzx":
-            total = mid[t][:, own_rows(rest), :].astype(F32)
-        else:
-            total = owned[t][own_rows(rest), :].astype(F32)
-        for k in range(1, depth):
-            by_rest(t, k).wait_recv()
-            total = total + shard[t][k - 1].astype(F32)
-        return total
+    def by_far(t):
+        return remote(level_3.at[t, far_rows(1 - far), :], level_4.at[t], send.at[4, t], recv.at[4, t], to_far)
+
+    def join(a, b):
+        return (a.astype(F32) + b.astype(F32)).astype(BF16)
 
     def after_core(t):
-        by_core(t).wait_recv()
-        for g in range(groups):
-            add_rows(half[t].at[g], sources[t].at[g], core * n_half, 96)
+        for block in range(4):
+            by_core(t, block).wait_recv()
+            for g in range(groups):
+                i, j = block // 2, block % 2
+                level_0[t, g, i, j] = join(level_0[t, g, i, j], source(t, core, block)[g])
         by_first(t).start()
 
     def after_first(t):
         by_first(t).wait_recv()
-        if WAYS[t] == "xyz":
-            add_rows(mid[t], half[t].at[0], 0, 96)
-        else:
-            for g in range(groups):
-                add_rows(mid[t].at[g], half[t].at[g], line * n_quarter, 96)
-        if WAYS[t] == "yzx":
-            start_rest(t)
-        else:
-            by_second(t).start()
-
-    def after_second(t, out):
-        if WAYS[t] == "yzx":
-            total = rest_sum(t)
-            out[...] = total[0]
-            owned[t][...] = total.astype(BF16)
-            by_second(t).start()
-            return
+        for g in range(groups):
+            for i in range(2):
+                kept = level_0[t, g, line, i] if t % 2 == 0 else level_0[t, g, i, near]
+                level_1[t, g, i] = join(level_1[t, g, i], kept)
+        by_second(t).start()
+
+    def after_second(t):
         by_second(t).wait_recv()
-        if WAYS[t] == "xyz":
-            add_rows(owned[t], mid[t], line * n_quarter, 96)
-        else:
-            add_rows(owned[t], mid[t].at[0], 0, 96)
-        start_rest(t)
+        for g in range(groups):
+            level_2[t, g] = join(level_2[t, g], level_1[t, g, near if t % 2 == 0 else line])
+        by_x(t).start()
+
+    def after_x(t):
+        by_x(t).wait_recv()
+        level_3[t] = join(level_3[t], level_2[t, 0])
+        by_far(t).start()
 
     def finish(t, out):
-        if WAYS[t] == "yzx":
-            by_second(t).wait_recv()
-            out[...] += last[...].astype(F32)
-        else:
-            out[...] = rest_sum(t)
+        by_far(t).wait_recv()
+        out[:, t % 2 * cut : (t % 2 + 1) * cut] = level_3[t, far_rows(far), :].astype(F32) + level_4[t].astype(F32)
 
     def send_output(b):
         rows = pl.ds(pl.multiple_of(b * length, length), length)
@@ -690,7 +667,8 @@
         def _(c):
             product(t_grad_ref, act_ref, g, columns(c))
 
-    by_core(0).start()
+    start_core(0)
+    start_core(1)
     for g in range(groups):
 
         @pl.loop(0, 3)
@@ -711,8 +689,10 @@
                 @pl.when(c == 1)
                 def _():
                     after_core(0)
-
-    by_core(1).start()
+                    after_core(1)
+
+    start_core(2)
+    start_core(3)
 
     @pl.loop(0, seqs)
     def _(b):
@@ -737,18 +717,27 @@
 
         @pl.when(s == 0)
         def _():
-            after_core(1)
-
-        @pl.when(s == min(1, seqs - 1))
+            after_first(0)
+            after_first(1)
+            after_core(2)
+            after_core(3)
+
+        @pl.when(s == 1)
         def _():
-            after_first(0)
+            after_second(0)
+            after_second(1)
+
+        @pl.when(s == 2)
+        def _():
+            after_first(2)
+            after_first(3)
 
     tiny_core = remote(tiny.at[0:3], tiny_1, send.at[3, 1], recv.at[3, 1], to_core)
     tiny_line = remote(tiny_1, tiny_2, send.at[3, 2], recv.at[3, 2], to_line)
     tiny_over = remote(tiny_2.at[1:3], tiny_x, send.at[3, 3], recv.at[3, 3], to_x)
 
     def tiny_rest(k):
-        return remote(tiny_x, tiny_z.at[k - 1], send_z.at[4, k - 1], recv_z.at[4, k - 1], to_rest(k))
+        return remote(tiny_x, tiny_z.at[k - 1], send_z.at[k - 1], recv_z.at[k - 1], to_rest(k))
 
     for g in range(groups):
         column = jnp.sum(qkv_ref[g].astype(F32), 0, keepdims=True)
@@ -764,13 +753,18 @@
     tiny_core.start()
     for g in range(groups):
         weight_products(g, t_low_ref, t_grad_ref, qkv_ref, ctx_ref, up_ref)
-    by_core(2).start()
-    by_core(3).start()
+    start_core(4)
+    start_core(5)
     tiny_core.wait_recv()
     tiny_1[...] += tiny[0:3]
     tiny_line.start()
-    after_core(2)
-    after_core(3)
+    after_core(4)
+    after_core(5)
+    after_second(2)
+    after_second(3)
+    tiny_line.wait_recv()
+    tiny_2[...] += tiny_1[...]
+    tiny_over.start()
     for i, (one, own, other) in enumerate(
         ((send_output, out_ref, out_peer_ref), (send_input, in_ref, in_peer_ref))
     ):
@@ -781,41 +775,44 @@
             put_back(s, i, own, other)
             put_out(s, i).start()
 
-    tiny_line.wait_recv()
-    tiny_2[...] += tiny_1[...]
-    tiny_over.start()
-    after_first(1)
-    after_second(0, rd_ref)
-    after_first(3)
+    after_x(0)
+    after_x(1)
+    after_first(4)
+    after_first(5)
+    after_x(2)
+    after_x(3)
     tiny_over.wait_recv()
     tiny_x[0] += tiny_2[0]
     tiny_x[1] += tiny_2[2]
     for k in range(1, depth):
         tiny_rest(k).start()
-    after_first(2)
-    after_second(1, ru_ref)
-    after_second(3, rb_ref)
+    after_second(4)
+    after_second(5)
     finish(0, rd_ref)
-    after_second(2, ra_ref)
+    finish(1, rd_ref)
+    finish(2, ru_ref)
+    finish(3, ru_ref)
     total = tiny_x[...]
     for k in range(1, depth):
         tiny_rest(k).wait_recv()
         total = total + tiny_z[k - 1]
     sums_ref[...] = total
-    finish(1, ru_ref)
-    finish(3, rb_ref)
-    finish(2, ra_ref)
+    after_x(4)
+    after_x(5)
+    finish(4, ra_ref)
+    finish(5, ra_ref)
     for s in range(seqs):
         send_output(s).wait_send()
         send_input(s).wait_send()
         for i in range(2):
             put_out(s, i).wait()
-    for t in range(4):
-        by_core(t).wait_send()
+    for t in range(6):
+        for block in range(4):
+            by_core(t, block).wait_send()
         by_first(t).wait_send()
         by_second(t).wait_send()
-        for k in range(1, depth):
-            by_rest(t, k).wait_send()
+        by_x(t).wait_send()
+        by_far(t).wait_send()
     tiny_core.wait_send()
     tiny_line.wait_send()
     tiny_over.wait_send()
@@ -909,21 +906,20 @@
     x_index = lax.axis_index("mp")
 
     remote = (
-        (model // n) % 16 == 0 and n % 4 == 0 and n > 4
+        (model // n) % 16 == 0 and n == 16
         and hidden == 2 * model and 4 * width == hidden and hidden % 384 == 0 and rows >= 3 and mine == model
     )
     if remote:
         depth = n // 4
         dma = pltpu.SemaphoreType.DMA
-        wide = (hidden, hidden, model, model)
-        quarter = model // 4
+        eighth = model // 8
         vectors = jnp.concatenate(
             [attn_gain, attn_shift, down_bias, ffn_gain, ffn_shift, out_bias, q_bias, v_bias, up_bias]
         ).astype(F32)[None]
-        layer_output, input_grad, g_down, g_up, g_first, g_last, sums = call(
+        layer_output, input_grad, g_down, g_up, g_attn, sums = call(
             functools.partial(whole_layer, n),
             [((tokens, model), BF16)] * 2
-            + [((model // n, c), F32) for c in wide]
+            + [((model // n, hidden), F32)] * 3
             + [((2, 8, hidden), F32)],
             [
                 ((mine, model), BF16),
@@ -951,18 +947,18 @@
                 ((model, mine), BF16),
                 ((8, model), F32),
             ]
-            + [((2, model // 2, c), BF16) for c in wide]
-            + [((2 * quarter, c) if w == "xyz" else (2, quarter, c), BF16) for w, c in zip(WAYS, wide)]
-            + [((2, model // n, c) if w == "yzx" else (quarter, c), BF16) for w, c in zip(WAYS, wide)]
-            + [((depth - 1,) + (2,) * (w == "yzx") + (model // n, c), BF16) for w, c in zip(WAYS, wide)]
             + [
+                ((6, 2, 2, 2, eighth, model), BF16),
+                ((6, 2, 2, eighth, model), BF16),
+                ((6, 2, eighth, model), BF16),
+                ((6, eighth, model), BF16),
+                ((6, model // n, model), BF16),
                 ((5, 8, hidden), F32),
                 ((3, 8, hidden), F32),
                 ((3, 8, hidden), F32),
                 ((2, 8, hidden), F32),
                 ((depth - 1, 2, 8, hidden), F32),
-                ((model // n, hidden), BF16),
-                dma((5, 4)), dma((5, 4)), dma((5, depth - 1)), dma((5, depth - 1)), dma((2, rows)), dma((2, rows)),
+                dma((5, 6)), dma((5, 6)), dma((6, 4)), dma((6, 4)), dma((depth - 1,)), dma((depth - 1,)), dma((2, rows)), dma((2, rows)),
                 dma((4, 10)), dma((4, 10)), dma((6,)), dma((2, 2 * rows)), dma((2, rows)),
             ],
             2 * mine * model * (24 * width + 12 * hidden),
@@ -970,7 +966,6 @@
             q_weight, k_weight, v_weight, out_weight, up_weight, down_weight,
             scalar=(0,), far=(1, 2, 4, 5, 6, 7, 8, 9), far_out=(0, 1), collective=0,
         )
-        g_attn = jnp.concatenate([g_first, g_last], -1)
         small = sums[1, :, :model]
         sums = jnp.concatenate([sums[0, 0, : 2 * width], sums[0, 1]])
     else:

time: 192 us -> 186 us (0.969)
  Pallas kernels: 172 us -> 166 us
    pallas_call x1, Pallas kernels: 172 us -> 166 us  [call(): pl.pallas_call(kernel, out_shape=shapes, in_specs=[pl.BlockSpec(memory_sp...]
where the time goes in v7:
time: 186 us
  Pallas kernels  166 us (89%)
  local copies, waits for them, and re-layouts  18.6 us (10%)
    pallas_call x1, Pallas kernels, call(): pl.pallas_call(kernel, out_shape=shapes, in_specs=[pl.BlockSpec(memory_sp...  166 us
    unnamed x18, local copies, waits for them, and re-layouts  11.7 us

profile of v7, /device:TPU:0, one launch (start us, length us, event | category | flops | bytes accessed | tf_op | source)
XLA Modules:
  0.0 185.6 jit_solution(13796713880843306619)
XLA Ops:
  0.7 0.7 constant_dynamic-update-slice_fusion.8
  1.3 0.7 constant_dynamic-update-slice_fusion.7
  2.0 0.7 constant_dynamic-update-slice_fusion.6
  2.7 0.7 constant_dynamic-update-slice_fusion.5
  3.4 0.7 constant_dynamic-update-slice_fusion.4
  4.1 0.7 constant_dynamic-update-slice_fusion.3
  4.8 0.7 constant_dynamic-update-slice_fusion.2
  5.5 0.7 constant_dynamic-update-slice_fusion.1
  6.2 0.7 constant_dynamic-update-slice_fusion
  6.9 0.6 convert_element_type.10.vec_ref
  7.5 165.6 %shard_map.305 = (bf16[1536,768]{1,0:T(8,128)(2,1)}, bf16[1536,768]{1,0:T(8,128)(2,1)}, f32[48,1536]{1,0:T(8,128)}, f32[48,1536]{1,0:T(8,128)}, f32[48,1536]{1,0:T(8,128)}, /*index=5*/f32[2,8,1536]{2,1,0:T(8,128)}) custom-call(s32[3,8]{1,0:T(4,128)} %doc_ref.1, bf16[1536,768]{1,0:T(8,128)(2,1)} %x_hbm.1, bf16[1536,768]{1,0:T(8,128)(2,1)} %cot_hbm.1, ...), custom_call_target="tpu_custom_call" | custom-call | flops 32614907904 | bytes 17525856 | tf_op jit(solution)/shard_map/pallas_call | solution.py:827
  173.1 1.8 slice_reduce_fusion.1
  174.9 1.7 slice_bitcast_fusion
  176.6 1.3 slice_reduce_fusion.7
  177.9 1.4 slice_reduce_fusion
  179.3 0.0 copy-start
  179.3 3.4 %copy.47 = bf16[1536,768]{1,0:T(8,128)(2,1)} copy(bf16[1536,768]{1,0:T(8,128)(2,1)} %get-tuple-element.58) | data formatting | bytes 4718592
  182.7 0.0 copy-done
  182.7 0.0 copy-start.2
  182.7 0.0 copy-start.1
  182.7 1.4 copy.48
  184.1 0.0 copy-done.2
  184.1 0.7 copy.49
  184.8 0.0 copy-done.1
  184.8 0.7 copy.50
Async XLA Ops:
  179.3 3.4 %copy-start = (bf16[1536,768]{1,0:T(8,128)(2,1)S(1)}, bf16[1536,768]{1,0:T(8,128)(2,1)}, u32[]{:S(2)}) copy-start(bf16[1536,768]{1,0:T(8,128)(2,1)} %get-tuple-element.59) | copy-start | bytes 7077892
  182.7 1.4 copy-start.2
  182.7 2.1 %copy-start.1 = (f32[48,1536]{1,0:T(8,128)S(1)}, f32[48,1536]{1,0:T(8,128)}, u32[]{:S(2)}) copy-start(f32[48,1536]{1,0:T(8,128)} %get-tuple-element.28) | copy-start | bytes 884740

commit v8 on v7

--- a/solution.py
+++ b/solution.py
@@ -251,15 +251,17 @@
 
 
 def whole_layer(
-    n, doc_ref, x_hbm, cot_hbm, vec_ref, wq_hbm, wk_hbm, wv_hbm, wo_hbm, up_hbm, down_hbm,
+    n, doc_ref, x_hbm, cot_hbm, wq_hbm, wk_hbm, wv_hbm, wo_hbm, up_hbm, down_hbm,
+    v_0, v_1, v_2, v_3, v_4, v_5, v_6, v_7, v_8,
     output_hbm, input_hbm, rd_ref, ru_ref, ra_ref, sums_ref,
-    x_ref, cot_ref, seg_c_ref, seg_r_ref, out_ref, out_peer_ref, in_peer_ref,
+    x_ref, cot_ref, vec_ref, seg_c_ref, seg_r_ref, out_ref, out_peer_ref, in_peer_ref,
     w_ref, wo_ref, up_ref, down_ref, bias_2, qkv_ref, p_ref, ctx_ref, xhat_ref, rstd_ref, low_ref, act_ref, slope_ref,
     acc_ref, t_low_ref, t_grad_ref, small_ref, *rest_refs,
 ):
     in_ref, dffn_ref = cot_ref, low_ref
-    level_0, level_1, level_2, level_3, level_4, tiny, tiny_1, tiny_2, tiny_x, tiny_z = rest_refs[:10]
-    send, recv, send_0, recv_0, send_z, recv_z, send_in, recv_in, g_send, g_recv, g_local, raw, done = rest_refs[10:]
+    level_0, level_1, level_2, level_3, level_4, ubg_ref = rest_refs[:6]
+    tiny, tiny_1, tiny_2, tiny_x, tiny_n, tiny_f = rest_refs[6:12]
+    send, recv, send_0, recv_0, send_in, recv_in, g_send, g_recv, g_local, raw, done = rest_refs[12:]
     seqs, length = seg_c_ref.shape[0], seg_c_ref.shape[1]
     groups, width, model = wo_ref.shape
     hidden = up_ref.shape[2]
@@ -345,6 +347,10 @@
         for hop in (1, 2, 3):
             pass_on(kind, c, hop).wait_send()
 
+    place = 0
+    for v in (v_0, v_1, v_2, v_3, v_4, v_5, v_6, v_7, v_8):
+        vec_ref[0:1, place : place + v.shape[0]] = v[...].astype(F32).reshape(1, v.shape[0])
+        place += v.shape[0]
     bias_ref = vec_ref.at[:, 6 * model :]
     bias_over = remote(bias_ref, bias_2, send.at[3, 0], recv.at[3, 0], to_x)
     bias_over.start()
@@ -682,7 +688,7 @@
                 d_low = d_upper.astype(BF16)
                 slope_ref[g, rows, at] = d_low
                 acc_ref[rows, :] += mm_t(d_low, up_ref[g, :, at])
-            tiny[3 + g, 0:1, at] = total
+            ubg_ref[g, 0:1, at] = total
             product(t_low_ref, slope_ref, g, at)
             if g == 0:
 
@@ -727,44 +733,55 @@
             after_second(0)
             after_second(1)
 
-        @pl.when(s == 2)
-        def _():
-            after_first(2)
-            after_first(3)
-
-    tiny_core = remote(tiny.at[0:3], tiny_1, send.at[3, 1], recv.at[3, 1], to_core)
+    tiny_core = remote(tiny, tiny_1, send.at[3, 1], recv.at[3, 1], to_core)
     tiny_line = remote(tiny_1, tiny_2, send.at[3, 2], recv.at[3, 2], to_line)
     tiny_over = remote(tiny_2.at[1:3], tiny_x, send.at[3, 3], recv.at[3, 3], to_x)
 
-    def tiny_rest(k):
-        return remote(tiny_x, tiny_z.at[k - 1], send_z.at[k - 1], recv_z.at[k - 1], to_rest(k))
+    tiny_near = remote(tiny_x, tiny_n, send.at[3, 4], recv.at[3, 4], to_near)
+    tiny_far = remote(tiny_n, tiny_f, send.at[3, 5], recv.at[3, 5], to_far)
 
     for g in range(groups):
         column = jnp.sum(qkv_ref[g].astype(F32), 0, keepdims=True)
         tiny[g, 0:1, :width] = column[:, :width]
         tiny[g, 0:1, width : 2 * width] = column[:, 2 * width :]
-        tiny[g, 1:2, :] = tiny[3 + g, 0:1, :]
-    tiny[2, :, :model] = small_ref[...]
+        tiny[g, 1:2, :] = ubg_ref[g, 0:1, :model]
+        tiny[g, 2:3, :] = ubg_ref[g, 0:1, model:]
+    tiny[2] = small_ref[...]
     for kind in range(4):
         sent(kind)
     for c in range(3):
         sent(4, c)
         sent(5, c)
     tiny_core.start()
-    for g in range(groups):
-        weight_products(g, t_low_ref, t_grad_ref, qkv_ref, ctx_ref, up_ref)
+
+    def products(left, right, first, columns_of):
+        for g in range(groups):
+
+            @pl.loop(0, model // block)
+            def _(b):
+                rows = pl.ds(pl.multiple_of(b * block, block), block)
+                made = mm(left[rows, :], right[g, :, columns_of]).astype(BF16)
+                up_ref[g, rows, first : first + made.shape[1]] = made
+
+    products(t_low_ref, qkv_ref, 0, slice(0, cut))
     start_core(4)
+    after_first(2)
+    after_first(3)
+    products(t_low_ref, qkv_ref, cut, slice(cut, 3 * width))
+    products(t_grad_ref, ctx_ref, 3 * width, slice(None))
     start_core(5)
     tiny_core.wait_recv()
-    tiny_1[...] += tiny[0:3]
+    tiny_1[...] += tiny[...]
     tiny_line.start()
     after_core(4)
+    after_x(0)
+    after_x(1)
     after_core(5)
-    after_second(2)
-    after_second(3)
     tiny_line.wait_recv()
     tiny_2[...] += tiny_1[...]
     tiny_over.start()
+    after_second(2)
+    after_second(3)
     for i, (one, own, other) in enumerate(
         ((send_output, out_ref, out_peer_ref), (send_input, in_ref, in_peer_ref))
     ):
@@ -775,28 +792,29 @@
             put_back(s, i, own, other)
             put_out(s, i).start()
 
-    after_x(0)
-    after_x(1)
-    after_first(4)
-    after_first(5)
-    after_x(2)
-    after_x(3)
     tiny_over.wait_recv()
     tiny_x[0] += tiny_2[0]
     tiny_x[1] += tiny_2[2]
-    for k in range(1, depth):
-        tiny_rest(k).start()
+    tiny_near.start()
+    after_x(2)
+    after_x(3)
+    finish(0, rd_ref)
+    finish(1, rd_ref)
+    after_first(4)
+    after_first(5)
+    tiny_near.wait_recv()
+    tiny_n[...] += tiny_x[...]
+    tiny_far.start()
+    finish(2, ru_ref)
+    finish(3, ru_ref)
     after_second(4)
     after_second(5)
-    finish(0, rd_ref)
-    finish(1, rd_ref)
-    finish(2, ru_ref)
-    finish(3, ru_ref)
-    total = tiny_x[...]
-    for k in range(1, depth):
-        tiny_rest(k).wait_recv()
-        total = total + tiny_z[k - 1]
-    sums_ref[...] = total
+    tiny_far.wait_recv()
+    total = tiny_n[...] + tiny_f[...]
+    for i in range(3):
+        sums_ref[0:1, i * model : (i + 1) * model] = total[0, i : i + 1, :]
+    for i in range(6):
+        sums_ref[0:1, (3 + i) * model : (4 + i) * model] = total[1, i : i + 1, :]
     after_x(4)
     after_x(5)
     finish(4, ra_ref)
@@ -816,8 +834,8 @@
     tiny_core.wait_send()
     tiny_line.wait_send()
     tiny_over.wait_send()
-    for k in range(1, depth):
-        tiny_rest(k).wait_send()
+    tiny_near.wait_send()
+    tiny_far.wait_send()
 
 
 def call(kernel, outs, scratch, flops, *args, scalar=(), far=(), far_out=(), collective=None):
@@ -910,20 +928,17 @@
         and hidden == 2 * model and 4 * width == hidden and hidden % 384 == 0 and rows >= 3 and mine == model
     )
     if remote:
-        depth = n // 4
         dma = pltpu.SemaphoreType.DMA
         eighth = model // 8
-        vectors = jnp.concatenate(
-            [attn_gain, attn_shift, down_bias, ffn_gain, ffn_shift, out_bias, q_bias, v_bias, up_bias]
-        ).astype(F32)[None]
         layer_output, input_grad, g_down, g_up, g_attn, sums = call(
             functools.partial(whole_layer, n),
             [((tokens, model), BF16)] * 2
             + [((model // n, hidden), F32)] * 3
-            + [((2, 8, hidden), F32)],
+            + [((1, 6 * model + 2 * width + hidden), F32)],
             [
                 ((mine, model), BF16),
                 ((mine, model), BF16),
+                ((1, 6 * model + 2 * width + hidden), F32),
                 ((rows, part, 1), jnp.int32),
                 ((rows, 1, part), jnp.int32),
                 ((mine, model), BF16),
@@ -953,21 +968,24 @@
                 ((6, 2, eighth, model), BF16),
                 ((6, eighth, model), BF16),
                 ((6, model // n, model), BF16),
-                ((5, 8, hidden), F32),
-                ((3, 8, hidden), F32),
-                ((3, 8, hidden), F32),
-                ((2, 8, hidden), F32),
-                ((depth - 1, 2, 8, hidden), F32),
-                dma((5, 6)), dma((5, 6)), dma((6, 4)), dma((6, 4)), dma((depth - 1,)), dma((depth - 1,)), dma((2, rows)), dma((2, rows)),
+                ((2, 1, hidden), F32),
+                ((3, 8, model), F32),
+                ((3, 8, model), F32),
+                ((3, 8, model), F32),
+                ((2, 8, model), F32),
+                ((2, 8, model), F32),
+                ((2, 8, model), F32),
+                dma((5, 6)), dma((5, 6)), dma((6, 4)), dma((6, 4)), dma((2, rows)), dma((2, rows)),
                 dma((4, 10)), dma((4, 10)), dma((6,)), dma((2, 2 * rows)), dma((2, rows)),
             ],
             2 * mine * model * (24 * width + 12 * hidden),
-            doc_lengths, layer_input, cotangent, vectors,
+            doc_lengths, layer_input, cotangent,
             q_weight, k_weight, v_weight, out_weight, up_weight, down_weight,
-            scalar=(0,), far=(1, 2, 4, 5, 6, 7, 8, 9), far_out=(0, 1), collective=0,
+            attn_gain, attn_shift, down_bias, ffn_gain, ffn_shift, out_bias, q_bias, v_bias, up_bias,
+            scalar=(0,), far=(1, 2, 3, 4, 5, 6, 7, 8), far_out=(0, 1), collective=0,
         )
-        small = sums[1, :, :model]
-        sums = jnp.concatenate([sums[0, 0, : 2 * width], sums[0, 1]])
+        sums = sums[0]
+        small = [sums[2 * width + hidden + i * model :][:model] for i in range(6)]
     else:
         ends = jnp.cumsum(doc_lengths, axis=-1, dtype=jnp.int32)
         start = jnp.sum(jnp.where(doc_lengths == part, ends - part, 0), -1)
@@ -1066,7 +1084,7 @@
         small[1],
         small[2],
         up_weight_grad,
-        sums[2 * width :],
+        sums[2 * width : 2 * width + hidden],
         down_weight_grad,
         small[3],
         small[4],

time: 186 us -> 171 us (0.919)
  Pallas kernels: 166 us -> 158 us
  local copies, waits for them, and re-layouts: 18.6 us -> 11.9 us
    pallas_call x1, Pallas kernels: 166 us -> 158 us  [call(): pl.pallas_call(kernel, out_shape=shapes, in_specs=[pl.BlockSpec(memory_sp...]
    unnamed x18 -> x10, local copies, waits for them, and re-layouts: 11.7 us -> 6.21 us
where the time goes in v8:
time: 171 us
  Pallas kernels  158 us (92%)
  local copies, waits for them, and re-layouts  11.9 us (7%)
    pallas_call x1, Pallas kernels, call(): pl.pallas_call(kernel, out_shape=shapes, in_specs=[pl.BlockSpec(memory_sp...  158 us
    unnamed x10, local copies, waits for them, and re-layouts  6.21 us

profile of v8, /device:TPU:0, one launch (start us, length us, event | category | flops | bytes accessed | tf_op | source)
XLA Modules:
  0.0 170.8 jit_solution(8654423448868502315)
XLA Ops:
  0.7 158.2 %shard_map.305 = (bf16[1536,768]{1,0:T(8,128)(2,1)}, bf16[1536,768]{1,0:T(8,128)(2,1)}, f32[48,1536]{1,0:T(8,128)}, f32[48,1536]{1,0:T(8,128)}, f32[48,1536]{1,0:T(8,128)}, /*index=5*/f32[1,6912]{1,0:T(1,128)}) custom-call(s32[3,8]{1,0:T(4,128)} %doc_ref.1, bf16[1536,768]{1,0:T(8,128)(2,1)} %x_hbm.1, bf16[1536,768]{1,0:T(8,128)(2,1)} %cot_hbm.1, ...), custom_call_target="tpu_custom_call" | custom-call | flops 32614907904 | bytes 17441376 | tf_op jit(solution)/shard_map/pallas_call | solution.py:845
  158.9 1.7 %slice_bitcast_fusion = (f32[384,48]{0,1:T(8,128)}, f32[48,384]{1,0:T(8,128)}, f32[48,384]{1,0:T(8,128)}, f32[48,384]{1,0:T(8,128)}) fusion(f32[48,1536]{1,0:T(8,128)} %get-tuple-element.25), kind=kLoop, calls=%fused_computation | loop fusion | bytes 589824 | tf_op jit(solution)/shard_map/transpose | solution.py:1082
  160.6 1.3 slice_reduce_fusion.7
  161.9 1.4 slice_reduce_fusion.1
  163.2 1.3 slice_reduce_fusion
  164.5 0.0 copy-start
  164.5 3.4 %copy.39 = bf16[1536,768]{1,0:T(8,128)(2,1)} copy(bf16[1536,768]{1,0:T(8,128)(2,1)} %get-tuple-element.58) | data formatting | bytes 4718592
  167.9 0.0 copy-done
  167.9 0.0 copy-start.2
  167.9 0.0 copy-start.1
  167.9 1.4 copy.40
  169.3 0.0 copy-done.2
  169.3 0.7 copy.41
  170.0 0.0 copy-done.1
  170.0 0.7 copy.42
Async XLA Ops:
  164.5 3.4 %copy-start = (bf16[1536,768]{1,0:T(8,128)(2,1)S(1)}, bf16[1536,768]{1,0:T(8,128)(2,1)}, u32[]{:S(2)}) copy-start(bf16[1536,768]{1,0:T(8,128)(2,1)} %get-tuple-element.59) | copy-start | bytes 7077892
  167.9 1.4 copy-start.2
  167.9 2.1 %copy-start.1 = (f32[48,1536]{1,0:T(8,128)S(1)}, f32[48,1536]{1,0:T(8,128)}, u32[]{:S(2)}) copy-start(f32[48,1536]{1,0:T(8,128)} %get-tuple-element.28) | copy-start | bytes 884740
